TPU v7x, 32 devices: a whole 2x2x4 slice. The times are simulated.
32 devices in a mesh: chain: 8 (over z, x), col: 4 (over y, core).
Axes of the slice: x: 2, y: 2, z: 4, core: 2. Of those that a mesh axis runs over, the one named last changes fastest.
Arguments:
- inverses: float32 [8, 2, 512, 512], P('chain', None, None, 'col'), may hold values from -3 to 3
- couplings: float32 [8, 2, 512, 512], P('chain', None, None, 'col'), may hold values from -3 to 3
- sources: float32 [8, 2, 512, 1024], P('chain', None, None, 'col'), may hold values from -6 to 6
- counts: int32 [8], P('chain'), may hold values from 384 to 512, as said below
Outputs:
- fields: float32 [8, 2, 512, 1024], P('chain', None, None, 'col')
Inputs may be any that keep to these rules, and one draw needn't show every extreme that they name: `counts`: some slice has exactly 512 orbitals in use.
All inputs are finite; a program needn't handle non-finite values.
Results may differ from a plain program's by a relative error of at most 0.0003.
Values sent between devices are 32-bit elements; how exact they have to be, the bound alone decides.
No kernel may reach another device: no remote copies, remote signals or barrier semaphores. Data moves between devices by JAX's collectives and lax.ppermute only.
A program may use at most 128 MiB of HBM per device.

v0:
```python
import jax
import jax.numpy as jnp
from jax import lax
from jax.sharding import PartitionSpec as P


def passed_along(shard, axis, by):
    count = lax.axis_size(axis)
    pairs = [(i, i + by) for i in range(count) if 0 <= i + by < count]
    return lax.ppermute(shard, axis, pairs)


def real_product(left_side, right_side):
    return jnp.dot(
        left_side, right_side, precision=lax.Precision.HIGHEST, preferred_element_type=jnp.float32
    )


def complex_product(left_side, right_side):
    gauss_sum = real_product(left_side[0] + left_side[1], right_side[0])
    gauss_diff = real_product(left_side[0], right_side[1] - right_side[0])
    gauss_cross = real_product(left_side[1], right_side[0] + right_side[1])
    return jnp.stack([gauss_sum - gauss_cross, gauss_sum + gauss_diff])


def local(inverses, couplings, sources, counts):
    local_inverse = inverses[0]
    local_coupling = couplings[0]
    local_source = sources[0]
    orbitals = local_inverse.shape[1]
    active = (lax.iota(jnp.int32, orbitals) < counts[0]).astype(jnp.float32)[:, None]
    whole_inverse, whole_coupling = (
        lax.all_gather(local_inverse, "col", axis=2, tiled=True),
        lax.all_gather(local_coupling, "col", axis=2, tiled=True),
    )
    offset = complex_product(whole_inverse, local_source) * active
    own_columns = complex_product(whole_inverse, local_coupling) * active
    chain_place = lax.axis_index("chain")
    chain_length = lax.axis_size("chain")
    own_map = own_columns
    own_offset = offset
    distance = 1
    while distance < chain_length:
        earlier_map, earlier_offset = passed_along((own_map, own_offset), "chain", distance)

        def fold_level(
            carried, piece, start, earlier_map=earlier_map, earlier_offset=earlier_offset
        ):
            return (complex_product(piece, earlier_map), complex_product(piece, earlier_offset))

        blank_pair = (jnp.zeros_like(own_map), jnp.zeros_like(own_offset))
        next_map, next_offset = fold_level(
            blank_pair, lax.all_gather(own_map, "col", axis=2, tiled=True), jnp.int32(0)
        )
        next_offset = next_offset + own_offset
        receiving = chain_place >= distance
        own_map = jnp.where(receiving, next_map, own_map)
        own_offset = jnp.where(receiving, next_offset, own_offset)
        distance = distance * 2
    return own_offset[None]


def solution(mesh):
    placed = (
        P("chain", None, None, "col"),
        P("chain", None, None, "col"),
        P("chain", None, None, "col"),
        P("chain"),
    )
    return jax.shard_map(
        local, mesh=mesh, in_specs=placed, out_specs=P("chain", None, None, "col"), check_vma=False
    )
```

profile of v0, /device:TPU:24, one launch (start us, length us, event | category | flops | bytes accessed | tf_op | source)
XLA Modules:
  0.0 208.8 jit_solution(42019146157228366)
XLA Ops:
  8.0 24.7 %all-gather.12.cloned.1.call-done = f32[1,2,512,512]{3,2,1,0:T(8,128)} async-done(((f32[1,2,512,128]{3,2,1,0:T(8,128)}), f32[1,2,512,512]{3,2,1,0:T(8,128)}) %all-gather.12.cloned.1.call-update) | async-done | bytes 2097168 | tf_op jit(solution)/shard_map/all_gather | solution.py:33
  32.7 2.7 %fusion.38 = f32[512,128]{1,0:T(8,128)S(1)} fusion(f32[1,2,512,512]{3,2,1,0:T(8,128)} %all-gather.12.cloned.1.call-done, f32[1,2,512,128]{3,2,1,0:T(8,128)} %param.5), kind=kOutput, calls=%fused_computation.59 | convolution fusion | flops 402915328 | bytes 2621440 | tf_op jit(solution)/shard_map/dot_general | solution.py:14
  35.4 2.2 %fusion.5 = f32[1,512,128]{2,1,0:T(8,128)S(1)} fusion(f32[512,128]{1,0:T(8,128)S(1)} %fusion.38, f32[1,2,512,512]{3,2,1,0:T(8,128)} %all-gather.12.cloned.1.call-done, f32[1,2,512,128]{3,2,1,0:T(8,128)S(1)} %copy-done.22), kind=kOutput, calls=%fused_computation.20 | convolution fusion | flops 402784256 | bytes 2097152 | tf_op jit(solution)/shard_map/dot_general | solution.py:14
  39.7 3.4 %collective-permute-start = (f32[2,512,128]{2,1,0:T(8,128)}, f32[2,512,128]{2,1,0:T(8,128)S(1)}, u32[]{:S(2)}, u32[]{:S(2)}) collective-permute-start(f32[2,512,128]{2,1,0:T(8,128)} %maximum_multiply_fusion.2), channel_id=1, source_target_pairs={{0,4},{4,8},{8,12},{12,16},{16,20},{20,24},{24,28},{1,5},{5,9},{9,... | collective-permute-start | bytes 1572872 | tf_op jit(solution)/shard_map/ppermute | solution.py:10
  43.1 13.7 %collective-permute-done = f32[2,512,128]{2,1,0:T(8,128)S(1)} collective-permute-done((f32[2,512,128]{2,1,0:T(8,128)}, f32[2,512,128]{2,1,0:T(8,128)S(1)}, u32[]{:S(2)}, u32[]{:S(2)}) %collective-permute-start) | collective-permute-done | bytes 524320 | tf_op jit(solution)/shard_map/ppermute | solution.py:10
  56.8 5.8 %all-gather.6.cloned.1.call-done = f32[2,512,512]{2,1,0:T(8,128)} async-done(((f32[2,512,128]{2,1,0:T(8,128)}), f32[2,512,512]{2,1,0:T(8,128)}) %all-gather.6.cloned.1.call-update) | async-done | bytes 2097168 | tf_op jit(solution)/shard_map/all_gather | solution.py:53
  62.6 2.7 %fusion.30 = f32[512,128]{1,0:T(8,128)S(1)} fusion(f32[2,512,512]{2,1,0:T(8,128)} %all-gather.6.cloned.1.call-done, f32[2,512,128]{2,1,0:T(8,128)S(1)} %collective-permute-done), kind=kOutput, calls=%fused_computation.51 | convolution fusion | flops 402915328 | bytes 2621440 | tf_op jit(solution)/shard_map/dot_general | solution.py:14
  65.3 2.3 %fusion.11 = f32[1,512,128]{2,1,0:T(8,128)S(1)} fusion(f32[512,128]{1,0:T(8,128)S(1)} %fusion.30, f32[2,512,512]{2,1,0:T(8,128)} %all-gather.6.cloned.1.call-done, f32[2,512,128]{2,1,0:T(8,128)} %copy-done.23), kind=kOutput, calls=%fused_computation.30 | convolution fusion | flops 402784256 | bytes 2097152 | tf_op jit(solution)/shard_map/dot_general | solution.py:14
  67.6 2.1 %fusion.10 = f32[1,512,128]{2,1,0:T(8,128)S(1)} fusion(f32[512,128]{1,0:T(8,128)S(1)} %fusion.30, f32[2,512,512]{2,1,0:T(8,128)S(1)} %copy-done.2, f32[2,512,128]{2,1,0:T(8,128)} %copy-done.23), kind=kOutput, calls=%fused_computation.28 | convolution fusion | flops 402784256 | bytes 2097152 | tf_op jit(solution)/shard_map/dot_general | solution.py:14
  70.8 2.1 %fusion.36 = f32[512,256]{1,0:T(8,128)S(1)} fusion(f32[1,2,512,256]{3,2,1,0:T(8,128)} %param.6, f32[1,2,512,512]{3,2,1,0:T(8,128)S(1)} %copy-done.1), kind=kOutput, calls=%fused_computation.57 | convolution fusion | flops 805568512 | bytes 3145728 | tf_op jit(solution)/shard_map/dot_general | solution.py:14
  73.0 2.2 %fusion.3 = f32[512,256]{1,0:T(8,128)S(1)} fusion(f32[512,256]{1,0:T(8,128)S(1)} %fusion.36, f32[1,2,512,512]{3,2,1,0:T(8,128)S(1)} %copy-done.1, f32[1,2,512,256]{3,2,1,0:T(8,128)} %param.6), kind=kOutput, calls=%fused_computation.16 | convolution fusion | flops 805568512 | bytes 3145728 | tf_op jit(solution)/shard_map/dot_general | solution.py:14
  77.3 3.4 %collective-permute-start.2 = (f32[2,512,256]{2,1,0:T(8,128)}, f32[2,512,256]{2,1,0:T(8,128)}, u32[]{:S(2)}, u32[]{:S(2)}) collective-permute-start(f32[2,512,256]{2,1,0:T(8,128)} %maximum_multiply_fusion), channel_id=1, source_target_pairs={{0,4},{4,8},{8,12},{12,16},{16,20},{20,24},{24,28},{1,5},{5,9},{9,... | collective-permute-start | bytes 3145736 | tf_op jit(solution)/shard_map/ppermute | solution.py:10
  82.2 24.4 %collective-permute-done.2 = f32[2,512,256]{2,1,0:T(8,128)} collective-permute-done((f32[2,512,256]{2,1,0:T(8,128)}, f32[2,512,256]{2,1,0:T(8,128)}, u32[]{:S(2)}, u32[]{:S(2)}) %collective-permute-start.2) | collective-permute-done | bytes 1048608 | tf_op jit(solution)/shard_map/ppermute | solution.py:10
  106.6 2.0 fusion.28
  108.6 2.2 %convolution_subtract_fusion.2 = f32[512,256]{1,0:T(8,128)S(1)} fusion(f32[512,256]{1,0:T(8,128)S(1)} %fusion.28, f32[2,512,512]{2,1,0:T(8,128)S(1)} %copy-done.3, f32[2,512,256]{2,1,0:T(8,128)} %collective-permute-done.2), kind=kOutput, calls=%fused_computation.12 | convolution fusion | flops 805568512 | bytes 3145728 | tf_op jit(solution)/shard_map/dot_general | solution.py:14
  110.9 2.4 %convolution_add_fusion.2 = f32[512,256]{1,0:T(8,128)S(1)} fusion(f32[512,256]{1,0:T(8,128)S(1)} %fusion.28, f32[2,512,512]{2,1,0:T(8,128)S(1)} %copy-done.3, f32[2,512,256]{2,1,0:T(8,128)} %collective-permute-done.2), kind=kOutput, calls=%fused_computation.11 | convolution fusion | flops 805568512 | bytes 3145728 | tf_op jit(solution)/shard_map/dot_general | solution.py:14
  115.8 2.7 %fusion.22 = f32[512,128]{1,0:T(8,128)S(1)} fusion(f32[2,512,512]{2,1,0:T(8,128)} %all-gather.8.cloned.1.call-done, f32[2,512,128]{2,1,0:T(8,128)} %collective-permute-done.1), kind=kOutput, calls=%fused_computation.43 | convolution fusion | flops 402915328 | bytes 2621440 | tf_op jit(solution)/shard_map/dot_general | solution.py:14
  118.5 2.4 %fusion.9 = f32[1,512,128]{2,1,0:T(8,128)S(1)} fusion(f32[512,128]{1,0:T(8,128)S(1)} %fusion.22, f32[2,512,512]{2,1,0:T(8,128)} %all-gather.8.cloned.1.call-done, f32[2,512,128]{2,1,0:T(8,128)} %collective-permute-done.1), kind=kOutput, calls=%fused_computation.26 | convolution fusion | flops 402784256 | bytes 2097152 | tf_op jit(solution)/shard_map/dot_general | solution.py:14
  124.0 16.4 %collective-permute-done.3 = f32[2,512,256]{2,1,0:T(8,128)} collective-permute-done((f32[2,512,256]{2,1,0:T(8,128)}, f32[2,512,256]{2,1,0:T(8,128)}, u32[]{:S(2)}, u32[]{:S(2)}) %collective-permute-start.3) | collective-permute-done | bytes 1048608 | tf_op jit(solution)/shard_map/ppermute | solution.py:10
  140.4 2.0 fusion.20
  142.5 2.3 %convolution_subtract_fusion.1 = f32[512,256]{1,0:T(8,128)S(1)} fusion(f32[512,256]{1,0:T(8,128)S(1)} %fusion.20, f32[2,512,512]{2,1,0:T(8,128)S(1)} %copy-done, f32[2,512,256]{2,1,0:T(8,128)} %collective-permute-done.3), kind=kOutput, calls=%fused_computation.10 | convolution fusion | flops 805568512 | bytes 3145728 | tf_op jit(solution)/shard_map/dot_general | solution.py:14
  144.8 2.4 %convolution_add_fusion.1 = f32[512,256]{1,0:T(8,128)S(1)} fusion(f32[512,256]{1,0:T(8,128)S(1)} %fusion.20, f32[2,512,512]{2,1,0:T(8,128)S(1)} %copy-done, f32[2,512,256]{2,1,0:T(8,128)} %collective-permute-done.3), kind=kOutput, calls=%fused_computation.9 | convolution fusion | flops 805568512 | bytes 3145728 | tf_op jit(solution)/shard_map/dot_general | solution.py:14
  149.5 46.6 %collective-permute-done.4 = f32[2,512,256]{2,1,0:T(8,128)S(1)} collective-permute-done((f32[2,512,256]{2,1,0:T(8,128)S(1)}, f32[2,512,256]{2,1,0:T(8,128)S(1)}, u32[]{:S(2)}, u32[]{:S(2)}) %collective-permute-start.4) | collective-permute-done | bytes 1048608 | tf_op jit(solution)/shard_map/ppermute | solution.py:10
  196.1 2.7 %fusion.14 = f32[512,256]{1,0:T(8,128)S(1)} fusion(f32[2,512,512]{2,1,0:T(8,128)} %all-gather.10.cloned.1.call-done, f32[2,512,256]{2,1,0:T(8,128)S(1)} %collective-permute-done.4), kind=kOutput, calls=%fused_computation.35 | convolution fusion | flops 805568512 | bytes 3145728 | tf_op jit(solution)/shard_map/dot_general | solution.py:14
  (75 shorter events, 18.5 us)
Async XLA Ops:
  6.5 28.9 %copy-start.22 = (f32[1,2,512,128]{3,2,1,0:T(8,128)S(1)}, f32[1,2,512,128]{3,2,1,0:T(8,128)}, u32[]{:S(2)}) copy-start(f32[1,2,512,128]{3,2,1,0:T(8,128)} %param.5) | copy-start | bytes 1572868
  6.5 26.2 %all-gather.12.cloned.1.call-start = ((), (), s32[]{:S(2)}) async-start(), calls=%async_computation.3 | async-start | bytes 2621440 | tf_op jit(solution)/shard_map/all_gather | solution.py:33
  7.3 55.3 %all-gather.6.cloned.1.call-start = ((), (), s32[]{:S(2)}) async-start(), calls=%async_computation | async-start | bytes 2621440 | tf_op jit(solution)/shard_map/all_gather | solution.py:53
  32.7 4.9 %copy-start.1 = (f32[1,2,512,512]{3,2,1,0:T(8,128)S(1)}, f32[1,2,512,512]{3,2,1,0:T(8,128)}, u32[]{:S(2)}) copy-start(f32[1,2,512,512]{3,2,1,0:T(8,128)} %all-gather.12.cloned.1.call-done) | copy-start | bytes 6291460
  38.7 31.1 %copy-start.15 = (f32[1,512,128]{2,1,0:T(8,128)}, f32[1,512,128]{2,1,0:T(8,128)S(1)}, u32[]{:S(2)}) copy-start(f32[1,512,128]{2,1,0:T(8,128)S(1)} %fusion.7) | copy-start | bytes 786436
  39.6 76.1 %all-gather.8.cloned.1.call-start = ((), (), s32[]{:S(2)}) async-start(), calls=%async_computation.1 | async-start | bytes 2621440 | tf_op jit(solution)/shard_map/all_gather | solution.py:53
  39.7 17.1 %collective-permute-start = (f32[2,512,128]{2,1,0:T(8,128)}, f32[2,512,128]{2,1,0:T(8,128)S(1)}, u32[]{:S(2)}, u32[]{:S(2)}) collective-permute-start(f32[2,512,128]{2,1,0:T(8,128)} %maximum_multiply_fusion.2), channel_id=1, source_target_pairs={{0,4},{4,8},{8,12},{12,16},{16,20},{20,24},{24,28},{1,5},{5,9},{9,... | collective-permute-start | bytes 1572872 | tf_op jit(solution)/shard_map/ppermute | solution.py:10
  56.8 5.8 %copy-start.23 = (f32[2,512,128]{2,1,0:T(8,128)}, f32[2,512,128]{2,1,0:T(8,128)S(1)}, u32[]{:S(2)}) copy-start(f32[2,512,128]{2,1,0:T(8,128)S(1)} %collective-permute-done) | copy-start | bytes 1572868
  62.6 5.0 %copy-start.2 = (f32[2,512,512]{2,1,0:T(8,128)S(1)}, f32[2,512,512]{2,1,0:T(8,128)}, u32[]{:S(2)}) copy-start(f32[2,512,512]{2,1,0:T(8,128)} %all-gather.6.cloned.1.call-done) | copy-start | bytes 6291460
  69.8 3.2 %copy-start.20 = (f32[1,512,128]{2,1,0:T(8,128)}, f32[1,512,128]{2,1,0:T(8,128)S(1)}, u32[]{:S(2)}) copy-start(f32[1,512,128]{2,1,0:T(8,128)S(1)} %fusion.10) | copy-start | bytes 786436
  70.7 125.3 %all-gather.10.cloned.1.call-start = ((), (), s32[]{:S(2)}) async-start(), calls=%async_computation.2 | async-start | bytes 2621440 | tf_op jit(solution)/shard_map/all_gather | solution.py:53
  70.8 4.4 %copy-start.17 = (f32[1,2,512,256]{3,2,1,0:T(8,128)S(1)}, f32[1,2,512,256]{3,2,1,0:T(8,128)}, u32[]{:S(2)}) copy-start(f32[1,2,512,256]{3,2,1,0:T(8,128)} %param.6) | copy-start | bytes 3145732
  76.2 30.4 %copy-start.3 = (f32[2,512,512]{2,1,0:T(8,128)S(1)}, f32[2,512,512]{2,1,0:T(8,128)}, u32[]{:S(2)}) copy-start(f32[2,512,512]{2,1,0:T(8,128)} %all-gather.6.cloned.1.call-done) | copy-start | bytes 6291460
  77.3 29.3 %collective-permute-start.2 = (f32[2,512,256]{2,1,0:T(8,128)}, f32[2,512,256]{2,1,0:T(8,128)}, u32[]{:S(2)}, u32[]{:S(2)}) collective-permute-start(f32[2,512,256]{2,1,0:T(8,128)} %maximum_multiply_fusion), channel_id=1, source_target_pairs={{0,4},{4,8},{8,12},{12,16},{16,20},{20,24},{24,28},{1,5},{5,9},{9,... | collective-permute-start | bytes 3145736 | tf_op jit(solution)/shard_map/ppermute | solution.py:10
  80.7 35.0 %collective-permute-start.1 = (f32[2,512,128]{2,1,0:T(8,128)}, f32[2,512,128]{2,1,0:T(8,128)}, u32[]{:S(2)}, u32[]{:S(2)}) collective-permute-start(f32[2,512,128]{2,1,0:T(8,128)} %maximum_select_fusion), channel_id=1, source_target_pairs={{0,8},{4,12},{8,16},{12,20},{16,24},{20,28},{1,9},{5,13},{9,17},{1... | collective-permute-start | bytes 1572872 | tf_op jit(solution)/shard_map/ppermute | solution.py:10
  110.8 3.6 %copy-start.4 = (f32[512,256]{1,0:T(8,128)}, f32[512,256]{1,0:T(8,128)S(1)}, u32[]{:S(2)}) copy-start(f32[512,256]{1,0:T(8,128)S(1)} %convolution_subtract_fusion.2) | copy-start | bytes 1572868
  114.4 26.0 %collective-permute-start.3 = (f32[2,512,256]{2,1,0:T(8,128)}, f32[2,512,256]{2,1,0:T(8,128)}, u32[]{:S(2)}, u32[]{:S(2)}) collective-permute-start(f32[2,512,256]{2,1,0:T(8,128)} %add_select_fusion.4), channel_id=1, source_target_pairs={{0,8},{4,12},{8,16},{12,20},{16,24},{20,28},{1,9},{5,13},{9,17},{1... | collective-permute-start | bytes 3145736 | tf_op jit(solution)/shard_map/ppermute | solution.py:10
  115.8 5.2 %copy-start = (f32[2,512,512]{2,1,0:T(8,128)S(1)}, f32[2,512,512]{2,1,0:T(8,128)}, u32[]{:S(2)}) copy-start(f32[2,512,512]{2,1,0:T(8,128)} %all-gather.8.cloned.1.call-done) | copy-start | bytes 6291460
  118.5 4.5 %copy-start.16 = (f32[1,512,128]{2,1,0:T(8,128)S(1)}, f32[1,512,128]{2,1,0:T(8,128)}, u32[]{:S(2)}) copy-start(f32[1,512,128]{2,1,0:T(8,128)} %copy-done.15) | copy-start | bytes 786436
  118.5 4.5 %copy-start.19 = (f32[1,512,128]{2,1,0:T(8,128)S(1)}, f32[1,512,128]{2,1,0:T(8,128)}, u32[]{:S(2)}) copy-start(f32[1,512,128]{2,1,0:T(8,128)} %copy-done.18) | copy-start | bytes 786436
  118.5 4.5 %copy-start.21 = (f32[1,512,128]{2,1,0:T(8,128)S(1)}, f32[1,512,128]{2,1,0:T(8,128)}, u32[]{:S(2)}) copy-start(f32[1,512,128]{2,1,0:T(8,128)} %copy-done.20) | copy-start | bytes 786436
  142.4 4.7 %copy-start.5 = (f32[512,256]{1,0:T(8,128)S(1)}, f32[512,256]{1,0:T(8,128)}, u32[]{:S(2)}) copy-start(f32[512,256]{1,0:T(8,128)} %copy-done.4) | copy-start | bytes 1572868
  142.4 4.7 %copy-start.8 = (f32[512,256]{1,0:T(8,128)S(1)}, f32[512,256]{1,0:T(8,128)}, u32[]{:S(2)}) copy-start(f32[512,256]{1,0:T(8,128)} %copy-done.7) | copy-start | bytes 1572868
  147.9 48.1 %collective-permute-start.4 = (f32[2,512,256]{2,1,0:T(8,128)S(1)}, f32[2,512,256]{2,1,0:T(8,128)S(1)}, u32[]{:S(2)}, u32[]{:S(2)}) collective-permute-start(f32[2,512,256]{2,1,0:T(8,128)S(1)} %add_select_fusion.3), channel_id=1, source_target_pairs={{0,16},{4,20},{8,24},{12,28},{1,17},{5,21},{9,25},{13,29},{2,18},{... | collective-permute-start | bytes 3145736 | tf_op jit(solution)/shard_map/ppermute | solution.py:10
  (9 other events, 20.1 us)
Sparse Core Ops, SparseCore 0:
  8.9 23.7 all-gather.11
  39.7 22.8 all-gather.5
  70.9 22.8 all-gather.7
  124.1 23.2 all-gather.9
where the time goes:
time: 210 us; the launch traced here: 209 us
  waiting for transfers between devices  132 us (63%)
  matrix products  43.5 us (21%)
  between operations  14.3 us (7%)
  starting transfers between devices  11.1 us (5%)
  other arithmetic  6.77 us (3%)
    ppermute x5, waiting for transfers between devices, passed_along(): return lax.ppermute(shard, axis, pairs)  101 us
    dot_general x21, matrix products, real_product(): jnp.dot(left_side, right_side, precision=lax.Precision.HIGHEST, preferred...  43.5 us
    all_gather x1, waiting for transfers between devices, local(): lax.all_gather(local_inverse, 'col', axis=2, tiled=True)  24.7 us
    ppermute x5, starting transfers between devices, passed_along(): return lax.ppermute(shard, axis, pairs)  11 us
    all_gather x3, waiting for transfers between devices, local(): lax.all_gather(own_map, 'col', axis=2, tiled=True)  5.85 us
  transfers between devices with their start and end apart: 9, of which 6 were waited for; matrix products, arithmetic and copies ran while one was open for 14% of the time, Pallas kernels for 0%

commit v1 on v0

v1 whole, which is shorter than its diff:
```python
import jax
import jax.numpy as jnp
from jax import lax
from jax.sharding import PartitionSpec as P

CHUNKS = 2


def exchange(shard, axis, bit):
    count = lax.axis_size(axis)
    return lax.ppermute(shard, axis, [(i, i ^ bit) for i in range(count)])


def real_product(left_side, right_side):
    return jnp.dot(
        left_side, right_side, precision=lax.Precision.HIGH, preferred_element_type=jnp.float32
    )


def complex_product(left_side, right_side):
    gauss_sum = real_product(left_side[0] + left_side[1], right_side[0])
    gauss_diff = real_product(left_side[0], right_side[1] - right_side[0])
    gauss_cross = real_product(left_side[1], right_side[0] + right_side[1])
    return jnp.stack([gauss_sum - gauss_cross, gauss_sum + gauss_diff])


def in_order(pieces, place):
    bit = 1
    while len(pieces) > 1:
        upper = (place & bit) != 0
        joined = []
        for low, high in zip(pieces[0::2], pieces[1::2]):
            joined.append(
                jnp.concatenate(
                    [jnp.where(upper, high, low), jnp.where(upper, low, high)], axis=2
                )
            )
        pieces = joined
        bit *= 2
    return pieces[0]


def gathered(own):
    pieces = [own]
    bit = lax.axis_size("col") // 2
    parts = {0: own}
    while bit >= 1:
        parts.update({t ^ bit: exchange(v, "col", bit) for t, v in list(parts.items())})
        bit //= 2
    return [parts[t] for t in range(lax.axis_size("col"))]


def local(inverses, couplings, sources, counts):
    own_inverse, own_coupling, own_source = inverses[0], couplings[0], sources[0]
    orbitals = own_inverse.shape[1]
    width = own_source.shape[2]
    half = width // 2
    active = (lax.iota(jnp.int32, orbitals) < counts[0]).astype(jnp.float32)[:, None]
    chain_place = lax.axis_index("chain")
    chain_length = lax.axis_size("chain")
    col_place = lax.axis_index("col")
    odd = (chain_place & 1) == 1

    inverse = in_order(gathered(own_inverse), col_place)
    own_map = complex_product(inverse, own_coupling) * active
    offset = complex_product(inverse, own_source) * active

    other_map = exchange(own_map, "chain", 1)
    kept = jnp.where(odd, offset[:, :, half:], offset[:, :, :half])
    sent = jnp.where(odd, offset[:, :, :half], offset[:, :, half:])
    got = exchange(sent, "chain", 1)
    same = in_order(gathered(own_map), col_place)
    other = in_order(gathered(other_map), col_place)
    first_map = jnp.where(odd, other, same)
    second_map = jnp.where(odd, same, other)
    first_offset = jnp.where(odd, got, kept)
    second_offset = jnp.where(odd, kept, got)

    step = half // CHUNKS
    outs = []
    hops = chain_length // 2 - 1
    states = []
    for c in range(CHUNKS):
        a = first_offset[:, :, c * step:(c + 1) * step]
        b = second_offset[:, :, c * step:(c + 1) * step]
        states.append([a, b, jnp.zeros_like(a), a, complex_product(second_map, a) + b])
    for hop in range(hops):
        pairs = [(2 * hop + i, 2 * hop + 2 + i) for i in range(2)]
        for state in states:
            a, b, come, _, last = state
            come = come + lax.ppermute(last, "chain", pairs)
            first = complex_product(first_map, come) + a
            second = complex_product(second_map, first) + b
            state[2:] = [come, first, second]
    for state in states:
        first, second = state[3:]
        back = exchange(jnp.where(odd, first, second), "chain", 1)
        outs.append((jnp.where(odd, back, first), jnp.where(odd, second, back)))
    return jnp.concatenate([o[0] for o in outs] + [o[1] for o in outs], axis=2)[None]


def solution(mesh):
    placed = (
        P("chain", None, None, "col"),
        P("chain", None, None, "col"),
        P("chain", None, None, "col"),
        P("chain"),
    )
    return jax.shard_map(
        local, mesh=mesh, in_specs=placed, out_specs=P("chain", None, None, "col"), check_vma=False
    )
```

time: 210 us -> 125 us (0.60)
  waiting for transfers between devices: 132 us -> 79.3 us
  matrix products: 43.5 us -> 21.1 us
  between operations: 14.3 us -> 1.37 us
  starting transfers between devices: 11.1 us -> 14.8 us
  local copies, waits for them, and re-layouts: 0.57 us -> 3.7 us
  other arithmetic: 6.77 us -> 4.33 us
    all_gather x4 -> x0, waiting for transfers between devices: 30.6 us -> none  [the longest x1 24.7 us: local(): lax.all_gather(local_inverse, 'col', axis=2, tiled=True)]
    dot_general x21 -> x48, matrix products: 43.5 us -> 21.1 us  [real_product(): jnp.dot(left_side, right_side, precision=lax.Precision.HIGH, preferred_el...]
    ppermute x5 -> x19, waiting for transfers between devices: 101 us -> 79.3 us  [the longest x13 47.8 us: exchange(): return lax.ppermute(shard, axis, [(i, i ^ bit) for i in range(count)])]
    ppermute x5 -> x19, starting transfers between devices: 11 us -> 14.8 us  [the longest x13 9.12 us: exchange(): return lax.ppermute(shard, axis, [(i, i ^ bit) for i in range(count)])]
    select_n x5 -> x15, other arithmetic: 4.73 us -> 2.9 us  [the longest x7 1.32 us: in_order(): jnp.where(upper, high, low)]
  transfers between devices with their start and end apart: 9 -> 19, of which waited for: 6 -> 10; matrix products, arithmetic and copies ran while one was open for 14% -> 4% of each run, Pallas kernels for 0% -> 0%
where the time goes in v1:
time: 125 us
  waiting for transfers between devices  79.3 us (63%)
  matrix products  21.1 us (17%)
  starting transfers between devices  14.8 us (12%)
  other arithmetic  4.33 us (3%)
  local copies, waits for them, and re-layouts  3.7 us (3%)
  between operations  1.37 us (1%)
    ppermute x13, waiting for transfers between devices, exchange(): return lax.ppermute(shard, axis, [(i, i ^ bit) for i in range(count)])  47.8 us
    ppermute x6, waiting for transfers between devices, local(): come = come + lax.ppermute(last, 'chain', pairs)  31.4 us
    dot_general x48, matrix products, real_product(): jnp.dot(left_side, right_side, precision=lax.Precision.HIGH, preferred_el...  21.1 us
    ppermute x13, starting transfers between devices, exchange(): return lax.ppermute(shard, axis, [(i, i ^ bit) for i in range(count)])  9.12 us
    ppermute x6, starting transfers between devices, local(): come = come + lax.ppermute(last, 'chain', pairs)  5.69 us
  transfers between devices with their start and end apart: 19, of which 10 were waited for; matrix products, arithmetic and copies ran while one was open for 4% of the time, Pallas kernels for 0%

profile of v1, /device:TPU:24, one launch (start us, length us, event | category | flops | bytes accessed | tf_op | source)
XLA Modules:
  0.0 124.6 jit_solution(6721764154807007771)
XLA Ops:
  0.0 1.2 copy.5
  1.2 1.6 %collective-permute-start = (f32[2,512,128]{1,2,0:T(8,128)S(1)}, f32[2,512,128]{1,2,0:T(8,128)S(1)}, u32[]{:S(2)}, u32[]{:S(2)}) collective-permute-start(f32[2,512,128]{1,2,0:T(8,128)S(1)} %bitcast.320), channel_id=1, source_target_pairs={{0,2},{1,3},{2,0},{3,1},{4,6},{5,7},{6,4},{7,5},{8,10},{9,11},{10,... | collective-permute-start | bytes 1572872 | tf_op jit(solution)/shard_map/ppermute | solution.py:11
  2.8 12.1 %collective-permute-done = f32[2,512,128]{1,2,0:T(8,128)S(1)} collective-permute-done((f32[2,512,128]{1,2,0:T(8,128)S(1)}, f32[2,512,128]{1,2,0:T(8,128)S(1)}, u32[]{:S(2)}, u32[]{:S(2)}) %collective-permute-start) | collective-permute-done | bytes 524320 | tf_op jit(solution)/shard_map/ppermute | solution.py:11
  15.8 1.1 collective-permute-done.1
  17.4 0.9 copy-done.1
  22.0 1.6 %collective-permute-start.7 = (f32[2,512,128]{1,2,0:T(8,128)S(1)}, f32[2,512,128]{1,2,0:T(8,128)S(1)}, u32[]{:S(2)}, u32[]{:S(2)}) collective-permute-start(f32[2,512,128]{1,2,0:T(8,128)S(1)} %maximum_multiply_fusion.1), channel_id=1, source_target_pairs={{0,2},{1,3},{2,0},{3,1},{4,6},{5,7},{6,4},{7,5},{8,10},{9,11},{10,... | collective-permute-start | bytes 1572872 | tf_op jit(solution)/shard_map/ppermute | solution.py:11
  23.6 1.5 %collective-permute-start.3 = (f32[2,512,128]{1,2,0:T(8,128)S(1)}, f32[2,512,128]{1,2,0:T(8,128)S(1)}, u32[]{:S(2)}, u32[]{:S(2)}) collective-permute-start(f32[2,512,128]{1,2,0:T(8,128)S(1)} %maximum_multiply_fusion.1), channel_id=1, source_target_pairs={{0,4},{4,0},{8,12},{12,8},{16,20},{20,16},{24,28},{28,24},{1,5},{5... | collective-permute-start | bytes 1572872 | tf_op jit(solution)/shard_map/ppermute | solution.py:11
  25.9 12.5 %collective-permute-done.3 = f32[2,512,128]{1,2,0:T(8,128)S(1)} collective-permute-done((f32[2,512,128]{1,2,0:T(8,128)S(1)}, f32[2,512,128]{1,2,0:T(8,128)S(1)}, u32[]{:S(2)}, u32[]{:S(2)}) %collective-permute-start.3) | collective-permute-done | bytes 524320 | tf_op jit(solution)/shard_map/ppermute | solution.py:11
  39.1 9.4 %collective-permute-done.10 = f32[2,512,128]{1,2,0:T(8,128)S(1)} collective-permute-done((f32[2,512,128]{1,2,0:T(8,128)S(1)}, f32[2,512,128]{1,2,0:T(8,128)S(1)}, u32[]{:S(2)}, u32[]{:S(2)}) %collective-permute-start.10) | collective-permute-done | bytes 524320 | tf_op jit(solution)/shard_map/ppermute | solution.py:11
  48.8 3.9 %collective-permute-done.4 = f32[2,512,128]{1,2,0:T(8,128)S(1)} collective-permute-done((f32[2,512,128]{1,2,0:T(8,128)S(1)}, f32[2,512,128]{1,2,0:T(8,128)S(1)}, u32[]{:S(2)}, u32[]{:S(2)}) %collective-permute-start.4) | collective-permute-done | bytes 524320 | tf_op jit(solution)/shard_map/ppermute | solution.py:11
  52.9 1.7 %collective-permute-done.5 = f32[2,512,128]{1,2,0:T(8,128)S(1)} collective-permute-done((f32[2,512,128]{1,2,0:T(8,128)S(1)}, f32[2,512,128]{1,2,0:T(8,128)S(1)}, u32[]{:S(2)}, u32[]{:S(2)}) %collective-permute-start.5) | collective-permute-done | bytes 524320 | tf_op jit(solution)/shard_map/ppermute | solution.py:11
  54.7 0.7 fusion.100
  57.5 0.7 collective-permute-start.11
  61.1 0.9 collective-permute-start.12
  65.1 1.3 %collective-permute-start.13 = (f32[2,512,64]{1,2,0:T(8,128)S(1)}, f32[2,512,64]{1,2,0:T(8,128)S(1)}, u32[]{:S(2)}, u32[]{:S(2)}) collective-permute-start(f32[2,512,64]{1,2,0:T(8,128)S(1)} %maximum_add_fusion.4), channel_id=1, source_target_pairs={{16,24},{20,28},{17,25},{21,29},{18,26},{22,30},{19,27},{23,31}} | collective-permute-start | bytes 786440 | tf_op jit(solution)/shard_map/ppermute | solution.py:91
  67.3 20.2 %collective-permute-done.13 = f32[2,512,64]{1,2,0:T(8,128)S(1)} collective-permute-done((f32[2,512,64]{1,2,0:T(8,128)S(1)}, f32[2,512,64]{1,2,0:T(8,128)S(1)}, u32[]{:S(2)}, u32[]{:S(2)}) %collective-permute-start.13) | collective-permute-done | bytes 262176 | tf_op jit(solution)/shard_map/ppermute | solution.py:91
  90.4 0.7 collective-permute-start.15
  91.1 1.6 %collective-permute-start.14 = (f32[2,512,64]{1,2,0:T(8,128)S(1)}, f32[2,512,64]{1,2,0:T(8,128)S(1)}, u32[]{:S(2)}, u32[]{:S(2)}) collective-permute-start(f32[2,512,64]{1,2,0:T(8,128)S(1)} %get-tuple-element.31), channel_id=1, source_target_pairs={{0,4},{4,0},{8,12},{12,8},{16,20},{20,16},{24,28},{28,24},{1,5},{5... | collective-permute-start | bytes 786440 | tf_op jit(solution)/shard_map/ppermute | solution.py:11
  95.3 2.2 %collective-permute-done.14 = f32[2,512,64]{1,2,0:T(8,128)S(1)} collective-permute-done((f32[2,512,64]{1,2,0:T(8,128)S(1)}, f32[2,512,64]{1,2,0:T(8,128)S(1)}, u32[]{:S(2)}, u32[]{:S(2)}) %collective-permute-start.14) | collective-permute-done | bytes 262176 | tf_op jit(solution)/shard_map/ppermute | solution.py:11
  101.1 1.5 %collective-permute-start.17 = (f32[2,512,64]{1,2,0:T(8,128)S(1)}, f32[2,512,64]{1,2,0:T(8,128)S(1)}, u32[]{:S(2)}, u32[]{:S(2)}) collective-permute-start(f32[2,512,64]{1,2,0:T(8,128)S(1)} %maximum_add_fusion.11), channel_id=1, source_target_pairs={{16,24},{20,28},{17,25},{21,29},{18,26},{22,30},{19,27},{23,31}} | collective-permute-start | bytes 786440 | tf_op jit(solution)/shard_map/ppermute | solution.py:91
  102.7 11.2 %collective-permute-done.17 = f32[2,512,64]{1,2,0:T(8,128)S(1)} collective-permute-done((f32[2,512,64]{1,2,0:T(8,128)S(1)}, f32[2,512,64]{1,2,0:T(8,128)S(1)}, u32[]{:S(2)}, u32[]{:S(2)}) %collective-permute-start.17) | collective-permute-done | bytes 262176 | tf_op jit(solution)/shard_map/ppermute | solution.py:91
  116.6 1.6 %collective-permute-start.18 = (f32[2,512,64]{1,2,0:T(8,128)S(1)}, f32[2,512,64]{1,2,0:T(8,128)S(1)}, u32[]{:S(2)}, u32[]{:S(2)}) collective-permute-start(f32[2,512,64]{1,2,0:T(8,128)S(1)} %broadcast_select_fusion.17), channel_id=1, source_target_pairs={{0,4},{4,0},{8,12},{12,8},{16,20},{20,16},{24,28},{28,24},{1,5},{5... | collective-permute-start | bytes 786440 | tf_op jit(solution)/shard_map/ppermute | solution.py:11
  118.2 4.9 %collective-permute-done.18 = f32[2,512,64]{1,2,0:T(8,128)S(1)} collective-permute-done((f32[2,512,64]{1,2,0:T(8,128)S(1)}, f32[2,512,64]{1,2,0:T(8,128)S(1)}, u32[]{:S(2)}, u32[]{:S(2)}) %collective-permute-start.18) | collective-permute-done | bytes 262176 | tf_op jit(solution)/shard_map/ppermute | solution.py:11
  123.3 1.3 %copy.6 = f32[1,2,512,256]{3,2,1,0:T(8,128)} copy(f32[1,2,512,256]{2,3,1,0:T(8,128)S(1)} %maximum_bitcast_fusion) | data formatting | bytes 2097152 | tf_op jit(solution)/shard_map/broadcast_in_dim | solution.py:99
  (104 shorter events, 27.1 us)
Async XLA Ops:
  1.2 13.7 %collective-permute-start = (f32[2,512,128]{1,2,0:T(8,128)S(1)}, f32[2,512,128]{1,2,0:T(8,128)S(1)}, u32[]{:S(2)}, u32[]{:S(2)}) collective-permute-start(f32[2,512,128]{1,2,0:T(8,128)S(1)} %bitcast.320), channel_id=1, source_target_pairs={{0,2},{1,3},{2,0},{3,1},{4,6},{5,7},{6,4},{7,5},{8,10},{9,11},{10,... | collective-permute-start | bytes 1572872 | tf_op jit(solution)/shard_map/ppermute | solution.py:11
  2.8 12.8 %collective-permute-start.2 = (f32[2,512,128]{1,2,0:T(8,128)S(1)}, f32[2,512,128]{1,2,0:T(8,128)S(1)}, u32[]{:S(2)}, u32[]{:S(2)}) collective-permute-start(f32[2,512,128]{1,2,0:T(8,128)S(1)} %bitcast.321), channel_id=1, source_target_pairs={{0,1},{1,0},{2,3},{3,2},{4,5},{5,4},{6,7},{7,6},{8,9},{9,8},{10,11... | collective-permute-start | bytes 1572872 | tf_op jit(solution)/shard_map/ppermute | solution.py:11
  15.0 1.9 %collective-permute-start.1 = (f32[2,512,128]{1,2,0:T(8,128)S(1)}, f32[2,512,128]{1,2,0:T(8,128)S(1)}, u32[]{:S(2)}, u32[]{:S(2)}) collective-permute-start(f32[2,512,128]{1,2,0:T(8,128)S(1)} %collective-permute-done), channel_id=1, source_target_pairs={{0,1},{1,0},{2,3},{3,2},{4,5},{5,4},{6,7},{7,6},{8,9},{9,8},{10,11... | collective-permute-start | bytes 1572872 | tf_op jit(solution)/shard_map/ppermute | solution.py:11
  17.2 1.0 copy-start.1
  18.8 1.2 copy-start
  22.0 16.9 %collective-permute-start.7 = (f32[2,512,128]{1,2,0:T(8,128)S(1)}, f32[2,512,128]{1,2,0:T(8,128)S(1)}, u32[]{:S(2)}, u32[]{:S(2)}) collective-permute-start(f32[2,512,128]{1,2,0:T(8,128)S(1)} %maximum_multiply_fusion.1), channel_id=1, source_target_pairs={{0,2},{1,3},{2,0},{3,1},{4,6},{5,7},{6,4},{7,5},{8,10},{9,11},{10,... | collective-permute-start | bytes 1572872 | tf_op jit(solution)/shard_map/ppermute | solution.py:11
  23.6 14.8 %collective-permute-start.3 = (f32[2,512,128]{1,2,0:T(8,128)S(1)}, f32[2,512,128]{1,2,0:T(8,128)S(1)}, u32[]{:S(2)}, u32[]{:S(2)}) collective-permute-start(f32[2,512,128]{1,2,0:T(8,128)S(1)} %maximum_multiply_fusion.1), channel_id=1, source_target_pairs={{0,4},{4,0},{8,12},{12,8},{16,20},{20,16},{24,28},{28,24},{1,5},{5... | collective-permute-start | bytes 1572872 | tf_op jit(solution)/shard_map/ppermute | solution.py:11
  25.3 23.2 %collective-permute-start.10 = (f32[2,512,128]{1,2,0:T(8,128)S(1)}, f32[2,512,128]{1,2,0:T(8,128)S(1)}, u32[]{:S(2)}, u32[]{:S(2)}) collective-permute-start(f32[2,512,128]{1,2,0:T(8,128)S(1)} %slice_select_fusion.1), channel_id=1, source_target_pairs={{0,4},{4,0},{8,12},{12,8},{16,20},{20,16},{24,28},{28,24},{1,5},{5... | collective-permute-start | bytes 1572872 | tf_op jit(solution)/shard_map/ppermute | solution.py:11
  25.9 22.8 %collective-permute-start.9 = (f32[2,512,128]{1,2,0:T(8,128)S(1)}, f32[2,512,128]{1,2,0:T(8,128)S(1)}, u32[]{:S(2)}, u32[]{:S(2)}) collective-permute-start(f32[2,512,128]{1,2,0:T(8,128)S(1)} %maximum_multiply_fusion.1), channel_id=1, source_target_pairs={{0,1},{1,0},{2,3},{3,2},{4,5},{5,4},{6,7},{7,6},{8,9},{9,8},{10,11... | collective-permute-start | bytes 1572872 | tf_op jit(solution)/shard_map/ppermute | solution.py:11
  38.4 14.5 %collective-permute-start.6 = (f32[2,512,128]{1,2,0:T(8,128)S(1)}, f32[2,512,128]{1,2,0:T(8,128)S(1)}, u32[]{:S(2)}, u32[]{:S(2)}) collective-permute-start(f32[2,512,128]{1,2,0:T(8,128)S(1)} %collective-permute-done.3), channel_id=1, source_target_pairs={{0,1},{1,0},{2,3},{3,2},{4,5},{5,4},{6,7},{7,6},{8,9},{9,8},{10,11... | collective-permute-start | bytes 1572872 | tf_op jit(solution)/shard_map/ppermute | solution.py:11
  38.4 14.3 %collective-permute-start.4 = (f32[2,512,128]{1,2,0:T(8,128)S(1)}, f32[2,512,128]{1,2,0:T(8,128)S(1)}, u32[]{:S(2)}, u32[]{:S(2)}) collective-permute-start(f32[2,512,128]{1,2,0:T(8,128)S(1)} %collective-permute-done.3), channel_id=1, source_target_pairs={{0,2},{1,3},{2,0},{3,1},{4,6},{5,7},{6,4},{7,5},{8,10},{9,11},{10,... | collective-permute-start | bytes 1572872 | tf_op jit(solution)/shard_map/ppermute | solution.py:11
  38.9 13.8 %collective-permute-start.8 = (f32[2,512,128]{1,2,0:T(8,128)S(1)}, f32[2,512,128]{1,2,0:T(8,128)S(1)}, u32[]{:S(2)}, u32[]{:S(2)}) collective-permute-start(f32[2,512,128]{1,2,0:T(8,128)S(1)} %collective-permute-done.7), channel_id=1, source_target_pairs={{0,1},{1,0},{2,3},{3,2},{4,5},{5,4},{6,7},{7,6},{8,9},{9,8},{10,11... | collective-permute-start | bytes 1572872 | tf_op jit(solution)/shard_map/ppermute | solution.py:11
  52.7 1.9 %collective-permute-start.5 = (f32[2,512,128]{1,2,0:T(8,128)S(1)}, f32[2,512,128]{1,2,0:T(8,128)S(1)}, u32[]{:S(2)}, u32[]{:S(2)}) collective-permute-start(f32[2,512,128]{1,2,0:T(8,128)S(1)} %collective-permute-done.4), channel_id=1, source_target_pairs={{0,1},{1,0},{2,3},{3,2},{4,5},{5,4},{6,7},{7,6},{8,9},{9,8},{10,11... | collective-permute-start | bytes 1572872 | tf_op jit(solution)/shard_map/ppermute | solution.py:11
  57.5 0.9 collective-permute-start.11
  61.1 1.3 %collective-permute-start.12 = (f32[2,512,64]{1,2,0:T(8,128)S(1)}, f32[2,512,64]{1,2,0:T(8,128)S(1)}, u32[]{:S(2)}, u32[]{:S(2)}) collective-permute-start(f32[2,512,64]{1,2,0:T(8,128)S(1)} %maximum_add_fusion.2), channel_id=1, source_target_pairs={{8,16},{12,20},{9,17},{13,21},{10,18},{14,22},{11,19},{15,23}} | collective-permute-start | bytes 786440 | tf_op jit(solution)/shard_map/ppermute | solution.py:91
  65.1 22.4 %collective-permute-start.13 = (f32[2,512,64]{1,2,0:T(8,128)S(1)}, f32[2,512,64]{1,2,0:T(8,128)S(1)}, u32[]{:S(2)}, u32[]{:S(2)}) collective-permute-start(f32[2,512,64]{1,2,0:T(8,128)S(1)} %maximum_add_fusion.4), channel_id=1, source_target_pairs={{16,24},{20,28},{17,25},{21,29},{18,26},{22,30},{19,27},{23,31}} | collective-permute-start | bytes 786440 | tf_op jit(solution)/shard_map/ppermute | solution.py:91
  90.4 2.2 %collective-permute-start.15 = (f32[2,512,64]{1,2,0:T(8,128)S(1)}, f32[2,512,64]{1,2,0:T(8,128)S(1)}, u32[]{:S(2)}, u32[]{:S(2)}) collective-permute-start(f32[2,512,64]{1,2,0:T(8,128)S(1)} %get-tuple-element.32), channel_id=1, source_target_pairs={{0,8},{4,12},{1,9},{5,13},{2,10},{6,14},{3,11},{7,15}} | collective-permute-start | bytes 786440 | tf_op jit(solution)/shard_map/ppermute | solution.py:91
  91.1 6.4 %collective-permute-start.14 = (f32[2,512,64]{1,2,0:T(8,128)S(1)}, f32[2,512,64]{1,2,0:T(8,128)S(1)}, u32[]{:S(2)}, u32[]{:S(2)}) collective-permute-start(f32[2,512,64]{1,2,0:T(8,128)S(1)} %get-tuple-element.31), channel_id=1, source_target_pairs={{0,4},{4,0},{8,12},{12,8},{16,20},{20,16},{24,28},{28,24},{1,5},{5... | collective-permute-start | bytes 786440 | tf_op jit(solution)/shard_map/ppermute | solution.py:11
  97.7 0.7 collective-permute-start.16
  101.1 12.7 %collective-permute-start.17 = (f32[2,512,64]{1,2,0:T(8,128)S(1)}, f32[2,512,64]{1,2,0:T(8,128)S(1)}, u32[]{:S(2)}, u32[]{:S(2)}) collective-permute-start(f32[2,512,64]{1,2,0:T(8,128)S(1)} %maximum_add_fusion.11), channel_id=1, source_target_pairs={{16,24},{20,28},{17,25},{21,29},{18,26},{22,30},{19,27},{23,31}} | collective-permute-start | bytes 786440 | tf_op jit(solution)/shard_map/ppermute | solution.py:91
  116.6 6.4 %collective-permute-start.18 = (f32[2,512,64]{1,2,0:T(8,128)S(1)}, f32[2,512,64]{1,2,0:T(8,128)S(1)}, u32[]{:S(2)}, u32[]{:S(2)}) collective-permute-start(f32[2,512,64]{1,2,0:T(8,128)S(1)} %broadcast_select_fusion.17), channel_id=1, source_target_pairs={{0,4},{4,0},{8,12},{12,8},{16,20},{20,16},{24,28},{28,24},{1,5},{5... | collective-permute-start | bytes 786440 | tf_op jit(solution)/shard_map/ppermute | solution.py:11

commit v2 on v0

v2 whole, which is shorter than its diff:
```python
import functools

import jax
import jax.numpy as jnp
from jax import lax
from jax.experimental import pallas as pl
from jax.experimental.pallas import tpu as pltpu
from jax.sharding import PartitionSpec as P

CHUNKS = 2
ROW_CHUNKS = 2
BF16, F32 = jnp.bfloat16, jnp.float32
WHOLE = pl.BlockSpec(memory_space=pltpu.VMEM)
SCALARS = pl.BlockSpec(memory_space=pltpu.SMEM)


def exchange(shard, axis, bit):
    count = lax.axis_size(axis)
    return lax.ppermute(shard, axis, [(i, i ^ bit) for i in range(count)])


def gathered(own):
    bit = lax.axis_size("col") // 2
    parts = {0: own}
    while bit >= 1:
        parts.update({t ^ bit: exchange(v, "col", bit) for t, v in list(parts.items())})
        bit //= 2
    return [parts[t] for t in range(lax.axis_size("col"))]


def kernel_call(kernel, scalars, arrays, outs, flops):
    return pl.pallas_call(
        kernel,
        out_shape=[jax.ShapeDtypeStruct(s, d) for s, d in outs],
        in_specs=[SCALARS] + [WHOLE] * len(arrays),
        out_specs=[WHOLE] * len(outs),
        compiler_params=pltpu.CompilerParams(vmem_limit_bytes=24 * 2**20),
        cost_estimate=pl.CostEstimate(flops=flops, bytes_accessed=4096, transcendentals=0),
    )(scalars, *arrays)


def split(value):
    high = value.astype(BF16)
    return high, (value - high.astype(F32)).astype(BF16)


def three_pass(left, right, dims):
    dot = functools.partial(lax.dot_general, dimension_numbers=(dims, ((), ())), preferred_element_type=F32)
    return dot(left[0], right[0]) + (dot(left[1], right[0]) + dot(left[0], right[1]))


def both_forms(real, imag):
    return jnp.concatenate(
        [jnp.concatenate([real, -imag], axis=1), jnp.concatenate([imag, real], axis=1)], axis=0
    )


def masked(value, start, count):
    lane = start + lax.broadcasted_iota(jnp.int32, value.shape, 1)
    return jnp.where(lane < count, value, 0.0)


def piece_order(ref, block, place, pieces):
    return jnp.concatenate(
        [ref[:, pl.ds(pl.multiple_of((place ^ t) * block, block), block)] for t in range(pieces)], axis=1
    )


def inverse_product(start, pieces, scal, left, *refs):
    parts = refs[:pieces]
    block = parts[0].shape[2]
    place, count = scal[0], scal[1]
    width = left.shape[1]
    ordered = [piece_order(left.at[i], block, place, pieces) for i in range(2)]
    right = jnp.concatenate([p[i] for i in range(2) for p in parts], axis=1)
    value = three_pass(split(both_forms(*ordered)), split(right), ((1,), (1,)))
    value = masked(value, start, count)
    return width, value


def map_kernel(start, pieces, scal, left, *refs):
    width, value = inverse_product(start, pieces, scal, left, *refs)
    out = refs[pieces]
    out[0] = value[:width]
    out[1] = value[width:]


def offset_kernel(row_chunks, pieces, chunks, scal, left, *refs):
    parts, outs = refs[:row_chunks * pieces], refs[row_chunks * pieces:]
    rows = parts[0].shape[1]
    half = left.shape[1] // 2
    step = half // chunks
    odd = scal[2]
    for r in range(row_chunks):
        for side in range(2):
            first = pl.multiple_of(jnp.where(odd == side, 0, half), half)
            rows_of = left.at[:, pl.ds(first, half)]
            width, value = inverse_product(
                r * rows, pieces, scal, rows_of, *parts[r * pieces:(r + 1) * pieces]
            )
            for c in range(chunks):
                for i in range(2):
                    outs[side * chunks + c][i, :, r * rows:(r + 1) * rows] = value[
                        i * width + c * step:i * width + (c + 1) * step
                    ]


def pack_kernel(row_chunks, pieces, scal, *refs):
    parts, (high, low) = refs[:-2], refs[-2:]
    block, rows = parts[0].shape[1:]
    place, odd = scal[0], scal[2]
    size = block * pieces
    for which in range(2):
        slot = jnp.where(which == 0, odd, 1 - odd)
        for r in range(row_chunks):
            for t in range(pieces):
                part = parts[(which * row_chunks + r) * pieces + t]
                for i in range(2):
                    at = pl.ds(pl.multiple_of((place ^ t) * block + i * size, block), block)
                    high_part, low_part = split(part[i])
                    high[slot, at, r * rows:(r + 1) * rows] = high_part
                    low[slot, at, r * rows:(r + 1) * rows] = low_part


def apply_map(slot, high, low, state):
    count = state.shape[0] // 2
    value = three_pass(
        split(both_forms(state[:count], state[count:])), (high[slot], low[slot]), ((1,), (0,))
    )
    return value


def stacked(ref):
    return jnp.concatenate([ref[0], ref[1]], axis=0)


def stage_kernel(mode, scal, high, low, kept, got, *refs):
    odd = scal[2] == 1
    mine, theirs = stacked(kept), stacked(got)
    first = jnp.where(odd, theirs, mine)
    second = jnp.where(odd, mine, theirs)
    if mode == "first":
        come, outs = None, refs
    elif mode == "middle":
        come, outs = stacked(refs[0]), refs[1:]
    else:
        come, outs = stacked(refs[0]) + stacked(refs[1]), refs[2:]
    if come is not None:
        first = first + apply_map(0, high, low, come)
    second = second + apply_map(1, high, low, first)
    count = kept.shape[1]
    if mode == "last":
        values = [jnp.where(odd, second, first), jnp.where(odd, first, second)]
    else:
        values = [second]
    for out, value in zip(outs, values):
        out[0] = value[:count]
        out[1] = value[count:]


def final_kernel(chunks, scal, *refs):
    keep, back, out = refs[:chunks], refs[chunks:-1], refs[-1]
    half = out.shape[2] // 2
    odd = scal[2]
    for side, pieces in ((0, keep), (1, back)):
        first = pl.multiple_of(jnp.where(odd == side, 0, half), half)
        for i in range(2):
            whole = jnp.concatenate([p[i] for p in pieces], axis=0)
            out[i, :, pl.ds(first, half)] = whole.T


def body(inverses, couplings, sources, counts):
    own_inverse, own_coupling, own_source = inverses[0], couplings[0], sources[0]
    orbitals, block = own_inverse.shape[1:]
    width = own_source.shape[2]
    half = width // 2
    step = half // CHUNKS
    pieces = lax.axis_size("col")
    chain_place = lax.axis_index("chain")
    chain_length = lax.axis_size("chain")
    col_place = lax.axis_index("col")
    scal = jnp.stack([col_place.astype(jnp.int32), counts[0], (chain_place & 1).astype(jnp.int32)])
    rows = orbitals // ROW_CHUNKS
    coupling_t = jnp.swapaxes(own_coupling, 1, 2)
    source_t = jnp.swapaxes(own_source, 1, 2)

    inverse, same, other = [], [], []
    for r in range(ROW_CHUNKS):
        parts = gathered(own_inverse[:, r * rows:(r + 1) * rows])
        inverse += parts
        (own_map,) = kernel_call(
            functools.partial(map_kernel, r * rows, pieces),
            scal,
            [coupling_t, *parts],
            [((2, block, rows), F32)],
            8 * rows * block * orbitals,
        )
        other_map = exchange(own_map, "chain", 1)
        same += gathered(own_map)
        other += gathered(other_map)
    shape = (2, step, orbitals)
    offsets = kernel_call(
        functools.partial(offset_kernel, ROW_CHUNKS, pieces, CHUNKS),
        scal,
        [source_t, *inverse],
        [(shape, F32)] * (2 * CHUNKS),
        8 * orbitals * orbitals * width,
    )
    kept, sent = offsets[:CHUNKS], offsets[CHUNKS:]
    packed = (2, 2 * orbitals, orbitals)
    high, low = kernel_call(
        functools.partial(pack_kernel, ROW_CHUNKS, pieces),
        scal,
        [*same, *other],
        [(packed, BF16)] * 2,
        8 * orbitals * orbitals,
    )
    hops = chain_length // 2 - 1
    flops = 16 * orbitals * orbitals * step
    got, last, come = [], [], [[] for _ in range(CHUNKS)]
    for c in range(CHUNKS):
        got.append(exchange(sent[c], "chain", 1))
        last += kernel_call(
            functools.partial(stage_kernel, "first"),
            scal,
            [high, low, kept[c], got[c]],
            [(shape, F32)],
            flops // 2,
        )
    keep, back = [], []
    for hop in range(hops):
        pairs = [(2 * hop + i, 2 * hop + 2 + i) for i in range(2)]
        for c in range(CHUNKS):
            arrived = lax.ppermute(last[c], "chain", pairs)
            final = hop == hops - 1
            earlier = come[c]
            come[c] = arrived if hop == 0 else earlier + arrived
            if final:
                inputs = [earlier if hop else jnp.zeros_like(arrived), arrived]
            else:
                inputs = [arrived]
            results = kernel_call(
                functools.partial(stage_kernel, "last" if final else "middle"),
                scal,
                [high, low, kept[c], got[c], *inputs],
                [(shape, F32)] * (2 if final else 1),
                flops,
            )
            if final:
                keep.append(results[0])
                back.append(exchange(results[1], "chain", 1))
            else:
                last[c] = results[0]
    (out,) = kernel_call(
        functools.partial(final_kernel, CHUNKS),
        scal,
        [*keep, *back],
        [((2, orbitals, width), F32)],
        orbitals * width,
    )
    return out[None]


def solution(mesh):
    placed = (
        P("chain", None, None, "col"),
        P("chain", None, None, "col"),
        P("chain", None, None, "col"),
        P("chain"),
    )
    return jax.shard_map(
        body, mesh=mesh, in_specs=placed, out_specs=P("chain", None, None, "col"), check_vma=False
    )
```

time: 210 us -> 99.6 us (0.47)
  waiting for transfers between devices: 132 us -> 50.5 us
  matrix products: 43.5 us -> 0 us
  Pallas kernels: 0 us -> 21.1 us
  between operations: 14.3 us -> 0.95 us
  starting transfers between devices: 11.1 us -> 19 us
  other arithmetic: 6.77 us -> 0.15 us
  local copies, waits for them, and re-layouts: 0.57 us -> 6.91 us
    ppermute x5 -> x30, waiting for transfers between devices: 101 us -> 50.5 us  [the longest x24 37.8 us: exchange(): return lax.ppermute(shard, axis, [(i, i ^ bit) for i in range(count)])]
    dot_general x21 -> x0, matrix products: 43.5 us -> none  [real_product(): jnp.dot(left_side, right_side, precision=lax.Precision.HIGHEST, preferred...]
    all_gather x4 -> x0, waiting for transfers between devices: 30.6 us -> none  [the longest x1 24.7 us: local(): lax.all_gather(local_inverse, 'col', axis=2, tiled=True)]
    pallas_call x0 -> x13, Pallas kernels: none -> 21.1 us  [kernel_call(): pl.pallas_call(kernel, out_shape=[jax.ShapeDtypeStruct(s, d) for s, d in...]
    ppermute x5 -> x30, starting transfers between devices: 11 us -> 19 us  [the longest x24 13.7 us: exchange(): return lax.ppermute(shard, axis, [(i, i ^ bit) for i in range(count)])]
    unnamed x48 -> x18, local copies, waits for them, and re-layouts: 0.57 us -> 5.85 us
    select_n x5 -> x0, other arithmetic: 4.73 us -> none  [the longest x3 2.84 us: local(): own_offset = jnp.where(receiving, next_offset, own_offset)]
  transfers between devices with their start and end apart: 9 -> 30, of which waited for: 6 -> 13; matrix products, arithmetic and copies ran while one was open for 14% -> 3% of each run, Pallas kernels for 0% -> 20%
where the time goes in v2:
time: 99.6 us; the launch traced here: 98.6 us
  waiting for transfers between devices  50.5 us (51%)
  Pallas kernels  21.1 us (21%)
  starting transfers between devices  19 us (19%)
  local copies, waits for them, and re-layouts  6.91 us (7%)
    ppermute x24, waiting for transfers between devices, exchange(): return lax.ppermute(shard, axis, [(i, i ^ bit) for i in range(count)])  37.8 us
    pallas_call x13, Pallas kernels, kernel_call(): pl.pallas_call(kernel, out_shape=[jax.ShapeDtypeStruct(s, d) for s, d in...  21.1 us
    ppermute x24, starting transfers between devices, exchange(): return lax.ppermute(shard, axis, [(i, i ^ bit) for i in range(count)])  13.7 us
    ppermute x6, waiting for transfers between devices, body(): arrived = lax.ppermute(last[c], 'chain', pairs)  12.7 us
    unnamed x18, local copies, waits for them, and re-layouts  5.85 us
    ppermute x6, starting transfers between devices, body(): arrived = lax.ppermute(last[c], 'chain', pairs)  5.29 us
  transfers between devices with their start and end apart: 30, of which 13 were waited for; matrix products, arithmetic and copies ran while one was open for 3% of the time, Pallas kernels for 20%

profile of v2, /device:TPU:24, one launch (start us, length us, event | category | flops | bytes accessed | tf_op | source)
XLA Modules:
  0.0 98.6 jit_solution(17495676141070477844)
XLA Ops:
  1.1 1.6 %collective-permute-start.7 = (f32[2,256,128]{2,1,0:T(8,128)S(1)}, f32[2,256,128]{2,1,0:T(8,128)S(1)}, u32[]{:S(2)}, u32[]{:S(2)}) collective-permute-start(f32[2,256,128]{2,1,0:T(8,128)S(1)} %get-tuple-element.25.refs_0_.refs_4_), channel_id=1, source_target_pairs={{0,2},{1,3},{2,0},{3,1},{4,6},{5,7},{6,4},{7,5},{8,10},{9,11},{10,... | collective-permute-start | bytes 786440 | tf_op jit(solution)/shard_map/ppermute | solution.py:19
  3.2 7.1 %collective-permute-done.7.refs_2_.refs_6_ = f32[2,256,128]{2,1,0:T(8,128)S(1)} collective-permute-done((f32[2,256,128]{2,1,0:T(8,128)S(1)}, f32[2,256,128]{2,1,0:T(8,128)S(1)}, u32[]{:S(2)}, u32[]{:S(2)}) %collective-permute-start.7) | collective-permute-done | bytes 262176 | tf_op jit(solution)/shard_map/ppermute | solution.py:19
  12.7 2.1 %collective-permute-done.1.refs_2_ = f32[2,256,128]{2,1,0:T(8,128)S(1)} collective-permute-done((f32[2,256,128]{2,1,0:T(8,128)S(1)}, f32[2,256,128]{2,1,0:T(8,128)S(1)}, u32[]{:S(2)}, u32[]{:S(2)}) %collective-permute-start.1) | collective-permute-done | bytes 262176 | tf_op jit(solution)/shard_map/ppermute | solution.py:19
  16.1 1.6 %collective-permute-start.16 = (f32[2,128,256]{2,1,0:T(8,128)S(1)}, f32[2,128,256]{2,1,0:T(8,128)}, u32[]{:S(2)}, u32[]{:S(2)}) collective-permute-start(f32[2,128,256]{2,1,0:T(8,128)S(1)} %shard_map.47.refs_4_), channel_id=1, source_target_pairs={{0,4},{4,0},{8,12},{12,8},{16,20},{20,16},{24,28},{28,24},{1,5},{5... | collective-permute-start | bytes 786440 | tf_op jit(solution)/shard_map/ppermute | solution.py:19
  17.6 1.5 %collective-permute-start.10 = (f32[2,128,256]{2,1,0:T(8,128)S(1)}, f32[2,128,256]{2,1,0:T(8,128)}, u32[]{:S(2)}, u32[]{:S(2)}) collective-permute-start(f32[2,128,256]{2,1,0:T(8,128)S(1)} %shard_map.47.refs_4_), channel_id=1, source_target_pairs={{0,2},{1,3},{2,0},{3,1},{4,6},{5,7},{6,4},{7,5},{8,10},{9,11},{10,... | collective-permute-start | bytes 786440 | tf_op jit(solution)/shard_map/ppermute | solution.py:19
  21.5 4.0 %collective-permute-done.16.refs_12_ = f32[2,128,256]{2,1,0:T(8,128)} collective-permute-done((f32[2,128,256]{2,1,0:T(8,128)S(1)}, f32[2,128,256]{2,1,0:T(8,128)}, u32[]{:S(2)}, u32[]{:S(2)}) %collective-permute-start.16) | collective-permute-done | bytes 262176 | tf_op jit(solution)/shard_map/ppermute | solution.py:19
  26.9 1.5 %collective-permute-start.18 = (f32[2,128,256]{2,1,0:T(8,128)}, f32[2,128,256]{2,1,0:T(8,128)}, u32[]{:S(2)}, u32[]{:S(2)}) collective-permute-start(f32[2,128,256]{2,1,0:T(8,128)} %collective-permute-done.16.refs_12_), channel_id=1, source_target_pairs={{0,2},{1,3},{2,0},{3,1},{4,6},{5,7},{6,4},{7,5},{8,10},{9,11},{10,... | collective-permute-start | bytes 786440 | tf_op jit(solution)/shard_map/ppermute | solution.py:19
  33.8 1.6 %copy.6 = f32[1,2,512,256]{2,3,1,0:T(8,128)S(1)} copy(f32[1,2,512,256]{3,2,1,0:T(8,128)} %param.6) | data formatting | bytes 2097152 | tf_op args[2]
  35.4 2.8 %collective-permute-done.18.refs_14_ = f32[2,128,256]{2,1,0:T(8,128)} collective-permute-done((f32[2,128,256]{2,1,0:T(8,128)}, f32[2,128,256]{2,1,0:T(8,128)}, u32[]{:S(2)}, u32[]{:S(2)}) %collective-permute-start.18) | collective-permute-done | bytes 262176 | tf_op jit(solution)/shard_map/ppermute | solution.py:19
  38.7 4.4 %collective-permute-done.14.refs_10_ = f32[2,128,256]{2,1,0:T(8,128)} collective-permute-done((f32[2,128,256]{2,1,0:T(8,128)}, f32[2,128,256]{2,1,0:T(8,128)}, u32[]{:S(2)}, u32[]{:S(2)}) %collective-permute-start.14) | collective-permute-done | bytes 262176 | tf_op jit(solution)/shard_map/ppermute | solution.py:19
  44.0 2.5 %shard_map.49 = (f32[2,64,512]{2,1,0:T(8,128)S(1)}, f32[2,64,512]{2,1,0:T(8,128)S(1)}, f32[2,64,512]{2,1,0:T(8,128)S(1)}, f32[2,64,512]{2,1,0:T(8,128)S(1)}) custom-call(s32[3]{0:T(128)S(1)} %pad_add_fusion.scal, f32[2,256,512]{2,1,0:T(8,128)S(1)} %bitcast.12, f32[2,256,128]{2,1,0:T(8,128)S(1)} %get-tuple-element.26.refs_0_, ...), custom_call_target="tpu_custom_call" | custom-call | flops 536870912 | bytes 4096 | tf_op jit(solution)/shard_map/pallas_call | solution.py:32
  48.6 2.0 %shard_map.48 = (bf16[2,1024,512]{2,1,0:T(8,128)(2,1)S(1)}, bf16[2,1024,512]{2,1,0:T(8,128)(2,1)S(1)}) custom-call(s32[3]{0:T(128)S(1)} %pad_add_fusion.scal, f32[2,128,256]{2,1,0:T(8,128)S(1)} %shard_map.46.refs_0_, f32[2,128,256]{2,1,0:T(8,128)S(1)} %copy-done.7, f32[2,128,256]{2,1,0:T(8,128)S(1)} %copy-done.5, ...), custom_call_target="tpu_custom_call" | custom-call | flops 2097152 | bytes 4096 | tf_op jit(solution)/shard_map/pallas_call | solution.py:32
  50.6 5.1 %collective-permute-done.20.got = f32[2,64,512]{2,1,0:T(8,128)S(1)} collective-permute-done((f32[2,64,512]{2,1,0:T(8,128)S(1)}, f32[2,64,512]{2,1,0:T(8,128)S(1)}, u32[]{:S(2)}, u32[]{:S(2)}) %collective-permute-start.20) | collective-permute-done | bytes 262176 | tf_op jit(solution)/shard_map/ppermute | solution.py:19
  57.6 3.3 %collective-permute-done.24.got = f32[2,64,512]{2,1,0:T(8,128)S(1)} collective-permute-done((f32[2,64,512]{2,1,0:T(8,128)S(1)}, f32[2,64,512]{2,1,0:T(8,128)S(1)}, u32[]{:S(2)}, u32[]{:S(2)}) %collective-permute-start.24) | collective-permute-done | bytes 262176 | tf_op jit(solution)/shard_map/ppermute | solution.py:19
  62.7 1.7 %shard_map.51 = f32[2,64,512]{2,1,0:T(8,128)S(1)} custom-call(s32[3]{0:T(128)S(1)} %pad_add_fusion.scal, bf16[2,1024,512]{2,1,0:T(8,128)(2,1)S(1)} %get-tuple-element.15.high, bf16[2,1024,512]{2,1,0:T(8,128)(2,1)S(1)} %get-tuple-element.16.low, f32[2,64,512]{2,1,0:T(8,128)S(1)} %get-tuple-element.17.kept, f32[2,64,512]{2,1,0:T(8,128)S(1)} %collective-permute-done.20.got, ...), custom_call_target="tpu_custom_call" | custom-call | flops 268435456 | bytes 4096 | tf_op jit(solution)/shard_map/pallas_call | solution.py:32
  65.1 1.7 %shard_map.55 = f32[2,64,512]{2,1,0:T(8,128)S(1)} custom-call(s32[3]{0:T(128)S(1)} %pad_add_fusion.scal, bf16[2,1024,512]{2,1,0:T(8,128)(2,1)S(1)} %get-tuple-element.15.high, bf16[2,1024,512]{2,1,0:T(8,128)(2,1)S(1)} %get-tuple-element.16.low, f32[2,64,512]{2,1,0:T(8,128)S(1)} %get-tuple-element.20.kept, f32[2,64,512]{2,1,0:T(8,128)S(1)} %collective-permute-done.24.got, ...), custom_call_target="tpu_custom_call" | custom-call | flops 268435456 | bytes 4096 | tf_op jit(solution)/shard_map/pallas_call | solution.py:32
  67.5 1.7 %shard_map.52 = f32[2,64,512]{2,1,0:T(8,128)S(1)} custom-call(s32[3]{0:T(128)S(1)} %pad_add_fusion.scal, bf16[2,1024,512]{2,1,0:T(8,128)(2,1)S(1)} %get-tuple-element.15.high, bf16[2,1024,512]{2,1,0:T(8,128)(2,1)S(1)} %get-tuple-element.16.low, f32[2,64,512]{2,1,0:T(8,128)S(1)} %get-tuple-element.17.kept, f32[2,64,512]{2,1,0:T(8,128)S(1)} %collective-permute-done.20.got, ...), custom_call_target="tpu_custom_call" | custom-call | flops 268435456 | bytes 4096 | tf_op jit(solution)/shard_map/pallas_call | solution.py:32
  70.5 1.7 %shard_map.56 = f32[2,64,512]{2,1,0:T(8,128)S(1)} custom-call(s32[3]{0:T(128)S(1)} %pad_add_fusion.scal, bf16[2,1024,512]{2,1,0:T(8,128)(2,1)S(1)} %get-tuple-element.15.high, bf16[2,1024,512]{2,1,0:T(8,128)(2,1)S(1)} %get-tuple-element.16.low, f32[2,64,512]{2,1,0:T(8,128)S(1)} %get-tuple-element.20.kept, f32[2,64,512]{2,1,0:T(8,128)S(1)} %collective-permute-done.24.got, ...), custom_call_target="tpu_custom_call" | custom-call | flops 268435456 | bytes 4096 | tf_op jit(solution)/shard_map/pallas_call | solution.py:32
  73.6 8.6 %collective-permute-done.23.refs_1_ = f32[2,64,512]{2,1,0:T(8,128)S(1)} collective-permute-done((f32[2,64,512]{2,1,0:T(8,128)S(1)}, f32[2,64,512]{2,1,0:T(8,128)S(1)}, u32[]{:S(2)}, u32[]{:S(2)}) %collective-permute-start.23) | collective-permute-done | bytes 262176 | tf_op jit(solution)/shard_map/ppermute | solution.py:234
  82.2 1.7 %shard_map.53 = (f32[2,64,512]{2,1,0:T(8,128)S(1)}, f32[2,64,512]{2,1,0:T(8,128)S(1)}) custom-call(s32[3]{0:T(128)S(1)} %pad_add_fusion.scal, bf16[2,1024,512]{2,1,0:T(8,128)(2,1)S(1)} %get-tuple-element.15.high, bf16[2,1024,512]{2,1,0:T(8,128)(2,1)S(1)} %get-tuple-element.16.low, f32[2,64,512]{2,1,0:T(8,128)S(1)} %get-tuple-element.17.kept, ...), custom_call_target="tpu_custom_call" | custom-call | flops 268435456 | bytes 4096 | tf_op jit(solution)/shard_map/pallas_call | solution.py:32
  84.5 4.1 %collective-permute-done.27.refs_1_ = f32[2,64,512]{2,1,0:T(8,128)S(1)} collective-permute-done((f32[2,64,512]{2,1,0:T(8,128)S(1)}, f32[2,64,512]{2,1,0:T(8,128)S(1)}, u32[]{:S(2)}, u32[]{:S(2)}) %collective-permute-start.27) | collective-permute-done | bytes 262176 | tf_op jit(solution)/shard_map/ppermute | solution.py:234
  88.6 1.7 %shard_map.57 = (f32[2,64,512]{2,1,0:T(8,128)S(1)}, f32[2,64,512]{2,1,0:T(8,128)S(1)}) custom-call(s32[3]{0:T(128)S(1)} %pad_add_fusion.scal, bf16[2,1024,512]{2,1,0:T(8,128)(2,1)S(1)} %get-tuple-element.15.high, bf16[2,1024,512]{2,1,0:T(8,128)(2,1)S(1)} %get-tuple-element.16.low, f32[2,64,512]{2,1,0:T(8,128)S(1)} %get-tuple-element.20.kept, ...), custom_call_target="tpu_custom_call" | custom-call | flops 268435456 | bytes 4096 | tf_op jit(solution)/shard_map/pallas_call | solution.py:32
  90.9 5.8 %collective-permute-done.29.refs_3_ = f32[2,64,512]{2,1,0:T(8,128)S(1)} collective-permute-done((f32[2,64,512]{2,1,0:T(8,128)S(1)}, f32[2,64,512]{2,1,0:T(8,128)S(1)}, u32[]{:S(2)}, u32[]{:S(2)}) %collective-permute-start.29) | collective-permute-done | bytes 262176 | tf_op jit(solution)/shard_map/ppermute | solution.py:19
  96.8 1.8 %shard_map.58 = f32[2,512,256]{2,1,0:T(8,128)} custom-call(s32[3]{0:T(128)S(1)} %pad_add_fusion.scal, f32[2,64,512]{2,1,0:T(8,128)S(1)} %get-tuple-element.19.refs_0_, f32[2,64,512]{2,1,0:T(8,128)S(1)} %get-tuple-element.22.refs_1_, f32[2,64,512]{2,1,0:T(8,128)S(1)} %collective-permute-done.28.refs_2_, f32[2,64,512]{2,1,0:T(8,128)S(1)} %collective-permute-done.29.refs_3_), custom_call_target="tpu_custom_call" | custom-call | flops 131072 | bytes 4096 | tf_op jit(solution)/shard_map/pallas_call | solution.py:32
  (71 shorter events, 26.2 us)
Async XLA Ops:
  1.1 9.2 %collective-permute-start.7 = (f32[2,256,128]{2,1,0:T(8,128)S(1)}, f32[2,256,128]{2,1,0:T(8,128)S(1)}, u32[]{:S(2)}, u32[]{:S(2)}) collective-permute-start(f32[2,256,128]{2,1,0:T(8,128)S(1)} %get-tuple-element.25.refs_0_.refs_4_), channel_id=1, source_target_pairs={{0,2},{1,3},{2,0},{3,1},{4,6},{5,7},{6,4},{7,5},{8,10},{9,11},{10,... | collective-permute-start | bytes 786440 | tf_op jit(solution)/shard_map/ppermute | solution.py:19
  2.7 12.1 %collective-permute-start.1 = (f32[2,256,128]{2,1,0:T(8,128)S(1)}, f32[2,256,128]{2,1,0:T(8,128)S(1)}, u32[]{:S(2)}, u32[]{:S(2)}) collective-permute-start(f32[2,256,128]{2,1,0:T(8,128)S(1)} %get-tuple-element.26.refs_0_), channel_id=1, source_target_pairs={{0,2},{1,3},{2,0},{3,1},{4,6},{5,7},{6,4},{7,5},{8,10},{9,11},{10,... | collective-permute-start | bytes 786440 | tf_op jit(solution)/shard_map/ppermute | solution.py:19
  3.2 11.7 %collective-permute-start.6 = (f32[2,256,128]{2,1,0:T(8,128)S(1)}, f32[2,256,128]{2,1,0:T(8,128)S(1)}, u32[]{:S(2)}, u32[]{:S(2)}) collective-permute-start(f32[2,256,128]{2,1,0:T(8,128)S(1)} %get-tuple-element.25.refs_0_.refs_4_), channel_id=1, source_target_pairs={{0,1},{1,0},{2,3},{3,2},{4,5},{5,4},{6,7},{7,6},{8,9},{9,8},{10,11... | collective-permute-start | bytes 786440 | tf_op jit(solution)/shard_map/ppermute | solution.py:19
  10.3 8.8 %collective-permute-start = (f32[2,256,128]{2,1,0:T(8,128)S(1)}, f32[2,256,128]{2,1,0:T(8,128)S(1)}, u32[]{:S(2)}, u32[]{:S(2)}) collective-permute-start(f32[2,256,128]{2,1,0:T(8,128)S(1)} %get-tuple-element.26.refs_0_), channel_id=1, source_target_pairs={{0,1},{1,0},{2,3},{3,2},{4,5},{5,4},{6,7},{7,6},{8,9},{9,8},{10,11... | collective-permute-start | bytes 786440 | tf_op jit(solution)/shard_map/ppermute | solution.py:19
  16.1 9.3 %collective-permute-start.16 = (f32[2,128,256]{2,1,0:T(8,128)S(1)}, f32[2,128,256]{2,1,0:T(8,128)}, u32[]{:S(2)}, u32[]{:S(2)}) collective-permute-start(f32[2,128,256]{2,1,0:T(8,128)S(1)} %shard_map.47.refs_4_), channel_id=1, source_target_pairs={{0,4},{4,0},{8,12},{12,8},{16,20},{20,16},{24,28},{28,24},{1,5},{5... | collective-permute-start | bytes 786440 | tf_op jit(solution)/shard_map/ppermute | solution.py:19
  17.6 9.3 %collective-permute-start.10 = (f32[2,128,256]{2,1,0:T(8,128)S(1)}, f32[2,128,256]{2,1,0:T(8,128)}, u32[]{:S(2)}, u32[]{:S(2)}) collective-permute-start(f32[2,128,256]{2,1,0:T(8,128)S(1)} %shard_map.47.refs_4_), channel_id=1, source_target_pairs={{0,2},{1,3},{2,0},{3,1},{4,6},{5,7},{6,4},{7,5},{8,10},{9,11},{10,... | collective-permute-start | bytes 786440 | tf_op jit(solution)/shard_map/ppermute | solution.py:19
  19.2 9.3 %collective-permute-start.9 = (f32[2,128,256]{2,1,0:T(8,128)S(1)}, f32[2,128,256]{2,1,0:T(8,128)S(1)}, u32[]{:S(2)}, u32[]{:S(2)}) collective-permute-start(f32[2,128,256]{2,1,0:T(8,128)S(1)} %shard_map.47.refs_4_), channel_id=1, source_target_pairs={{0,1},{1,0},{2,3},{3,2},{4,5},{5,4},{6,7},{7,6},{8,9},{9,8},{10,11... | collective-permute-start | bytes 786440 | tf_op jit(solution)/shard_map/ppermute | solution.py:19
  20.4 10.2 %collective-permute-start.12 = (f32[2,128,256]{2,1,0:T(8,128)S(1)}, f32[2,128,256]{2,1,0:T(8,128)}, u32[]{:S(2)}, u32[]{:S(2)}) collective-permute-start(f32[2,128,256]{2,1,0:T(8,128)S(1)} %shard_map.46.refs_0_), channel_id=1, source_target_pairs={{0,4},{4,0},{8,12},{12,8},{16,20},{20,16},{24,28},{28,24},{1,5},{5... | collective-permute-start | bytes 786440 | tf_op jit(solution)/shard_map/ppermute | solution.py:19
  21.0 11.5 %collective-permute-start.4 = (f32[2,128,256]{2,1,0:T(8,128)S(1)}, f32[2,128,256]{2,1,0:T(8,128)S(1)}, u32[]{:S(2)}, u32[]{:S(2)}) collective-permute-start(f32[2,128,256]{2,1,0:T(8,128)S(1)} %shard_map.46.refs_0_), channel_id=1, source_target_pairs={{0,2},{1,3},{2,0},{3,1},{4,6},{5,7},{6,4},{7,5},{8,10},{9,11},{10,... | collective-permute-start | bytes 786440 | tf_op jit(solution)/shard_map/ppermute | solution.py:19
  25.4 7.0 %collective-permute-start.3 = (f32[2,128,256]{2,1,0:T(8,128)S(1)}, f32[2,128,256]{2,1,0:T(8,128)S(1)}, u32[]{:S(2)}, u32[]{:S(2)}) collective-permute-start(f32[2,128,256]{2,1,0:T(8,128)S(1)} %shard_map.46.refs_0_), channel_id=1, source_target_pairs={{0,1},{1,0},{2,3},{3,2},{4,5},{5,4},{6,7},{7,6},{8,9},{9,8},{10,11... | collective-permute-start | bytes 786440 | tf_op jit(solution)/shard_map/ppermute | solution.py:19
  26.9 11.2 %collective-permute-start.18 = (f32[2,128,256]{2,1,0:T(8,128)}, f32[2,128,256]{2,1,0:T(8,128)}, u32[]{:S(2)}, u32[]{:S(2)}) collective-permute-start(f32[2,128,256]{2,1,0:T(8,128)} %collective-permute-done.16.refs_12_), channel_id=1, source_target_pairs={{0,2},{1,3},{2,0},{3,1},{4,6},{5,7},{6,4},{7,5},{8,10},{9,11},{10,... | collective-permute-start | bytes 786440 | tf_op jit(solution)/shard_map/ppermute | solution.py:19
  29.2 9.0 %collective-permute-start.17 = (f32[2,128,256]{2,1,0:T(8,128)}, f32[2,128,256]{2,1,0:T(8,128)}, u32[]{:S(2)}, u32[]{:S(2)}) collective-permute-start(f32[2,128,256]{2,1,0:T(8,128)} %collective-permute-done.16.refs_12_), channel_id=1, source_target_pairs={{0,1},{1,0},{2,3},{3,2},{4,5},{5,4},{6,7},{7,6},{8,9},{9,8},{10,11... | collective-permute-start | bytes 786440 | tf_op jit(solution)/shard_map/ppermute | solution.py:19
  30.6 12.4 %collective-permute-start.14 = (f32[2,128,256]{2,1,0:T(8,128)}, f32[2,128,256]{2,1,0:T(8,128)}, u32[]{:S(2)}, u32[]{:S(2)}) collective-permute-start(f32[2,128,256]{2,1,0:T(8,128)} %collective-permute-done.12.refs_8_), channel_id=1, source_target_pairs={{0,2},{1,3},{2,0},{3,1},{4,6},{5,7},{6,4},{7,5},{8,10},{9,11},{10,... | collective-permute-start | bytes 786440 | tf_op jit(solution)/shard_map/ppermute | solution.py:19
  32.4 14.0 %collective-permute-start.11 = (f32[2,128,256]{2,1,0:T(8,128)}, f32[2,128,256]{2,1,0:T(8,128)}, u32[]{:S(2)}, u32[]{:S(2)}) collective-permute-start(f32[2,128,256]{2,1,0:T(8,128)} %collective-permute-done.10.refs_6_), channel_id=1, source_target_pairs={{0,1},{1,0},{2,3},{3,2},{4,5},{5,4},{6,7},{7,6},{8,9},{9,8},{10,11... | collective-permute-start | bytes 786440 | tf_op jit(solution)/shard_map/ppermute | solution.py:19
  33.8 13.3 %collective-permute-start.13 = (f32[2,128,256]{2,1,0:T(8,128)}, f32[2,128,256]{2,1,0:T(8,128)}, u32[]{:S(2)}, u32[]{:S(2)}) collective-permute-start(f32[2,128,256]{2,1,0:T(8,128)} %collective-permute-done.12.refs_8_), channel_id=1, source_target_pairs={{0,1},{1,0},{2,3},{3,2},{4,5},{5,4},{6,7},{7,6},{8,9},{9,8},{10,11... | collective-permute-start | bytes 786440 | tf_op jit(solution)/shard_map/ppermute | solution.py:19
  38.1 10.4 %collective-permute-start.5 = (f32[2,128,256]{2,1,0:T(8,128)}, f32[2,128,256]{2,1,0:T(8,128)S(1)}, u32[]{:S(2)}, u32[]{:S(2)}) collective-permute-start(f32[2,128,256]{2,1,0:T(8,128)} %copy-done.4), channel_id=1, source_target_pairs={{0,1},{1,0},{2,3},{3,2},{4,5},{5,4},{6,7},{7,6},{8,9},{9,8},{10,11... | collective-permute-start | bytes 786440 | tf_op jit(solution)/shard_map/ppermute | solution.py:19
  38.2 10.4 %collective-permute-start.19 = (f32[2,128,256]{2,1,0:T(8,128)}, f32[2,128,256]{2,1,0:T(8,128)S(1)}, u32[]{:S(2)}, u32[]{:S(2)}) collective-permute-start(f32[2,128,256]{2,1,0:T(8,128)} %collective-permute-done.18.refs_14_), channel_id=1, source_target_pairs={{0,1},{1,0},{2,3},{3,2},{4,5},{5,4},{6,7},{7,6},{8,9},{9,8},{10,11... | collective-permute-start | bytes 786440 | tf_op jit(solution)/shard_map/ppermute | solution.py:19
  46.5 9.2 %collective-permute-start.20 = (f32[2,64,512]{2,1,0:T(8,128)S(1)}, f32[2,64,512]{2,1,0:T(8,128)S(1)}, u32[]{:S(2)}, u32[]{:S(2)}) collective-permute-start(f32[2,64,512]{2,1,0:T(8,128)S(1)} %get-tuple-element.18), channel_id=1, source_target_pairs={{0,4},{4,0},{8,12},{12,8},{16,20},{20,16},{24,28},{28,24},{1,5},{5... | collective-permute-start | bytes 786440 | tf_op jit(solution)/shard_map/ppermute | solution.py:19
  47.1 13.8 %collective-permute-start.24 = (f32[2,64,512]{2,1,0:T(8,128)S(1)}, f32[2,64,512]{2,1,0:T(8,128)S(1)}, u32[]{:S(2)}, u32[]{:S(2)}) collective-permute-start(f32[2,64,512]{2,1,0:T(8,128)S(1)} %get-tuple-element.21), channel_id=1, source_target_pairs={{0,4},{4,0},{8,12},{12,8},{16,20},{20,16},{24,28},{28,24},{1,5},{5... | collective-permute-start | bytes 786440 | tf_op jit(solution)/shard_map/ppermute | solution.py:19
  56.9 5.9 %collective-permute-start.21 = (f32[2,64,512]{2,1,0:T(8,128)S(1)}, f32[2,64,512]{2,1,0:T(8,128)S(1)}, u32[]{:S(2)}, u32[]{:S(2)}) collective-permute-start(f32[2,64,512]{2,1,0:T(8,128)S(1)} %shard_map.50), channel_id=1, source_target_pairs={{0,8},{4,12},{1,9},{5,13},{2,10},{6,14},{3,11},{7,15}} | collective-permute-start | bytes 786440 | tf_op jit(solution)/shard_map/ppermute | solution.py:234
  69.2 13.0 %collective-permute-start.23 = (f32[2,64,512]{2,1,0:T(8,128)S(1)}, f32[2,64,512]{2,1,0:T(8,128)S(1)}, u32[]{:S(2)}, u32[]{:S(2)}) collective-permute-start(f32[2,64,512]{2,1,0:T(8,128)S(1)} %shard_map.52), channel_id=1, source_target_pairs={{16,24},{20,28},{17,25},{21,29},{18,26},{22,30},{19,27},{23,31}} | collective-permute-start | bytes 786440 | tf_op jit(solution)/shard_map/ppermute | solution.py:234
  72.2 16.4 %collective-permute-start.27 = (f32[2,64,512]{2,1,0:T(8,128)S(1)}, f32[2,64,512]{2,1,0:T(8,128)S(1)}, u32[]{:S(2)}, u32[]{:S(2)}) collective-permute-start(f32[2,64,512]{2,1,0:T(8,128)S(1)} %shard_map.56), channel_id=1, source_target_pairs={{16,24},{20,28},{17,25},{21,29},{18,26},{22,30},{19,27},{23,31}} | collective-permute-start | bytes 786440 | tf_op jit(solution)/shard_map/ppermute | solution.py:234
  83.9 7.0 %collective-permute-start.28 = (f32[2,64,512]{2,1,0:T(8,128)S(1)}, f32[2,64,512]{2,1,0:T(8,128)S(1)}, u32[]{:S(2)}, u32[]{:S(2)}) collective-permute-start(f32[2,64,512]{2,1,0:T(8,128)S(1)} %get-tuple-element.23), channel_id=1, source_target_pairs={{0,4},{4,0},{8,12},{12,8},{16,20},{20,16},{24,28},{28,24},{1,5},{5... | collective-permute-start | bytes 786440 | tf_op jit(solution)/shard_map/ppermute | solution.py:19
  90.3 6.4 %collective-permute-start.29 = (f32[2,64,512]{2,1,0:T(8,128)S(1)}, f32[2,64,512]{2,1,0:T(8,128)S(1)}, u32[]{:S(2)}, u32[]{:S(2)}) collective-permute-start(f32[2,64,512]{2,1,0:T(8,128)S(1)} %get-tuple-element.24), channel_id=1, source_target_pairs={{0,4},{4,0},{8,12},{12,8},{16,20},{20,16},{24,28},{28,24},{1,5},{5... | collective-permute-start | bytes 786440 | tf_op jit(solution)/shard_map/ppermute | solution.py:19
  (14 other events, 54.5 us)

commit v3 on v0

v3 whole, which is shorter than its diff:
```python
import functools

import jax
import jax.numpy as jnp
from jax import lax
from jax.experimental import pallas as pl
from jax.experimental.pallas import tpu as pltpu
from jax.sharding import PartitionSpec as P

PARTS = (2, 3, 3)
CHUNKS = len(PARTS)
ROW_CHUNKS = 2
BF16, F32 = jnp.bfloat16, jnp.float32
WHOLE = pl.BlockSpec(memory_space=pltpu.VMEM)


def column_spans(width):
    cuts = [-(-width * sum(PARTS[:c]) // (8 * sum(PARTS))) * 8 for c in range(CHUNKS + 1)]
    return list(zip(cuts, cuts[1:]))


def exchange(shard, axis, bit):
    count = lax.axis_size(axis)
    return lax.ppermute(shard, axis, [(i, i ^ bit) for i in range(count)])


def gathered(own):
    bit = lax.axis_size("col") // 2
    parts = {0: own}
    while bit >= 1:
        parts.update({t ^ bit: exchange(v, "col", bit) for t, v in list(parts.items())})
        bit //= 2
    return [parts[t] for t in range(lax.axis_size("col"))]


def kernel_call(kernel, arrays, outs, flops):
    return pl.pallas_call(
        kernel,
        out_shape=[jax.ShapeDtypeStruct(s, d) for s, d in outs],
        in_specs=[WHOLE] * len(arrays),
        out_specs=[WHOLE] * len(outs),
        compiler_params=pltpu.CompilerParams(vmem_limit_bytes=24 * 2**20),
        cost_estimate=pl.CostEstimate(flops=flops, bytes_accessed=4096, transcendentals=0),
    )(*arrays)


def col_place():
    return lax.axis_index("col").astype(jnp.int32)


def chain_half():
    return lax.axis_index("chain").astype(jnp.int32) & 1


def split(value):
    high = value.astype(BF16)
    return high, (value - high.astype(F32)).astype(BF16)


def three_pass(left, right, dims):
    dot = functools.partial(lax.dot_general, dimension_numbers=(dims, ((), ())), preferred_element_type=F32)
    return dot(left[0], right[0]) + (dot(left[1], right[0]) + dot(left[0], right[1]))


def both_forms(real, imag):
    return jnp.concatenate(
        [jnp.concatenate([real, -imag], axis=1), jnp.concatenate([imag, real], axis=1)], axis=0
    )


def masked(value, active):
    return jnp.where(active > 0.0, value, 0.0)


def couple_kernel(pieces, natural, high, low):
    size = natural.shape[1]
    block = size // pieces
    place = col_place()
    ordered = []
    for i in range(2):
        rows = [
            natural[i, pl.ds(pl.multiple_of((place ^ t) * block, block), block)]
            for t in range(pieces)
        ]
        ordered.append(jnp.concatenate(rows, axis=0).T)
    high[...], low[...] = split(both_forms(*ordered))


def source_kernel(pieces, natural, high, low):
    size, width = natural.shape[1:]
    block, half = size // pieces, width // 2
    place, odd = col_place(), chain_half()
    for side in range(2):
        first = pl.multiple_of(jnp.where(odd == side, 0, half), half)
        ordered = []
        for i in range(2):
            rows = [
                natural[i, pl.ds(pl.multiple_of((place ^ t) * block, block), block), pl.ds(first, half)]
                for t in range(pieces)
            ]
            ordered.append(jnp.concatenate(rows, axis=0).T)
        high[side], low[side] = split(both_forms(*ordered))


def inverse_product(left, parts):
    right = jnp.concatenate([p[i] for i in range(2) for p in parts], axis=1)
    return three_pass(left, split(right), ((1,), (1,)))


def columns_of(refs, first, count):
    half = refs[0].shape[1] // 2
    return [
        jnp.concatenate([ref[:, i * half + first:i * half + first + count] for i in range(2)], axis=1)
        for ref in refs
    ]


def near_kernel(high, low, *refs):
    parts, out = refs[:-1], refs[-1]
    count = sum(p.shape[2] for p in parts)
    out[...] = inverse_product(columns_of((high, low), 0, count), parts)


def map_kernel(start, active, high, low, near, *refs):
    parts, out = refs[:-1], refs[-1]
    count = sum(p.shape[2] for p in parts)
    left = columns_of((high, low), high.shape[1] // 2 - count, count)
    width, rows = out.shape[1:]
    value = masked(near[...] + inverse_product(left, parts), active[:1, start:start + rows])
    out[0] = value[:width]
    out[1] = value[width:]


def offset_kernel(row_chunks, pieces, spans, active, high, low, *refs):
    parts, outs = refs[:row_chunks * pieces], refs[row_chunks * pieces:]
    rows = parts[0].shape[1]
    half = high.shape[1] // 2
    left = [jnp.concatenate([ref[0], ref[1]], axis=0) for ref in (high, low)]
    for r in range(row_chunks):
        value = inverse_product(left, parts[r * pieces:(r + 1) * pieces])
        value = masked(value, active[:1, r * rows:(r + 1) * rows])
        for side in range(2):
            for c, (low_end, high_end) in enumerate(spans):
                for i in range(2):
                    at = (2 * side + i) * half
                    out = outs[side * len(spans) + c]
                    out[i, :, r * rows:(r + 1) * rows] = value[at + low_end:at + high_end]


def pack_kernel(pieces, *refs):
    parts, (high, low) = refs[:-2], refs[-2:]
    block = parts[0].shape[1]
    place, odd = col_place(), chain_half()
    size = block * pieces
    for which in range(2):
        slot = odd if which == 0 else 1 - odd
        for t in range(pieces):
            part = parts[which * pieces + t]
            for i in range(2):
                at = pl.ds(pl.multiple_of((place ^ t) * block + i * size, block), block)
                high[slot, at, :], low[slot, at, :] = split(part[i])


def forms_of(value):
    count = value.shape[0] // 2
    return split(both_forms(value[:count], value[count:]))


def apply_map(left, pair):
    (high, low), (right_high, right_low) = left, pair
    count = high.shape[0]
    dot = functools.partial(jnp.dot, preferred_element_type=F32)
    both = dot(jnp.concatenate([high, low], axis=0), right_high)
    return both[:count] + (both[count:] + dot(high, right_low))


def stacked(ref):
    return jnp.concatenate([ref[0], ref[1]], axis=0)


def put(ref, value, at=slice(None)):
    count = value.shape[0] // 2
    ref[0, :, at] = value[:count]
    ref[1, :, at] = value[count:]


def row_pairs(packs, slot):
    count = len(packs) // 2
    return [(packs[r][slot], packs[count + r][slot]) for r in range(count)]


def apply_maps(left, packs, slot):
    return jnp.concatenate([apply_map(left, pair) for pair in row_pairs(packs, slot)], axis=1)


def stage_kernel(hop, final, kept, got, *refs):
    before, refs = (refs[:3], refs[3:]) if hop else ((), refs)
    packs, outs = (refs[:-2], refs[-2:]) if final else (refs[:-3], refs[-3:])
    turn = lax.axis_index("chain").astype(jnp.int32) >> 1 == hop

    @pl.when(turn)
    def _():
        odd = chain_half() == 1
        mine, theirs = stacked(kept), stacked(got)
        first = jnp.where(odd, theirs, mine)
        if hop:
            first = first + apply_maps(forms_of(stacked(before[0])), packs, 0)
        second = jnp.where(odd, mine, theirs) + apply_maps(forms_of(first), packs, 1)
        if not final:
            put(outs[0], second)
        put(outs[-2], jnp.where(odd, second, first))
        put(outs[-1], jnp.where(odd, first, second))

    if hop:

        @pl.when(jnp.logical_not(turn))
        def _():
            outs[-2][...] = before[1][...]
            outs[-1][...] = before[2][...]


def half_kernel(side, chunks, *refs):
    parts, (out, block, sems) = refs[:chunks], refs[-3:]
    half = block.shape[2]
    first = pl.multiple_of(jnp.where(chain_half() == side, 0, half), half)
    copies = []
    for i in range(2):
        block[i] = jnp.concatenate([p[i] for p in parts], axis=0).T
        copies.append(pltpu.make_async_copy(block.at[i], out.at[i, :, pl.ds(first, half)], sems.at[i]))
        copies[i].start()
    for copy in copies:
        copy.wait()


def body(inverses, couplings, sources, counts):
    own_inverse, own_coupling, own_source = inverses[0], couplings[0], sources[0]
    orbitals, block = own_inverse.shape[1:]
    width = own_source.shape[2]
    half = width // 2
    spans = column_spans(half)
    pieces = lax.axis_size("col")
    far = pieces // 2
    chain_length = lax.axis_size("chain")
    active = (lax.broadcasted_iota(jnp.int32, (8, orbitals), 1) < counts[0]).astype(F32)
    rows = orbitals // ROW_CHUNKS
    flops = 8 * orbitals * orbitals

    couple = kernel_call(
        functools.partial(couple_kernel, pieces),
        [own_coupling],
        [((2 * block, 2 * orbitals), BF16)] * 2,
        flops,
    )
    source = kernel_call(
        functools.partial(source_kernel, pieces),
        [own_source],
        [((2, width, 2 * orbitals), BF16)] * 2,
        flops,
    )
    inverse, packs = [], []
    for r in range(ROW_CHUNKS):
        source_rows = lax.optimization_barrier(own_inverse) if r else own_inverse
        parts = gathered(source_rows[:, r * rows:(r + 1) * rows])
        inverse += parts
        (near,) = kernel_call(
            near_kernel, [*couple, *parts[:far]], [((2 * block, rows), F32)], flops * block
        )
        (own_map,) = kernel_call(
            functools.partial(map_kernel, r * rows),
            [active, *couple, near, *parts[far:]],
            [((2, block, rows), F32)],
            flops * block // ROW_CHUNKS,
        )
        same = gathered(own_map)
        other_map = exchange(own_map, "chain", 1)
        if r % 2 == 0:
            other = [other_map] + [None] * (pieces - 1)
            for t in range(1, far):
                other[t] = exchange(other_map, "col", t)
            for t in range(far, pieces):
                if t == far:
                    other[t] = exchange(same[t], "chain", 1)
                else:
                    other[t] = exchange(other[far], "col", t ^ far)
        else:
            other = gathered(other_map)
        packs.append(
            kernel_call(
                functools.partial(pack_kernel, pieces),
                    [*same, *other],
                [((2, 2 * orbitals, rows), BF16)] * 2,
                flops,
            )
        )
    packs = [p[0] for p in packs] + [p[1] for p in packs]
    shapes = [(2, end - start, orbitals) for start, end in spans]
    offsets = kernel_call(
        functools.partial(offset_kernel, ROW_CHUNKS, pieces, spans),
        [active, *source, *inverse],
        [(shape, F32) for shape in shapes] * 2,
        flops * width,
    )
    kept, sent = offsets[:CHUNKS], offsets[CHUNKS:]
    hops = chain_length // 2 - 1
    got = [exchange(sent[c], "chain", 1) for c in range(CHUNKS)]
    held = [[] for _ in range(CHUNKS)]
    keep, back = [], []
    for hop in range(hops + 1):
        final = hop == hops
        pairs = [(2 * hop + i, 2 * hop + 2 + i) for i in range(2)]
        for c in range(CHUNKS):
            *passed, mine, theirs = kernel_call(
                functools.partial(stage_kernel, hop, final),
                    [kept[c], got[c], *held[c], *packs],
                [(shapes[c], F32)] * (2 if final else 3),
                flops * half,
            )
            if final:
                keep.append(mine)
                back.append(exchange(theirs, "chain", 1))
            else:
                held[c] = [lax.ppermute(passed[0], "chain", pairs), mine, theirs]
    out = None
    for side, parts in enumerate((keep, back)):
        out = pl.pallas_call(
            functools.partial(half_kernel, side, CHUNKS),
            out_shape=jax.ShapeDtypeStruct((2, orbitals, width), F32),
            in_specs=[WHOLE] * CHUNKS + [pl.BlockSpec(memory_space=pl.ANY)] * side,
            out_specs=pl.BlockSpec(memory_space=pl.ANY),
            scratch_shapes=[pltpu.VMEM((2, orbitals, half), F32), pltpu.SemaphoreType.DMA((2,))],
            input_output_aliases={CHUNKS: 0} if side else {},
            compiler_params=pltpu.CompilerParams(vmem_limit_bytes=24 * 2**20),
            cost_estimate=pl.CostEstimate(flops=flops, bytes_accessed=4096, transcendentals=0),
        )(*parts, *([out] if side else []))
    return out[None]


def solution(mesh):
    placed = (
        P("chain", None, None, "col"),
        P("chain", None, None, "col"),
        P("chain", None, None, "col"),
        P("chain"),
    )
    return jax.shard_map(
        body, mesh=mesh, in_specs=placed, out_specs=P("chain", None, None, "col"), check_vma=False
    )
```

time: 210 us -> 90.8 us (0.43)
  waiting for transfers between devices: 132 us -> 50.5 us
  matrix products: 43.5 us -> 0 us
  starting transfers between devices: 11.1 us -> 26.9 us
  between operations: 14.3 us -> 1.01 us
  Pallas kernels: 0 us -> 9.52 us
  other arithmetic: 6.77 us -> 0.01 us
    ppermute x5 -> x35, waiting for transfers between devices: 101 us -> 50.5 us  [the longest x26 38.2 us: exchange(): return lax.ppermute(shard, axis, [(i, i ^ bit) for i in range(count)])]
    dot_general x21 -> x0, matrix products: 43.5 us -> none  [real_product(): jnp.dot(left_side, right_side, precision=lax.Precision.HIGHEST, preferred...]
    all_gather x4 -> x0, waiting for transfers between devices: 30.6 us -> none  [the longest x1 24.7 us: local(): lax.all_gather(local_inverse, 'col', axis=2, tiled=True)]
    ppermute x5 -> x35, starting transfers between devices: 11 us -> 26.9 us  [the longest x26 19.1 us: exchange(): return lax.ppermute(shard, axis, [(i, i ^ bit) for i in range(count)])]
    pallas_call x0 -> x23, Pallas kernels: none -> 9.52 us  [the longest x21 7.64 us: kernel_call(): pl.pallas_call(kernel, out_shape=[jax.ShapeDtypeStruct(s, d) for s, d in...]
    select_n x5 -> x0, other arithmetic: 4.73 us -> none  [the longest x3 2.84 us: local(): own_offset = jnp.where(receiving, next_offset, own_offset)]
  transfers between devices with their start and end apart: 9 -> 35, of which waited for: 6 -> 13; matrix products, arithmetic and copies ran while one was open for 14% -> 0% of each run, Pallas kernels for 0% -> 10%
where the time goes in v3:
time: 90.8 us; the launch traced here: 89.1 us
  waiting for transfers between devices  50.5 us (56%)
  starting transfers between devices  26.9 us (30%)
  Pallas kernels  9.52 us (10%)
  local copies, waits for them, and re-layouts  1.09 us (1%)
  between operations  1.01 us (1%)
    ppermute x26, waiting for transfers between devices, exchange(): return lax.ppermute(shard, axis, [(i, i ^ bit) for i in range(count)])  38.2 us
    ppermute x26, starting transfers between devices, exchange(): return lax.ppermute(shard, axis, [(i, i ^ bit) for i in range(count)])  19.1 us
    ppermute x9, waiting for transfers between devices, body(): held[c] = [lax.ppermute(passed[0], 'chain', pairs), mine, theirs]  12.3 us
    ppermute x9, starting transfers between devices, body(): held[c] = [lax.ppermute(passed[0], 'chain', pairs), mine, theirs]  7.87 us
    pallas_call x21, Pallas kernels, kernel_call(): pl.pallas_call(kernel, out_shape=[jax.ShapeDtypeStruct(s, d) for s, d in...  7.64 us
    pallas_call x2, Pallas kernels, body(): pl.pallas_call(functools.partial(half_kernel, side, CHUNKS), out_shape=ja...  1.88 us
  transfers between devices with their start and end apart: 35, of which 13 were waited for; matrix products, arithmetic and copies ran while one was open for 0% of the time, Pallas kernels for 10%

profile of v3, /device:TPU:24, one launch (start us, length us, event | category | flops | bytes accessed | tf_op | source)
XLA Modules:
  0.0 89.1 jit_solution(11262148416884265874)
XLA Ops:
  1.1 1.6 %collective-permute-start.1 = (f32[2,256,128]{2,1,0:T(8,128)S(1)}, f32[2,256,128]{2,1,0:T(8,128)S(1)}, u32[]{:S(2)}, u32[]{:S(2)}) collective-permute-start(f32[2,256,128]{2,1,0:T(8,128)S(1)} %slice.8.refs_0_), channel_id=1, source_target_pairs={{0,2},{1,3},{2,0},{3,1},{4,6},{5,7},{6,4},{7,5},{8,10},{9,11},{10,... | collective-permute-start | bytes 786440 | tf_op jit(solution)/shard_map/ppermute | solution.py:24
  3.2 7.1 %collective-permute-done.1.refs_2_.refs_0_ = f32[2,256,128]{2,1,0:T(8,128)S(1)} collective-permute-done((f32[2,256,128]{2,1,0:T(8,128)S(1)}, f32[2,256,128]{2,1,0:T(8,128)S(1)}, u32[]{:S(2)}, u32[]{:S(2)}) %collective-permute-start.1) | collective-permute-done | bytes 262176 | tf_op jit(solution)/shard_map/ppermute | solution.py:24
  11.7 3.1 %collective-permute-done.4.refs_6_.refs_0_ = f32[2,256,128]{2,1,0:T(8,128)S(1)} collective-permute-done((f32[2,256,128]{2,1,0:T(8,128)S(1)}, f32[2,256,128]{2,1,0:T(8,128)S(1)}, u32[]{:S(2)}, u32[]{:S(2)}) %collective-permute-start.4) | collective-permute-done | bytes 262176 | tf_op jit(solution)/shard_map/ppermute | solution.py:24
  15.7 1.6 %collective-permute-start.8 = (f32[2,128,256]{2,1,0:T(8,128)S(1)}, f32[2,128,256]{2,1,0:T(8,128)S(1)}, u32[]{:S(2)}, u32[]{:S(2)}) collective-permute-start(f32[2,128,256]{2,1,0:T(8,128)S(1)} %shard_map.50.refs_0_), channel_id=1, source_target_pairs={{0,2},{1,3},{2,0},{3,1},{4,6},{5,7},{6,4},{7,5},{8,10},{9,11},{10,... | collective-permute-start | bytes 786440 | tf_op jit(solution)/shard_map/ppermute | solution.py:24
  18.0 1.5 %collective-permute-start.10 = (f32[2,128,256]{2,1,0:T(8,128)S(1)}, f32[2,128,256]{2,1,0:T(8,128)S(1)}, u32[]{:S(2)}, u32[]{:S(2)}) collective-permute-start(f32[2,128,256]{2,1,0:T(8,128)S(1)} %shard_map.50.refs_0_), channel_id=1, source_target_pairs={{0,4},{4,0},{8,12},{12,8},{16,20},{20,16},{24,28},{28,24},{1,5},{5... | collective-permute-start | bytes 786440 | tf_op jit(solution)/shard_map/ppermute | solution.py:24
  20.5 4.0 %collective-permute-done.8.refs_2_ = f32[2,128,256]{2,1,0:T(8,128)S(1)} collective-permute-done((f32[2,128,256]{2,1,0:T(8,128)S(1)}, f32[2,128,256]{2,1,0:T(8,128)S(1)}, u32[]{:S(2)}, u32[]{:S(2)}) %collective-permute-start.8) | collective-permute-done | bytes 262176 | tf_op jit(solution)/shard_map/ppermute | solution.py:24
  24.4 1.5 %collective-permute-start.12 = (f32[2,128,256]{2,1,0:T(8,128)S(1)}, f32[2,128,256]{2,1,0:T(8,128)S(1)}, u32[]{:S(2)}, u32[]{:S(2)}) collective-permute-start(f32[2,128,256]{2,1,0:T(8,128)S(1)} %collective-permute-done.8.refs_2_), channel_id=1, source_target_pairs={{0,4},{4,0},{8,12},{12,8},{16,20},{20,16},{24,28},{28,24},{1,5},{5... | collective-permute-start | bytes 786440 | tf_op jit(solution)/shard_map/ppermute | solution.py:24
  25.9 1.5 %collective-permute-start.15 = (f32[2,128,256]{2,1,0:T(8,128)S(1)}, f32[2,128,256]{2,1,0:T(8,128)S(1)}, u32[]{:S(2)}, u32[]{:S(2)}) collective-permute-start(f32[2,128,256]{2,1,0:T(8,128)S(1)} %shard_map.53.refs_0_), channel_id=1, source_target_pairs={{0,2},{1,3},{2,0},{3,1},{4,6},{5,7},{6,4},{7,5},{8,10},{9,11},{10,... | collective-permute-start | bytes 786440 | tf_op jit(solution)/shard_map/ppermute | solution.py:24
  27.5 5.3 %collective-permute-done.17.refs_4_ = f32[2,128,256]{2,1,0:T(8,128)S(1)} collective-permute-done((f32[2,128,256]{2,1,0:T(8,128)S(1)}, f32[2,128,256]{2,1,0:T(8,128)S(1)}, u32[]{:S(2)}, u32[]{:S(2)}) %collective-permute-start.17) | collective-permute-done | bytes 262176 | tf_op jit(solution)/shard_map/ppermute | solution.py:24
  33.3 4.4 %collective-permute-done.12.refs_6_ = f32[2,128,256]{2,1,0:T(8,128)S(1)} collective-permute-done((f32[2,128,256]{2,1,0:T(8,128)S(1)}, f32[2,128,256]{2,1,0:T(8,128)S(1)}, u32[]{:S(2)}, u32[]{:S(2)}) %collective-permute-start.12) | collective-permute-done | bytes 262176 | tf_op jit(solution)/shard_map/ppermute | solution.py:24
  38.3 1.4 %collective-permute-done.19.refs_6_ = f32[2,128,256]{2,1,0:T(8,128)S(1)} collective-permute-done((f32[2,128,256]{2,1,0:T(8,128)S(1)}, f32[2,128,256]{2,1,0:T(8,128)S(1)}, u32[]{:S(2)}, u32[]{:S(2)}) %collective-permute-start.19) | collective-permute-done | bytes 262176 | tf_op jit(solution)/shard_map/ppermute | solution.py:24
  40.1 1.8 %shard_map.47 = (f32[2,32,512]{2,1,0:T(8,128)S(1)}, f32[2,48,512]{2,1,0:T(8,128)S(1)}, f32[2,48,512]{2,1,0:T(8,128)S(1)}, f32[2,32,512]{2,1,0:T(8,128)S(1)}, f32...) custom-call(f32[8,512]{1,0:T(8,128)S(1)} %iota.7.active, bf16[2,256,1024]{2,1,0:T(8,128)(2,1)S(1)} %get-tuple-element.52.high, ...), custom_call_target="tpu_custom_call" | custom-call | flops 536870912 | bytes 4096 | tf_op jit(solution)/shard_map/pallas_call | solution.py:37
  41.9 1.6 %collective-permute-start.25 = (f32[2,48,512]{2,1,0:T(8,128)S(1)}, f32[2,48,512]{2,1,0:T(8,128)S(1)}, u32[]{:S(2)}, u32[]{:S(2)}) collective-permute-start(f32[2,48,512]{2,1,0:T(8,128)S(1)} %get-tuple-element.73), channel_id=1, source_target_pairs={{0,4},{4,0},{8,12},{12,8},{16,20},{20,16},{24,28},{28,24},{1,5},{5... | collective-permute-start | bytes 589832 | tf_op jit(solution)/shard_map/ppermute | solution.py:24
  44.6 5.2 %collective-permute-done.25.got = f32[2,48,512]{2,1,0:T(8,128)S(1)} collective-permute-done((f32[2,48,512]{2,1,0:T(8,128)S(1)}, f32[2,48,512]{2,1,0:T(8,128)S(1)}, u32[]{:S(2)}, u32[]{:S(2)}) %collective-permute-start.25) | collective-permute-done | bytes 196640 | tf_op jit(solution)/shard_map/ppermute | solution.py:24
  50.4 3.1 %collective-permute-done.30.got = f32[2,48,512]{2,1,0:T(8,128)S(1)} collective-permute-done((f32[2,48,512]{2,1,0:T(8,128)S(1)}, f32[2,48,512]{2,1,0:T(8,128)S(1)}, u32[]{:S(2)}, u32[]{:S(2)}) %collective-permute-start.30) | collective-permute-done | bytes 196640 | tf_op jit(solution)/shard_map/ppermute | solution.py:24
  54.2 1.6 %collective-permute-start.6 = (f32[2,32,512]{2,1,0:T(8,128)S(1)}, f32[2,32,512]{2,1,0:T(8,128)S(1)}, u32[]{:S(2)}, u32[]{:S(2)}) collective-permute-start(f32[2,32,512]{2,1,0:T(8,128)S(1)} %get-tuple-element.55), channel_id=1, source_target_pairs={{0,4},{4,0},{8,12},{12,8},{16,20},{20,16},{24,28},{28,24},{1,5},{5... | collective-permute-start | bytes 393224 | tf_op jit(solution)/shard_map/ppermute | solution.py:24
  57.2 2.1 %collective-permute-done.6.got = f32[2,32,512]{2,1,0:T(8,128)S(1)} collective-permute-done((f32[2,32,512]{2,1,0:T(8,128)S(1)}, f32[2,32,512]{2,1,0:T(8,128)S(1)}, u32[]{:S(2)}, u32[]{:S(2)}) %collective-permute-start.6) | collective-permute-done | bytes 131104 | tf_op jit(solution)/shard_map/ppermute | solution.py:24
  64.8 5.8 %collective-permute-done.28.refs_0_ = f32[2,48,512]{2,1,0:T(8,128)S(1)} collective-permute-done((f32[2,48,512]{2,1,0:T(8,128)S(1)}, f32[2,48,512]{2,1,0:T(8,128)S(1)}, u32[]{:S(2)}, u32[]{:S(2)}) %collective-permute-start.28) | collective-permute-done | bytes 196640 | tf_op jit(solution)/shard_map/ppermute | solution.py:322
  71.6 1.6 %collective-permute-start.29 = (f32[2,48,512]{2,1,0:T(8,128)S(1)}, f32[2,48,512]{2,1,0:T(8,128)S(1)}, u32[]{:S(2)}, u32[]{:S(2)}) collective-permute-start(f32[2,48,512]{2,1,0:T(8,128)S(1)} %get-tuple-element.83), channel_id=1, source_target_pairs={{0,4},{4,0},{8,12},{12,8},{16,20},{20,16},{24,28},{28,24},{1,5},{5... | collective-permute-start | bytes 589832 | tf_op jit(solution)/shard_map/ppermute | solution.py:24
  73.2 1.7 %collective-permute-done.33.refs_0_ = f32[2,48,512]{2,1,0:T(8,128)S(1)} collective-permute-done((f32[2,48,512]{2,1,0:T(8,128)S(1)}, f32[2,48,512]{2,1,0:T(8,128)S(1)}, u32[]{:S(2)}, u32[]{:S(2)}) %collective-permute-start.33) | collective-permute-done | bytes 196640 | tf_op jit(solution)/shard_map/ppermute | solution.py:322
  75.9 1.5 %collective-permute-start.34 = (f32[2,48,512]{2,1,0:T(8,128)S(1)}, f32[2,48,512]{2,1,0:T(8,128)S(1)}, u32[]{:S(2)}, u32[]{:S(2)}) collective-permute-start(f32[2,48,512]{2,1,0:T(8,128)S(1)} %get-tuple-element.95), channel_id=1, source_target_pairs={{0,4},{4,0},{8,12},{12,8},{16,20},{20,16},{24,28},{28,24},{1,5},{5... | collective-permute-start | bytes 589832 | tf_op jit(solution)/shard_map/ppermute | solution.py:24
  77.4 4.8 %collective-permute-done.23.refs_0_ = f32[2,32,512]{2,1,0:T(8,128)S(1)} collective-permute-done((f32[2,32,512]{2,1,0:T(8,128)S(1)}, f32[2,32,512]{2,1,0:T(8,128)S(1)}, u32[]{:S(2)}, u32[]{:S(2)}) %collective-permute-start.23) | collective-permute-done | bytes 131104 | tf_op jit(solution)/shard_map/ppermute | solution.py:322
  83.1 1.6 %collective-permute-start.24 = (f32[2,32,512]{2,1,0:T(8,128)S(1)}, f32[2,32,512]{2,1,0:T(8,128)S(1)}, u32[]{:S(2)}, u32[]{:S(2)}) collective-permute-start(f32[2,32,512]{2,1,0:T(8,128)S(1)} %get-tuple-element.71), channel_id=1, source_target_pairs={{0,4},{4,0},{8,12},{12,8},{16,20},{20,16},{24,28},{28,24},{1,5},{5... | collective-permute-start | bytes 393224 | tf_op jit(solution)/shard_map/ppermute | solution.py:24
  85.6 2.5 %collective-permute-done.24.refs_0_ = f32[2,32,512]{2,1,0:T(8,128)S(1)} collective-permute-done((f32[2,32,512]{2,1,0:T(8,128)S(1)}, f32[2,32,512]{2,1,0:T(8,128)S(1)}, u32[]{:S(2)}, u32[]{:S(2)}) %collective-permute-start.24) | collective-permute-done | bytes 131104 | tf_op jit(solution)/shard_map/ppermute | solution.py:24
  (79 shorter events, 20.3 us)
Async XLA Ops:
  1.1 9.2 %collective-permute-start.1 = (f32[2,256,128]{2,1,0:T(8,128)S(1)}, f32[2,256,128]{2,1,0:T(8,128)S(1)}, u32[]{:S(2)}, u32[]{:S(2)}) collective-permute-start(f32[2,256,128]{2,1,0:T(8,128)S(1)} %slice.8.refs_0_), channel_id=1, source_target_pairs={{0,2},{1,3},{2,0},{3,1},{4,6},{5,7},{6,4},{7,5},{8,10},{9,11},{10,... | collective-permute-start | bytes 786440 | tf_op jit(solution)/shard_map/ppermute | solution.py:24
  2.7 12.1 %collective-permute-start.4 = (f32[2,256,128]{2,1,0:T(8,128)S(1)}, f32[2,256,128]{2,1,0:T(8,128)S(1)}, u32[]{:S(2)}, u32[]{:S(2)}) collective-permute-start(f32[2,256,128]{2,1,0:T(8,128)S(1)} %slice.9.refs_4_.refs_0_), channel_id=1, source_target_pairs={{0,2},{1,3},{2,0},{3,1},{4,6},{5,7},{6,4},{7,5},{8,10},{9,11},{10,... | collective-permute-start | bytes 786440 | tf_op jit(solution)/shard_map/ppermute | solution.py:24
  3.2 11.6 %collective-permute-start = (f32[2,256,128]{2,1,0:T(8,128)S(1)}, f32[2,256,128]{2,1,0:T(8,128)S(1)}, u32[]{:S(2)}, u32[]{:S(2)}) collective-permute-start(f32[2,256,128]{2,1,0:T(8,128)S(1)} %slice.8.refs_0_), channel_id=1, source_target_pairs={{0,1},{1,0},{2,3},{3,2},{4,5},{5,4},{6,7},{7,6},{8,9},{9,8},{10,11... | collective-permute-start | bytes 786440 | tf_op jit(solution)/shard_map/ppermute | solution.py:24
  10.3 6.9 %collective-permute-start.3 = (f32[2,256,128]{2,1,0:T(8,128)S(1)}, f32[2,256,128]{2,1,0:T(8,128)S(1)}, u32[]{:S(2)}, u32[]{:S(2)}) collective-permute-start(f32[2,256,128]{2,1,0:T(8,128)S(1)} %slice.9.refs_4_.refs_0_), channel_id=1, source_target_pairs={{0,1},{1,0},{2,3},{3,2},{4,5},{5,4},{6,7},{7,6},{8,9},{9,8},{10,11... | collective-permute-start | bytes 786440 | tf_op jit(solution)/shard_map/ppermute | solution.py:24
  15.7 8.8 %collective-permute-start.8 = (f32[2,128,256]{2,1,0:T(8,128)S(1)}, f32[2,128,256]{2,1,0:T(8,128)S(1)}, u32[]{:S(2)}, u32[]{:S(2)}) collective-permute-start(f32[2,128,256]{2,1,0:T(8,128)S(1)} %shard_map.50.refs_0_), channel_id=1, source_target_pairs={{0,2},{1,3},{2,0},{3,1},{4,6},{5,7},{6,4},{7,5},{8,10},{9,11},{10,... | collective-permute-start | bytes 786440 | tf_op jit(solution)/shard_map/ppermute | solution.py:24
  17.7 8.3 %collective-permute-start.7 = (f32[2,128,256]{2,1,0:T(8,128)S(1)}, f32[2,128,256]{2,1,0:T(8,128)S(1)}, u32[]{:S(2)}, u32[]{:S(2)}) collective-permute-start(f32[2,128,256]{2,1,0:T(8,128)S(1)} %shard_map.50.refs_0_), channel_id=1, source_target_pairs={{0,1},{1,0},{2,3},{3,2},{4,5},{5,4},{6,7},{7,6},{8,9},{9,8},{10,11... | collective-permute-start | bytes 786440 | tf_op jit(solution)/shard_map/ppermute | solution.py:24
  18.0 9.5 %collective-permute-start.10 = (f32[2,128,256]{2,1,0:T(8,128)S(1)}, f32[2,128,256]{2,1,0:T(8,128)S(1)}, u32[]{:S(2)}, u32[]{:S(2)}) collective-permute-start(f32[2,128,256]{2,1,0:T(8,128)S(1)} %shard_map.50.refs_0_), channel_id=1, source_target_pairs={{0,4},{4,0},{8,12},{12,8},{16,20},{20,16},{24,28},{28,24},{1,5},{5... | collective-permute-start | bytes 786440 | tf_op jit(solution)/shard_map/ppermute | solution.py:24
  19.9 12.9 %collective-permute-start.17 = (f32[2,128,256]{2,1,0:T(8,128)S(1)}, f32[2,128,256]{2,1,0:T(8,128)S(1)}, u32[]{:S(2)}, u32[]{:S(2)}) collective-permute-start(f32[2,128,256]{2,1,0:T(8,128)S(1)} %shard_map.53.refs_0_), channel_id=1, source_target_pairs={{0,4},{4,0},{8,12},{12,8},{16,20},{20,16},{24,28},{28,24},{1,5},{5... | collective-permute-start | bytes 786440 | tf_op jit(solution)/shard_map/ppermute | solution.py:24
  20.5 12.8 %collective-permute-start.14 = (f32[2,128,256]{2,1,0:T(8,128)S(1)}, f32[2,128,256]{2,1,0:T(8,128)S(1)}, u32[]{:S(2)}, u32[]{:S(2)}) collective-permute-start(f32[2,128,256]{2,1,0:T(8,128)S(1)} %shard_map.53.refs_0_), channel_id=1, source_target_pairs={{0,1},{1,0},{2,3},{3,2},{4,5},{5,4},{6,7},{7,6},{8,9},{9,8},{10,11... | collective-permute-start | bytes 786440 | tf_op jit(solution)/shard_map/ppermute | solution.py:24
  24.4 13.3 %collective-permute-start.12 = (f32[2,128,256]{2,1,0:T(8,128)S(1)}, f32[2,128,256]{2,1,0:T(8,128)S(1)}, u32[]{:S(2)}, u32[]{:S(2)}) collective-permute-start(f32[2,128,256]{2,1,0:T(8,128)S(1)} %collective-permute-done.8.refs_2_), channel_id=1, source_target_pairs={{0,4},{4,0},{8,12},{12,8},{16,20},{20,16},{24,28},{28,24},{1,5},{5... | collective-permute-start | bytes 786440 | tf_op jit(solution)/shard_map/ppermute | solution.py:24
  25.9 11.8 %collective-permute-start.15 = (f32[2,128,256]{2,1,0:T(8,128)S(1)}, f32[2,128,256]{2,1,0:T(8,128)S(1)}, u32[]{:S(2)}, u32[]{:S(2)}) collective-permute-start(f32[2,128,256]{2,1,0:T(8,128)S(1)} %shard_map.53.refs_0_), channel_id=1, source_target_pairs={{0,2},{1,3},{2,0},{3,1},{4,6},{5,7},{6,4},{7,5},{8,10},{9,11},{10,... | collective-permute-start | bytes 786440 | tf_op jit(solution)/shard_map/ppermute | solution.py:24
  27.5 10.8 %collective-permute-start.9 = (f32[2,128,256]{2,1,0:T(8,128)S(1)}, f32[2,128,256]{2,1,0:T(8,128)S(1)}, u32[]{:S(2)}, u32[]{:S(2)}) collective-permute-start(f32[2,128,256]{2,1,0:T(8,128)S(1)} %collective-permute-done.8.refs_2_), channel_id=1, source_target_pairs={{0,1},{1,0},{2,3},{3,2},{4,5},{5,4},{6,7},{7,6},{8,9},{9,8},{10,11... | collective-permute-start | bytes 786440 | tf_op jit(solution)/shard_map/ppermute | solution.py:24
  32.8 7.0 %collective-permute-start.19 = (f32[2,128,256]{2,1,0:T(8,128)S(1)}, f32[2,128,256]{2,1,0:T(8,128)S(1)}, u32[]{:S(2)}, u32[]{:S(2)}) collective-permute-start(f32[2,128,256]{2,1,0:T(8,128)S(1)} %collective-permute-done.17.refs_4_), channel_id=1, source_target_pairs={{0,2},{1,3},{2,0},{3,1},{4,6},{5,7},{6,4},{7,5},{8,10},{9,11},{10,... | collective-permute-start | bytes 786440 | tf_op jit(solution)/shard_map/ppermute | solution.py:24
  33.3 8.7 %collective-permute-start.11 = (f32[2,128,256]{2,1,0:T(8,128)S(1)}, f32[2,128,256]{2,1,0:T(8,128)S(1)}, u32[]{:S(2)}, u32[]{:S(2)}) collective-permute-start(f32[2,128,256]{2,1,0:T(8,128)S(1)} %collective-permute-done.10.refs_4_), channel_id=1, source_target_pairs={{0,1},{1,0},{2,3},{3,2},{4,5},{5,4},{6,7},{7,6},{8,9},{9,8},{10,11... | collective-permute-start | bytes 786440 | tf_op jit(solution)/shard_map/ppermute | solution.py:24
  37.7 6.6 %collective-permute-start.18 = (f32[2,128,256]{2,1,0:T(8,128)S(1)}, f32[2,128,256]{2,1,0:T(8,128)S(1)}, u32[]{:S(2)}, u32[]{:S(2)}) collective-permute-start(f32[2,128,256]{2,1,0:T(8,128)S(1)} %collective-permute-done.17.refs_4_), channel_id=1, source_target_pairs={{0,1},{1,0},{2,3},{3,2},{4,5},{5,4},{6,7},{7,6},{8,9},{9,8},{10,11... | collective-permute-start | bytes 786440 | tf_op jit(solution)/shard_map/ppermute | solution.py:24
  38.2 6.1 %collective-permute-start.16 = (f32[2,128,256]{2,1,0:T(8,128)S(1)}, f32[2,128,256]{2,1,0:T(8,128)S(1)}, u32[]{:S(2)}, u32[]{:S(2)}) collective-permute-start(f32[2,128,256]{2,1,0:T(8,128)S(1)} %collective-permute-done.15.refs_2_), channel_id=1, source_target_pairs={{0,1},{1,0},{2,3},{3,2},{4,5},{5,4},{6,7},{7,6},{8,9},{9,8},{10,11... | collective-permute-start | bytes 786440 | tf_op jit(solution)/shard_map/ppermute | solution.py:24
  41.9 7.8 %collective-permute-start.25 = (f32[2,48,512]{2,1,0:T(8,128)S(1)}, f32[2,48,512]{2,1,0:T(8,128)S(1)}, u32[]{:S(2)}, u32[]{:S(2)}) collective-permute-start(f32[2,48,512]{2,1,0:T(8,128)S(1)} %get-tuple-element.73), channel_id=1, source_target_pairs={{0,4},{4,0},{8,12},{12,8},{16,20},{20,16},{24,28},{28,24},{1,5},{5... | collective-permute-start | bytes 589832 | tf_op jit(solution)/shard_map/ppermute | solution.py:24
  43.5 10.0 %collective-permute-start.30 = (f32[2,48,512]{2,1,0:T(8,128)S(1)}, f32[2,48,512]{2,1,0:T(8,128)S(1)}, u32[]{:S(2)}, u32[]{:S(2)}) collective-permute-start(f32[2,48,512]{2,1,0:T(8,128)S(1)} %get-tuple-element.85), channel_id=1, source_target_pairs={{0,4},{4,0},{8,12},{12,8},{16,20},{20,16},{24,28},{28,24},{1,5},{5... | collective-permute-start | bytes 589832 | tf_op jit(solution)/shard_map/ppermute | solution.py:24
  49.8 6.0 %collective-permute-start.26 = (f32[2,48,512]{2,1,0:T(8,128)S(1)}, f32[2,48,512]{2,1,0:T(8,128)S(1)}, u32[]{:S(2)}, u32[]{:S(2)}) collective-permute-start(f32[2,48,512]{2,1,0:T(8,128)S(1)} %get-tuple-element.74), channel_id=1, source_target_pairs={{0,8},{4,12},{1,9},{5,13},{2,10},{6,14},{3,11},{7,15}} | collective-permute-start | bytes 589832 | tf_op jit(solution)/shard_map/ppermute | solution.py:322
  60.8 9.8 %collective-permute-start.28 = (f32[2,48,512]{2,1,0:T(8,128)S(1)}, f32[2,48,512]{2,1,0:T(8,128)S(1)}, u32[]{:S(2)}, u32[]{:S(2)}) collective-permute-start(f32[2,48,512]{2,1,0:T(8,128)S(1)} %get-tuple-element.80), channel_id=1, source_target_pairs={{16,24},{20,28},{17,25},{21,29},{18,26},{22,30},{19,27},{23,31}} | collective-permute-start | bytes 589832 | tf_op jit(solution)/shard_map/ppermute | solution.py:322
  62.1 12.7 %collective-permute-start.33 = (f32[2,48,512]{2,1,0:T(8,128)S(1)}, f32[2,48,512]{2,1,0:T(8,128)S(1)}, u32[]{:S(2)}, u32[]{:S(2)}) collective-permute-start(f32[2,48,512]{2,1,0:T(8,128)S(1)} %get-tuple-element.92), channel_id=1, source_target_pairs={{16,24},{20,28},{17,25},{21,29},{18,26},{22,30},{19,27},{23,31}} | collective-permute-start | bytes 589832 | tf_op jit(solution)/shard_map/ppermute | solution.py:322
  63.5 18.7 %collective-permute-start.23 = (f32[2,32,512]{2,1,0:T(8,128)S(1)}, f32[2,32,512]{2,1,0:T(8,128)S(1)}, u32[]{:S(2)}, u32[]{:S(2)}) collective-permute-start(f32[2,32,512]{2,1,0:T(8,128)S(1)} %get-tuple-element.68), channel_id=1, source_target_pairs={{16,24},{20,28},{17,25},{21,29},{18,26},{22,30},{19,27},{23,31}} | collective-permute-start | bytes 393224 | tf_op jit(solution)/shard_map/ppermute | solution.py:322
  71.6 16.5 %collective-permute-start.29 = (f32[2,48,512]{2,1,0:T(8,128)S(1)}, f32[2,48,512]{2,1,0:T(8,128)S(1)}, u32[]{:S(2)}, u32[]{:S(2)}) collective-permute-start(f32[2,48,512]{2,1,0:T(8,128)S(1)} %get-tuple-element.83), channel_id=1, source_target_pairs={{0,4},{4,0},{8,12},{12,8},{16,20},{20,16},{24,28},{28,24},{1,5},{5... | collective-permute-start | bytes 589832 | tf_op jit(solution)/shard_map/ppermute | solution.py:24
  75.9 12.2 %collective-permute-start.34 = (f32[2,48,512]{2,1,0:T(8,128)S(1)}, f32[2,48,512]{2,1,0:T(8,128)S(1)}, u32[]{:S(2)}, u32[]{:S(2)}) collective-permute-start(f32[2,48,512]{2,1,0:T(8,128)S(1)} %get-tuple-element.95), channel_id=1, source_target_pairs={{0,4},{4,0},{8,12},{12,8},{16,20},{20,16},{24,28},{28,24},{1,5},{5... | collective-permute-start | bytes 589832 | tf_op jit(solution)/shard_map/ppermute | solution.py:24
  (14 other events, 83.7 us)

commit v4 on v3

--- a/solution.py
+++ b/solution.py
@@ -7,7 +7,7 @@
 from jax.experimental.pallas import tpu as pltpu
 from jax.sharding import PartitionSpec as P
 
-PARTS = (2, 3, 3)
+PARTS = (1, 1, 1, 1)
 CHUNKS = len(PARTS)
 ROW_CHUNKS = 2
 BF16, F32 = jnp.bfloat16, jnp.float32
@@ -193,8 +193,9 @@
     return jnp.concatenate([apply_map(left, pair) for pair in row_pairs(packs, slot)], axis=1)
 
 
-def stage_kernel(hop, final, kept, got, *refs):
-    before, refs = (refs[:3], refs[3:]) if hop else ((), refs)
+def stage_kernel(hop, final, early, kept, got, *refs):
+    count = (2 if early else 3) if hop else 0
+    before, refs = refs[:count], refs[count:]
     packs, outs = (refs[:-2], refs[-2:]) if final else (refs[:-3], refs[-3:])
     turn = lax.axis_index("chain").astype(jnp.int32) >> 1 == hop
 
@@ -216,16 +217,21 @@
         @pl.when(jnp.logical_not(turn))
         def _():
             outs[-2][...] = before[1][...]
-            outs[-1][...] = before[2][...]
-
-
-def half_kernel(side, chunks, *refs):
-    parts, (out, block, sems) = refs[:chunks], refs[-3:]
+            if not early:
+                outs[-1][...] = before[2][...]
+
+
+def half_kernel(side, chunks, hops, *refs):
+    parts, (out, block, sems) = refs[:-3 - side], refs[-3:]
     half = block.shape[2]
     first = pl.multiple_of(jnp.where(chain_half() == side, 0, half), half)
+    last = lax.axis_index("chain").astype(jnp.int32) >> 1 == hops
     copies = []
     for i in range(2):
-        block[i] = jnp.concatenate([p[i] for p in parts], axis=0).T
+        pieces = [p[i] for p in parts]
+        if len(pieces) > chunks:
+            pieces = [jnp.where(last, pieces[1], pieces[0])] + pieces[2:]
+        block[i] = jnp.concatenate(pieces, axis=0).T
         copies.append(pltpu.make_async_copy(block.at[i], out.at[i, :, pl.ds(first, half)], sems.at[i]))
         copies[i].start()
     for copy in copies:
@@ -310,25 +316,31 @@
         pairs = [(2 * hop + i, 2 * hop + 2 + i) for i in range(2)]
         for c in range(CHUNKS):
             *passed, mine, theirs = kernel_call(
-                functools.partial(stage_kernel, hop, final),
+                functools.partial(stage_kernel, hop, final, final and c == 0),
                     [kept[c], got[c], *held[c], *packs],
                 [(shapes[c], F32)] * (2 if final else 3),
                 flops * half,
             )
-            if final:
-                keep.append(mine)
+            if not final:
+                held[c] = [lax.ppermute(passed[0], "chain", pairs), mine, theirs]
+                if c == 0 and hop == hops - 1:
+                    early = exchange(held[c].pop(), "chain", 1)
+                continue
+            keep.append(mine)
+            if c == 0 and hops:
+                own = [(2 * hops + i, 2 * hops + 1 - i) for i in range(2)]
+                back += [early, lax.ppermute(theirs, "chain", own)]
+            else:
                 back.append(exchange(theirs, "chain", 1))
-            else:
-                held[c] = [lax.ppermute(passed[0], "chain", pairs), mine, theirs]
     out = None
     for side, parts in enumerate((keep, back)):
         out = pl.pallas_call(
-            functools.partial(half_kernel, side, CHUNKS),
+            functools.partial(half_kernel, side, CHUNKS, hops),
             out_shape=jax.ShapeDtypeStruct((2, orbitals, width), F32),
-            in_specs=[WHOLE] * CHUNKS + [pl.BlockSpec(memory_space=pl.ANY)] * side,
+            in_specs=[WHOLE] * len(parts) + [pl.BlockSpec(memory_space=pl.ANY)] * side,
             out_specs=pl.BlockSpec(memory_space=pl.ANY),
             scratch_shapes=[pltpu.VMEM((2, orbitals, half), F32), pltpu.SemaphoreType.DMA((2,))],
-            input_output_aliases={CHUNKS: 0} if side else {},
+            input_output_aliases={len(parts): 0} if side else {},
             compiler_params=pltpu.CompilerParams(vmem_limit_bytes=24 * 2**20),
             cost_estimate=pl.CostEstimate(flops=flops, bytes_accessed=4096, transcendentals=0),
         )(*parts, *([out] if side else []))

time: 90.8 us -> 89.9 us (0.990)
  the two profiles are of different devices: /device:TPU:24 before, /device:TPU:16 now
where the time goes in v4:
time: 89.9 us; the launch traced here: 89.6 us
  waiting for transfers between devices  44.9 us (50%)
  starting transfers between devices  32 us (36%)
  Pallas kernels  10.4 us (12%)
  between operations  1.23 us (1%)
  local copies, waits for them, and re-layouts  1.09 us (1%)
    ppermute x28, waiting for transfers between devices, exchange(): return lax.ppermute(shard, axis, [(i, i ^ bit) for i in range(count)])  41.3 us
    ppermute x28, starting transfers between devices, exchange(): return lax.ppermute(shard, axis, [(i, i ^ bit) for i in range(count)])  18.4 us
    ppermute x12, starting transfers between devices, body(): held[c] = [lax.ppermute(passed[0], 'chain', pairs), mine, theirs]  13 us
    pallas_call x25, Pallas kernels, kernel_call(): pl.pallas_call(kernel, out_shape=[jax.ShapeDtypeStruct(s, d) for s, d in...  8.46 us
    ppermute x12, waiting for transfers between devices, body(): held[c] = [lax.ppermute(passed[0], 'chain', pairs), mine, theirs]  3.56 us
    pallas_call x2, Pallas kernels, body(): pl.pallas_call(functools.partial(half_kernel, side, CHUNKS, hops), out_sh...  1.89 us
  transfers between devices with their start and end apart: 41, of which 18 were waited for; matrix products, arithmetic and copies ran while one was open for 0% of the time, Pallas kernels for 10%

profile of v4, /device:TPU:16, one launch (start us, length us, event | category | flops | bytes accessed | tf_op | source)
XLA Modules:
  0.0 89.6 jit_solution(11893204586089769395)
XLA Ops:
  1.1 1.6 %collective-permute-start.1 = (f32[2,256,128]{2,1,0:T(8,128)S(1)}, f32[2,256,128]{2,1,0:T(8,128)S(1)}, u32[]{:S(2)}, u32[]{:S(2)}) collective-permute-start(f32[2,256,128]{2,1,0:T(8,128)S(1)} %slice.8.refs_0_), channel_id=1, source_target_pairs={{0,2},{1,3},{2,0},{3,1},{4,6},{5,7},{6,4},{7,5},{8,10},{9,11},{10,... | collective-permute-start | bytes 786440 | tf_op jit(solution)/shard_map/ppermute | solution.py:24
  3.2 7.1 %collective-permute-done.1.refs_2_.refs_0_ = f32[2,256,128]{2,1,0:T(8,128)S(1)} collective-permute-done((f32[2,256,128]{2,1,0:T(8,128)S(1)}, f32[2,256,128]{2,1,0:T(8,128)S(1)}, u32[]{:S(2)}, u32[]{:S(2)}) %collective-permute-start.1) | collective-permute-done | bytes 262176 | tf_op jit(solution)/shard_map/ppermute | solution.py:24
  10.8 4.0 %collective-permute-done.4.refs_6_.refs_0_ = f32[2,256,128]{2,1,0:T(8,128)S(1)} collective-permute-done((f32[2,256,128]{2,1,0:T(8,128)S(1)}, f32[2,256,128]{2,1,0:T(8,128)S(1)}, u32[]{:S(2)}, u32[]{:S(2)}) %collective-permute-start.4) | collective-permute-done | bytes 262176 | tf_op jit(solution)/shard_map/ppermute | solution.py:24
  17.1 1.5 %collective-permute-start.8 = (f32[2,128,256]{2,1,0:T(8,128)S(1)}, f32[2,128,256]{2,1,0:T(8,128)S(1)}, u32[]{:S(2)}, u32[]{:S(2)}) collective-permute-start(f32[2,128,256]{2,1,0:T(8,128)S(1)} %shard_map.50.refs_0_), channel_id=1, source_target_pairs={{0,2},{1,3},{2,0},{3,1},{4,6},{5,7},{6,4},{7,5},{8,10},{9,11},{10,... | collective-permute-start | bytes 786440 | tf_op jit(solution)/shard_map/ppermute | solution.py:24
  18.6 1.5 %collective-permute-start.10 = (f32[2,128,256]{2,1,0:T(8,128)S(1)}, f32[2,128,256]{2,1,0:T(8,128)S(1)}, u32[]{:S(2)}, u32[]{:S(2)}) collective-permute-start(f32[2,128,256]{2,1,0:T(8,128)S(1)} %shard_map.50.refs_0_), channel_id=1, source_target_pairs={{0,4},{4,0},{8,12},{12,8},{16,20},{20,16},{24,28},{28,24},{1,5},{5... | collective-permute-start | bytes 786440 | tf_op jit(solution)/shard_map/ppermute | solution.py:24
  22.1 4.0 %collective-permute-done.8.refs_2_ = f32[2,128,256]{2,1,0:T(8,128)S(1)} collective-permute-done((f32[2,128,256]{2,1,0:T(8,128)S(1)}, f32[2,128,256]{2,1,0:T(8,128)S(1)}, u32[]{:S(2)}, u32[]{:S(2)}) %collective-permute-start.8) | collective-permute-done | bytes 262176 | tf_op jit(solution)/shard_map/ppermute | solution.py:24
  26.1 1.7 %collective-permute-done.10.refs_4_ = f32[2,128,256]{2,1,0:T(8,128)S(1)} collective-permute-done((f32[2,128,256]{2,1,0:T(8,128)S(1)}, f32[2,128,256]{2,1,0:T(8,128)S(1)}, u32[]{:S(2)}, u32[]{:S(2)}) %collective-permute-start.10) | collective-permute-done | bytes 262176 | tf_op jit(solution)/shard_map/ppermute | solution.py:24
  27.8 1.5 %collective-permute-start.12 = (f32[2,128,256]{2,1,0:T(8,128)S(1)}, f32[2,128,256]{2,1,0:T(8,128)S(1)}, u32[]{:S(2)}, u32[]{:S(2)}) collective-permute-start(f32[2,128,256]{2,1,0:T(8,128)S(1)} %collective-permute-done.8.refs_2_), channel_id=1, source_target_pairs={{0,4},{4,0},{8,12},{12,8},{16,20},{20,16},{24,28},{28,24},{1,5},{5... | collective-permute-start | bytes 786440 | tf_op jit(solution)/shard_map/ppermute | solution.py:24
  29.3 4.1 %collective-permute-done.17.refs_4_ = f32[2,128,256]{2,1,0:T(8,128)S(1)} collective-permute-done((f32[2,128,256]{2,1,0:T(8,128)S(1)}, f32[2,128,256]{2,1,0:T(8,128)S(1)}, u32[]{:S(2)}, u32[]{:S(2)}) %collective-permute-start.17) | collective-permute-done | bytes 262176 | tf_op jit(solution)/shard_map/ppermute | solution.py:24
  34.5 3.3 %collective-permute-done.12.refs_6_ = f32[2,128,256]{2,1,0:T(8,128)S(1)} collective-permute-done((f32[2,128,256]{2,1,0:T(8,128)S(1)}, f32[2,128,256]{2,1,0:T(8,128)S(1)}, u32[]{:S(2)}, u32[]{:S(2)}) %collective-permute-start.12) | collective-permute-done | bytes 262176 | tf_op jit(solution)/shard_map/ppermute | solution.py:24
  37.9 1.9 %collective-permute-done.19.refs_6_ = f32[2,128,256]{2,1,0:T(8,128)S(1)} collective-permute-done((f32[2,128,256]{2,1,0:T(8,128)S(1)}, f32[2,128,256]{2,1,0:T(8,128)S(1)}, u32[]{:S(2)}, u32[]{:S(2)}) %collective-permute-start.19) | collective-permute-done | bytes 262176 | tf_op jit(solution)/shard_map/ppermute | solution.py:24
  40.2 1.8 %shard_map.47 = (f32[2,32,512]{2,1,0:T(8,128)S(1)}, f32[2,32,512]{2,1,0:T(8,128)S(1)}, f32[2,32,512]{2,1,0:T(8,128)S(1)}, f32[2,32,512]{2,1,0:T(8,128)S(1)}, f32...) custom-call(f32[8,512]{1,0:T(8,128)S(1)} %iota.7.active, ...), custom_call_target="tpu_custom_call" | custom-call | flops 536870912 | bytes 4096 | tf_op jit(solution)/shard_map/pallas_call | solution.py:37
  42.0 1.6 %collective-permute-start.6 = (f32[2,32,512]{2,1,0:T(8,128)S(1)}, f32[2,32,512]{2,1,0:T(8,128)S(1)}, u32[]{:S(2)}, u32[]{:S(2)}) collective-permute-start(f32[2,32,512]{2,1,0:T(8,128)S(1)} %get-tuple-element.68), channel_id=1, source_target_pairs={{0,4},{4,0},{8,12},{12,8},{16,20},{20,16},{24,28},{28,24},{1,5},{5... | collective-permute-start | bytes 393224 | tf_op jit(solution)/shard_map/ppermute | solution.py:24
  44.1 1.5 %collective-permute-start.31 = (f32[2,32,512]{2,1,0:T(8,128)S(1)}, f32[2,32,512]{2,1,0:T(8,128)S(1)}, u32[]{:S(2)}, u32[]{:S(2)}) collective-permute-start(f32[2,32,512]{2,1,0:T(8,128)S(1)} %get-tuple-element.98), channel_id=1, source_target_pairs={{0,4},{4,0},{8,12},{12,8},{16,20},{20,16},{24,28},{28,24},{1,5},{5... | collective-permute-start | bytes 393224 | tf_op jit(solution)/shard_map/ppermute | solution.py:24
  46.7 1.8 %collective-permute-done.6.got = f32[2,32,512]{2,1,0:T(8,128)S(1)} collective-permute-done((f32[2,32,512]{2,1,0:T(8,128)S(1)}, f32[2,32,512]{2,1,0:T(8,128)S(1)}, u32[]{:S(2)}, u32[]{:S(2)}) %collective-permute-start.6) | collective-permute-done | bytes 131104 | tf_op jit(solution)/shard_map/ppermute | solution.py:24
  49.1 2.1 %collective-permute-done.26.got = f32[2,32,512]{2,1,0:T(8,128)S(1)} collective-permute-done((f32[2,32,512]{2,1,0:T(8,128)S(1)}, f32[2,32,512]{2,1,0:T(8,128)S(1)}, u32[]{:S(2)}, u32[]{:S(2)}) %collective-permute-start.26) | collective-permute-done | bytes 131104 | tf_op jit(solution)/shard_map/ppermute | solution.py:24
  51.9 2.1 %collective-permute-done.31.got = f32[2,32,512]{2,1,0:T(8,128)S(1)} collective-permute-done((f32[2,32,512]{2,1,0:T(8,128)S(1)}, f32[2,32,512]{2,1,0:T(8,128)S(1)}, u32[]{:S(2)}, u32[]{:S(2)}) %collective-permute-start.31) | collective-permute-done | bytes 131104 | tf_op jit(solution)/shard_map/ppermute | solution.py:24
  54.7 1.7 %collective-permute-done.36.got = f32[2,32,512]{2,1,0:T(8,128)S(1)} collective-permute-done((f32[2,32,512]{2,1,0:T(8,128)S(1)}, f32[2,32,512]{2,1,0:T(8,128)S(1)}, u32[]{:S(2)}, u32[]{:S(2)}) %collective-permute-start.36) | collective-permute-done | bytes 131104 | tf_op jit(solution)/shard_map/ppermute | solution.py:24
  62.5 2.2 %collective-permute-done.22.refs_0_ = f32[2,32,512]{2,1,0:T(8,128)S(1)} collective-permute-done((f32[2,32,512]{2,1,0:T(8,128)S(1)}, f32[2,32,512]{2,1,0:T(8,128)S(1)}, u32[]{:S(2)}, u32[]{:S(2)}) %collective-permute-start.22) | collective-permute-done | bytes 131104 | tf_op jit(solution)/shard_map/ppermute | solution.py:325
  75.0 1.6 %collective-permute-start.23 = (f32[2,32,512]{2,1,0:T(8,128)S(1)}, f32[2,32,512]{2,1,0:T(8,128)S(1)}, u32[]{:S(2)}, u32[]{:S(2)}) collective-permute-start(f32[2,32,512]{2,1,0:T(8,128)S(1)} %get-tuple-element.81), channel_id=1, source_target_pairs={{0,4},{4,0},{8,12},{12,8},{16,20},{20,16},{24,28},{28,24},{1,5},{5... | collective-permute-start | bytes 393224 | tf_op jit(solution)/shard_map/ppermute | solution.py:24
  78.0 1.6 %collective-permute-start.35 = (f32[2,32,512]{2,1,0:T(8,128)S(1)}, f32[2,32,512]{2,1,0:T(8,128)S(1)}, u32[]{:S(2)}, u32[]{:S(2)}) collective-permute-start(f32[2,32,512]{2,1,0:T(8,128)S(1)} %get-tuple-element.108), channel_id=1, source_target_pairs={{0,4},{4,0},{8,12},{12,8},{16,20},{20,16},{24,28},{28,24},{1,5},{5... | collective-permute-start | bytes 393224 | tf_op jit(solution)/shard_map/ppermute | solution.py:24
  81.3 2.8 %collective-permute-done.30.refs_2_ = f32[2,32,512]{2,1,0:T(8,128)S(1)} collective-permute-done((f32[2,32,512]{2,1,0:T(8,128)S(1)}, f32[2,32,512]{2,1,0:T(8,128)S(1)}, u32[]{:S(2)}, u32[]{:S(2)}) %collective-permute-start.30) | collective-permute-done | bytes 131104 | tf_op jit(solution)/shard_map/ppermute | solution.py:24
  84.1 2.8 %collective-permute-done.35.refs_3_ = f32[2,32,512]{2,1,0:T(8,128)S(1)} collective-permute-done((f32[2,32,512]{2,1,0:T(8,128)S(1)}, f32[2,32,512]{2,1,0:T(8,128)S(1)}, u32[]{:S(2)}, u32[]{:S(2)}) %collective-permute-start.35) | collective-permute-done | bytes 131104 | tf_op jit(solution)/shard_map/ppermute | solution.py:24
  87.0 1.5 %collective-permute-done.40.refs_4_ = f32[2,32,512]{2,1,0:T(8,128)S(1)} collective-permute-done((f32[2,32,512]{2,1,0:T(8,128)S(1)}, f32[2,32,512]{2,1,0:T(8,128)S(1)}, u32[]{:S(2)}, u32[]{:S(2)}) %collective-permute-start.40) | collective-permute-done | bytes 131104 | tf_op jit(solution)/shard_map/ppermute | solution.py:24
  (95 shorter events, 31.1 us)
Async XLA Ops:
  1.1 9.2 %collective-permute-start.1 = (f32[2,256,128]{2,1,0:T(8,128)S(1)}, f32[2,256,128]{2,1,0:T(8,128)S(1)}, u32[]{:S(2)}, u32[]{:S(2)}) collective-permute-start(f32[2,256,128]{2,1,0:T(8,128)S(1)} %slice.8.refs_0_), channel_id=1, source_target_pairs={{0,2},{1,3},{2,0},{3,1},{4,6},{5,7},{6,4},{7,5},{8,10},{9,11},{10,... | collective-permute-start | bytes 786440 | tf_op jit(solution)/shard_map/ppermute | solution.py:24
  2.7 12.1 %collective-permute-start.4 = (f32[2,256,128]{2,1,0:T(8,128)S(1)}, f32[2,256,128]{2,1,0:T(8,128)S(1)}, u32[]{:S(2)}, u32[]{:S(2)}) collective-permute-start(f32[2,256,128]{2,1,0:T(8,128)S(1)} %slice.9.refs_4_.refs_0_), channel_id=1, source_target_pairs={{0,2},{1,3},{2,0},{3,1},{4,6},{5,7},{6,4},{7,5},{8,10},{9,11},{10,... | collective-permute-start | bytes 786440 | tf_op jit(solution)/shard_map/ppermute | solution.py:24
  3.2 12.4 %collective-permute-start = (f32[2,256,128]{2,1,0:T(8,128)S(1)}, f32[2,256,128]{2,1,0:T(8,128)S(1)}, u32[]{:S(2)}, u32[]{:S(2)}) collective-permute-start(f32[2,256,128]{2,1,0:T(8,128)S(1)} %slice.8.refs_0_), channel_id=1, source_target_pairs={{0,1},{1,0},{2,3},{3,2},{4,5},{5,4},{6,7},{7,6},{8,9},{9,8},{10,11... | collective-permute-start | bytes 786440 | tf_op jit(solution)/shard_map/ppermute | solution.py:24
  10.3 9.8 %collective-permute-start.3 = (f32[2,256,128]{2,1,0:T(8,128)S(1)}, f32[2,256,128]{2,1,0:T(8,128)S(1)}, u32[]{:S(2)}, u32[]{:S(2)}) collective-permute-start(f32[2,256,128]{2,1,0:T(8,128)S(1)} %slice.9.refs_4_.refs_0_), channel_id=1, source_target_pairs={{0,1},{1,0},{2,3},{3,2},{4,5},{5,4},{6,7},{7,6},{8,9},{9,8},{10,11... | collective-permute-start | bytes 786440 | tf_op jit(solution)/shard_map/ppermute | solution.py:24
  17.1 9.0 %collective-permute-start.8 = (f32[2,128,256]{2,1,0:T(8,128)S(1)}, f32[2,128,256]{2,1,0:T(8,128)S(1)}, u32[]{:S(2)}, u32[]{:S(2)}) collective-permute-start(f32[2,128,256]{2,1,0:T(8,128)S(1)} %shard_map.50.refs_0_), channel_id=1, source_target_pairs={{0,2},{1,3},{2,0},{3,1},{4,6},{5,7},{6,4},{7,5},{8,10},{9,11},{10,... | collective-permute-start | bytes 786440 | tf_op jit(solution)/shard_map/ppermute | solution.py:24
  18.6 9.2 %collective-permute-start.10 = (f32[2,128,256]{2,1,0:T(8,128)S(1)}, f32[2,128,256]{2,1,0:T(8,128)S(1)}, u32[]{:S(2)}, u32[]{:S(2)}) collective-permute-start(f32[2,128,256]{2,1,0:T(8,128)S(1)} %shard_map.50.refs_0_), channel_id=1, source_target_pairs={{0,4},{4,0},{8,12},{12,8},{16,20},{20,16},{24,28},{28,24},{1,5},{5... | collective-permute-start | bytes 786440 | tf_op jit(solution)/shard_map/ppermute | solution.py:24
  21.0 12.4 %collective-permute-start.17 = (f32[2,128,256]{2,1,0:T(8,128)S(1)}, f32[2,128,256]{2,1,0:T(8,128)S(1)}, u32[]{:S(2)}, u32[]{:S(2)}) collective-permute-start(f32[2,128,256]{2,1,0:T(8,128)S(1)} %shard_map.53.refs_0_), channel_id=1, source_target_pairs={{0,4},{4,0},{8,12},{12,8},{16,20},{20,16},{24,28},{28,24},{1,5},{5... | collective-permute-start | bytes 786440 | tf_op jit(solution)/shard_map/ppermute | solution.py:24
  21.6 12.4 %collective-permute-start.14 = (f32[2,128,256]{2,1,0:T(8,128)S(1)}, f32[2,128,256]{2,1,0:T(8,128)S(1)}, u32[]{:S(2)}, u32[]{:S(2)}) collective-permute-start(f32[2,128,256]{2,1,0:T(8,128)S(1)} %shard_map.53.refs_0_), channel_id=1, source_target_pairs={{0,1},{1,0},{2,3},{3,2},{4,5},{5,4},{6,7},{7,6},{8,9},{9,8},{10,11... | collective-permute-start | bytes 786440 | tf_op jit(solution)/shard_map/ppermute | solution.py:24
  21.6 12.4 %collective-permute-start.15 = (f32[2,128,256]{2,1,0:T(8,128)S(1)}, f32[2,128,256]{2,1,0:T(8,128)S(1)}, u32[]{:S(2)}, u32[]{:S(2)}) collective-permute-start(f32[2,128,256]{2,1,0:T(8,128)S(1)} %shard_map.53.refs_0_), channel_id=1, source_target_pairs={{0,2},{1,3},{2,0},{3,1},{4,6},{5,7},{6,4},{7,5},{8,10},{9,11},{10,... | collective-permute-start | bytes 786440 | tf_op jit(solution)/shard_map/ppermute | solution.py:24
  26.1 8.3 %collective-permute-start.9 = (f32[2,128,256]{2,1,0:T(8,128)S(1)}, f32[2,128,256]{2,1,0:T(8,128)S(1)}, u32[]{:S(2)}, u32[]{:S(2)}) collective-permute-start(f32[2,128,256]{2,1,0:T(8,128)S(1)} %collective-permute-done.8.refs_2_), channel_id=1, source_target_pairs={{0,1},{1,0},{2,3},{3,2},{4,5},{5,4},{6,7},{7,6},{8,9},{9,8},{10,11... | collective-permute-start | bytes 786440 | tf_op jit(solution)/shard_map/ppermute | solution.py:24
  27.8 10.1 %collective-permute-start.12 = (f32[2,128,256]{2,1,0:T(8,128)S(1)}, f32[2,128,256]{2,1,0:T(8,128)S(1)}, u32[]{:S(2)}, u32[]{:S(2)}) collective-permute-start(f32[2,128,256]{2,1,0:T(8,128)S(1)} %collective-permute-done.8.refs_2_), channel_id=1, source_target_pairs={{0,4},{4,0},{8,12},{12,8},{16,20},{20,16},{24,28},{28,24},{1,5},{5... | collective-permute-start | bytes 786440 | tf_op jit(solution)/shard_map/ppermute | solution.py:24
  34.0 8.1 %collective-permute-start.11 = (f32[2,128,256]{2,1,0:T(8,128)S(1)}, f32[2,128,256]{2,1,0:T(8,128)S(1)}, u32[]{:S(2)}, u32[]{:S(2)}) collective-permute-start(f32[2,128,256]{2,1,0:T(8,128)S(1)} %collective-permute-done.10.refs_4_), channel_id=1, source_target_pairs={{0,1},{1,0},{2,3},{3,2},{4,5},{5,4},{6,7},{7,6},{8,9},{9,8},{10,11... | collective-permute-start | bytes 786440 | tf_op jit(solution)/shard_map/ppermute | solution.py:24
  34.0 9.6 %collective-permute-start.16 = (f32[2,128,256]{2,1,0:T(8,128)S(1)}, f32[2,128,256]{2,1,0:T(8,128)S(1)}, u32[]{:S(2)}, u32[]{:S(2)}) collective-permute-start(f32[2,128,256]{2,1,0:T(8,128)S(1)} %collective-permute-done.15.refs_2_), channel_id=1, source_target_pairs={{0,1},{1,0},{2,3},{3,2},{4,5},{5,4},{6,7},{7,6},{8,9},{9,8},{10,11... | collective-permute-start | bytes 786440 | tf_op jit(solution)/shard_map/ppermute | solution.py:24
  34.5 9.6 %collective-permute-start.18 = (f32[2,128,256]{2,1,0:T(8,128)S(1)}, f32[2,128,256]{2,1,0:T(8,128)S(1)}, u32[]{:S(2)}, u32[]{:S(2)}) collective-permute-start(f32[2,128,256]{2,1,0:T(8,128)S(1)} %collective-permute-done.17.refs_4_), channel_id=1, source_target_pairs={{0,1},{1,0},{2,3},{3,2},{4,5},{5,4},{6,7},{7,6},{8,9},{9,8},{10,11... | collective-permute-start | bytes 786440 | tf_op jit(solution)/shard_map/ppermute | solution.py:24
  44.1 10.0 %collective-permute-start.31 = (f32[2,32,512]{2,1,0:T(8,128)S(1)}, f32[2,32,512]{2,1,0:T(8,128)S(1)}, u32[]{:S(2)}, u32[]{:S(2)}) collective-permute-start(f32[2,32,512]{2,1,0:T(8,128)S(1)} %get-tuple-element.98), channel_id=1, source_target_pairs={{0,4},{4,0},{8,12},{12,8},{16,20},{20,16},{24,28},{28,24},{1,5},{5... | collective-permute-start | bytes 393224 | tf_op jit(solution)/shard_map/ppermute | solution.py:24
  45.6 10.8 %collective-permute-start.36 = (f32[2,32,512]{2,1,0:T(8,128)S(1)}, f32[2,32,512]{2,1,0:T(8,128)S(1)}, u32[]{:S(2)}, u32[]{:S(2)}) collective-permute-start(f32[2,32,512]{2,1,0:T(8,128)S(1)} %get-tuple-element.110), channel_id=1, source_target_pairs={{0,4},{4,0},{8,12},{12,8},{16,20},{20,16},{24,28},{28,24},{1,5},{5... | collective-permute-start | bytes 393224 | tf_op jit(solution)/shard_map/ppermute | solution.py:24
  48.5 8.6 %collective-permute-start.21 = (f32[2,32,512]{2,1,0:T(8,128)S(1)}, f32[2,32,512]{2,1,0:T(8,128)S(1)}, u32[]{:S(2)}, u32[]{:S(2)}) collective-permute-start(f32[2,32,512]{2,1,0:T(8,128)S(1)} %get-tuple-element.75), channel_id=1, source_target_pairs={{0,8},{4,12},{1,9},{5,13},{2,10},{6,14},{3,11},{7,15}} | collective-permute-start | bytes 393224 | tf_op jit(solution)/shard_map/ppermute | solution.py:325
  58.5 9.1 %collective-permute-start.28 = (f32[2,32,512]{2,1,0:T(8,128)S(1)}, f32[2,32,512]{2,1,0:T(8,128)S(1)}, u32[]{:S(2)}, u32[]{:S(2)}) collective-permute-start(f32[2,32,512]{2,1,0:T(8,128)S(1)} %get-tuple-element.90), channel_id=1, source_target_pairs={{8,16},{12,20},{9,17},{13,21},{10,18},{14,22},{11,19},{15,23}} | collective-permute-start | bytes 393224 | tf_op jit(solution)/shard_map/ppermute | solution.py:325
  59.9 10.6 %collective-permute-start.33 = (f32[2,32,512]{2,1,0:T(8,128)S(1)}, f32[2,32,512]{2,1,0:T(8,128)S(1)}, u32[]{:S(2)}, u32[]{:S(2)}) collective-permute-start(f32[2,32,512]{2,1,0:T(8,128)S(1)} %get-tuple-element.102), channel_id=1, source_target_pairs={{8,16},{12,20},{9,17},{13,21},{10,18},{14,22},{11,19},{15,23}} | collective-permute-start | bytes 393224 | tf_op jit(solution)/shard_map/ppermute | solution.py:325
  61.2 11.4 %collective-permute-start.38 = (f32[2,32,512]{2,1,0:T(8,128)S(1)}, f32[2,32,512]{2,1,0:T(8,128)S(1)}, u32[]{:S(2)}, u32[]{:S(2)}) collective-permute-start(f32[2,32,512]{2,1,0:T(8,128)S(1)} %get-tuple-element.114), channel_id=1, source_target_pairs={{8,16},{12,20},{9,17},{13,21},{10,18},{14,22},{11,19},{15,23}} | collective-permute-start | bytes 393224 | tf_op jit(solution)/shard_map/ppermute | solution.py:325
  65.6 11.0 %collective-permute-start.24 = (f32[2,32,512]{2,1,0:T(8,128)S(1)}, f32[2,32,512]{2,1,0:T(8,128)S(1)}, u32[]{:S(2)}, u32[]{:S(2)}) collective-permute-start(f32[2,32,512]{2,1,0:T(8,128)S(1)} %get-tuple-element.82), channel_id=1, source_target_pairs={{16,24},{20,28},{17,25},{21,29},{18,26},{22,30},{19,27},{23,31}} | collective-permute-start | bytes 393224 | tf_op jit(solution)/shard_map/ppermute | solution.py:325
  68.5 8.8 %collective-permute-start.29 = (f32[2,32,512]{2,1,0:T(8,128)S(1)}, f32[2,32,512]{2,1,0:T(8,128)S(1)}, u32[]{:S(2)}, u32[]{:S(2)}) collective-permute-start(f32[2,32,512]{2,1,0:T(8,128)S(1)} %get-tuple-element.93), channel_id=1, source_target_pairs={{16,24},{20,28},{17,25},{21,29},{18,26},{22,30},{19,27},{23,31}} | collective-permute-start | bytes 393224 | tf_op jit(solution)/shard_map/ppermute | solution.py:325
  78.0 9.0 %collective-permute-start.35 = (f32[2,32,512]{2,1,0:T(8,128)S(1)}, f32[2,32,512]{2,1,0:T(8,128)S(1)}, u32[]{:S(2)}, u32[]{:S(2)}) collective-permute-start(f32[2,32,512]{2,1,0:T(8,128)S(1)} %get-tuple-element.108), channel_id=1, source_target_pairs={{0,4},{4,0},{8,12},{12,8},{16,20},{20,16},{24,28},{28,24},{1,5},{5... | collective-permute-start | bytes 393224 | tf_op jit(solution)/shard_map/ppermute | solution.py:24
  79.5 8.9 %collective-permute-start.40 = (f32[2,32,512]{2,1,0:T(8,128)S(1)}, f32[2,32,512]{2,1,0:T(8,128)S(1)}, u32[]{:S(2)}, u32[]{:S(2)}) collective-permute-start(f32[2,32,512]{2,1,0:T(8,128)S(1)} %get-tuple-element.120), channel_id=1, source_target_pairs={{0,4},{4,0},{8,12},{12,8},{16,20},{20,16},{24,28},{28,24},{1,5},{5... | collective-permute-start | bytes 393224 | tf_op jit(solution)/shard_map/ppermute | solution.py:24
  (20 other events, 144.2 us)

commit v5 on v4

--- a/solution.py
+++ b/solution.py
@@ -22,6 +22,16 @@
 def exchange(shard, axis, bit):
     count = lax.axis_size(axis)
     return lax.ppermute(shard, axis, [(i, i ^ bit) for i in range(count)])
+
+
+def between(shard, moves):
+    chain, col = lax.axis_size("chain"), lax.axis_size("col")
+    pairs = []
+    for i in range(chain):
+        for j in range(col):
+            to = moves[i] * col + j if i in moves else i * col + (j ^ 1)
+            pairs.append((i * col + j, to))
+    return lax.ppermute(shard, ("chain", "col"), pairs)
 
 
 def gathered(own):
@@ -322,9 +332,13 @@
                 flops * half,
             )
             if not final:
-                held[c] = [lax.ppermute(passed[0], "chain", pairs), mine, theirs]
+                if hop:
+                    come = lax.ppermute(passed[0], "chain", pairs)
+                else:
+                    come = between(passed[0], {i: i ^ 2 for i in range(4)})
+                held[c] = [come, mine, theirs]
                 if c == 0 and hop == hops - 1:
-                    early = exchange(held[c].pop(), "chain", 1)
+                    early = between(held[c].pop(), {i: i ^ 1 for i in range(2 * hops)})
                 continue
             keep.append(mine)
             if c == 0 and hops:

time: 89.9 us -> 89.8 us (level)
  waiting for transfers between devices: 44.9 us -> 47.6 us
  starting transfers between devices: 32 us -> 29.4 us
    ppermute x28 -> x27, waiting for transfers between devices: 41.3 us -> 43.3 us  [exchange(): return lax.ppermute(shard, axis, [(i, i ^ bit) for i in range(count)])]
    ppermute x28 -> x27, starting transfers between devices: 18.4 us -> 16.8 us  [exchange(): return lax.ppermute(shard, axis, [(i, i ^ bit) for i in range(count)])]
    ppermute x12 -> x13, starting transfers between devices: 13 us -> 11.9 us  [the longest x8 10.4 us: body(): come = lax.ppermute(passed[0], 'chain', pairs)]
    ppermute x12 -> x13, waiting for transfers between devices: 3.56 us -> 4.3 us  [the longest x8 4.28 us: body(): come = lax.ppermute(passed[0], 'chain', pairs)]
where the time goes in v5:
time: 89.8 us; the launch traced here: 89.5 us
  waiting for transfers between devices  47.6 us (53%)
  starting transfers between devices  29.4 us (33%)
  Pallas kernels  10.2 us (11%)
  between operations  1.2 us (1%)
  local copies, waits for them, and re-layouts  1.09 us (1%)
    ppermute x27, waiting for transfers between devices, exchange(): return lax.ppermute(shard, axis, [(i, i ^ bit) for i in range(count)])  43.3 us
    ppermute x27, starting transfers between devices, exchange(): return lax.ppermute(shard, axis, [(i, i ^ bit) for i in range(count)])  16.8 us
    ppermute x8, starting transfers between devices, body(): come = lax.ppermute(passed[0], 'chain', pairs)  10.4 us
    pallas_call x25, Pallas kernels, kernel_call(): pl.pallas_call(kernel, out_shape=[jax.ShapeDtypeStruct(s, d) for s, d in...  8.32 us
    ppermute x8, waiting for transfers between devices, body(): come = lax.ppermute(passed[0], 'chain', pairs)  4.28 us
    pallas_call x2, Pallas kernels, body(): pl.pallas_call(functools.partial(half_kernel, side, CHUNKS, hops), out_sh...  1.89 us
  transfers between devices with their start and end apart: 41, of which 18 were waited for; matrix products, arithmetic and copies ran while one was open for 0% of the time, Pallas kernels for 10%

profile of v5, /device:TPU:16, one launch (start us, length us, event | category | flops | bytes accessed | tf_op | source)
XLA Modules:
  0.0 89.5 jit_solution(17618501060367355223)
XLA Ops:
  1.1 1.6 %collective-permute-start.1 = (f32[2,256,128]{2,1,0:T(8,128)S(1)}, f32[2,256,128]{2,1,0:T(8,128)S(1)}, u32[]{:S(2)}, u32[]{:S(2)}) collective-permute-start(f32[2,256,128]{2,1,0:T(8,128)S(1)} %slice.8.refs_0_), channel_id=1, source_target_pairs={{0,2},{1,3},{2,0},{3,1},{4,6},{5,7},{6,4},{7,5},{8,10},{9,11},{10,... | collective-permute-start | bytes 786440 | tf_op jit(solution)/shard_map/ppermute | solution.py:24
  3.2 7.1 %collective-permute-done.1.refs_2_.refs_0_ = f32[2,256,128]{2,1,0:T(8,128)S(1)} collective-permute-done((f32[2,256,128]{2,1,0:T(8,128)S(1)}, f32[2,256,128]{2,1,0:T(8,128)S(1)}, u32[]{:S(2)}, u32[]{:S(2)}) %collective-permute-start.1) | collective-permute-done | bytes 262176 | tf_op jit(solution)/shard_map/ppermute | solution.py:24
  10.8 4.0 %collective-permute-done.4.refs_6_.refs_0_ = f32[2,256,128]{2,1,0:T(8,128)S(1)} collective-permute-done((f32[2,256,128]{2,1,0:T(8,128)S(1)}, f32[2,256,128]{2,1,0:T(8,128)S(1)}, u32[]{:S(2)}, u32[]{:S(2)}) %collective-permute-start.4) | collective-permute-done | bytes 262176 | tf_op jit(solution)/shard_map/ppermute | solution.py:24
  17.1 1.5 %collective-permute-start.8 = (f32[2,128,256]{2,1,0:T(8,128)S(1)}, f32[2,128,256]{2,1,0:T(8,128)S(1)}, u32[]{:S(2)}, u32[]{:S(2)}) collective-permute-start(f32[2,128,256]{2,1,0:T(8,128)S(1)} %shard_map.50.refs_0_), channel_id=1, source_target_pairs={{0,2},{1,3},{2,0},{3,1},{4,6},{5,7},{6,4},{7,5},{8,10},{9,11},{10,... | collective-permute-start | bytes 786440 | tf_op jit(solution)/shard_map/ppermute | solution.py:24
  18.6 1.5 %collective-permute-start.10 = (f32[2,128,256]{2,1,0:T(8,128)S(1)}, f32[2,128,256]{2,1,0:T(8,128)S(1)}, u32[]{:S(2)}, u32[]{:S(2)}) collective-permute-start(f32[2,128,256]{2,1,0:T(8,128)S(1)} %shard_map.50.refs_0_), channel_id=1, source_target_pairs={{0,4},{4,0},{8,12},{12,8},{16,20},{20,16},{24,28},{28,24},{1,5},{5... | collective-permute-start | bytes 786440 | tf_op jit(solution)/shard_map/ppermute | solution.py:24
  22.1 4.0 %collective-permute-done.8.refs_2_ = f32[2,128,256]{2,1,0:T(8,128)S(1)} collective-permute-done((f32[2,128,256]{2,1,0:T(8,128)S(1)}, f32[2,128,256]{2,1,0:T(8,128)S(1)}, u32[]{:S(2)}, u32[]{:S(2)}) %collective-permute-start.8) | collective-permute-done | bytes 262176 | tf_op jit(solution)/shard_map/ppermute | solution.py:24
  26.1 1.7 %collective-permute-done.10.refs_4_ = f32[2,128,256]{2,1,0:T(8,128)S(1)} collective-permute-done((f32[2,128,256]{2,1,0:T(8,128)S(1)}, f32[2,128,256]{2,1,0:T(8,128)S(1)}, u32[]{:S(2)}, u32[]{:S(2)}) %collective-permute-start.10) | collective-permute-done | bytes 262176 | tf_op jit(solution)/shard_map/ppermute | solution.py:24
  27.8 1.5 %collective-permute-start.12 = (f32[2,128,256]{2,1,0:T(8,128)S(1)}, f32[2,128,256]{2,1,0:T(8,128)S(1)}, u32[]{:S(2)}, u32[]{:S(2)}) collective-permute-start(f32[2,128,256]{2,1,0:T(8,128)S(1)} %collective-permute-done.8.refs_2_), channel_id=1, source_target_pairs={{0,4},{4,0},{8,12},{12,8},{16,20},{20,16},{24,28},{28,24},{1,5},{5... | collective-permute-start | bytes 786440 | tf_op jit(solution)/shard_map/ppermute | solution.py:24
  29.3 4.1 %collective-permute-done.17.refs_4_ = f32[2,128,256]{2,1,0:T(8,128)S(1)} collective-permute-done((f32[2,128,256]{2,1,0:T(8,128)S(1)}, f32[2,128,256]{2,1,0:T(8,128)S(1)}, u32[]{:S(2)}, u32[]{:S(2)}) %collective-permute-start.17) | collective-permute-done | bytes 262176 | tf_op jit(solution)/shard_map/ppermute | solution.py:24
  34.5 3.3 %collective-permute-done.12.refs_6_ = f32[2,128,256]{2,1,0:T(8,128)S(1)} collective-permute-done((f32[2,128,256]{2,1,0:T(8,128)S(1)}, f32[2,128,256]{2,1,0:T(8,128)S(1)}, u32[]{:S(2)}, u32[]{:S(2)}) %collective-permute-start.12) | collective-permute-done | bytes 262176 | tf_op jit(solution)/shard_map/ppermute | solution.py:24
  37.9 1.9 %collective-permute-done.19.refs_6_ = f32[2,128,256]{2,1,0:T(8,128)S(1)} collective-permute-done((f32[2,128,256]{2,1,0:T(8,128)S(1)}, f32[2,128,256]{2,1,0:T(8,128)S(1)}, u32[]{:S(2)}, u32[]{:S(2)}) %collective-permute-start.19) | collective-permute-done | bytes 262176 | tf_op jit(solution)/shard_map/ppermute | solution.py:24
  40.2 1.8 %shard_map.47 = (f32[2,32,512]{2,1,0:T(8,128)S(1)}, f32[2,32,512]{2,1,0:T(8,128)S(1)}, f32[2,32,512]{2,1,0:T(8,128)S(1)}, f32[2,32,512]{2,1,0:T(8,128)S(1)}, f32...) custom-call(f32[8,512]{1,0:T(8,128)S(1)} %iota.7.active, ...), custom_call_target="tpu_custom_call" | custom-call | flops 536870912 | bytes 4096 | tf_op jit(solution)/shard_map/pallas_call | solution.py:47
  42.0 1.6 %collective-permute-start.6 = (f32[2,32,512]{2,1,0:T(8,128)S(1)}, f32[2,32,512]{2,1,0:T(8,128)S(1)}, u32[]{:S(2)}, u32[]{:S(2)}) collective-permute-start(f32[2,32,512]{2,1,0:T(8,128)S(1)} %get-tuple-element.68), channel_id=1, source_target_pairs={{0,4},{4,0},{8,12},{12,8},{16,20},{20,16},{24,28},{28,24},{1,5},{5... | collective-permute-start | bytes 393224 | tf_op jit(solution)/shard_map/ppermute | solution.py:24
  44.1 1.5 %collective-permute-start.31 = (f32[2,32,512]{2,1,0:T(8,128)S(1)}, f32[2,32,512]{2,1,0:T(8,128)S(1)}, u32[]{:S(2)}, u32[]{:S(2)}) collective-permute-start(f32[2,32,512]{2,1,0:T(8,128)S(1)} %get-tuple-element.98), channel_id=1, source_target_pairs={{0,4},{4,0},{8,12},{12,8},{16,20},{20,16},{24,28},{28,24},{1,5},{5... | collective-permute-start | bytes 393224 | tf_op jit(solution)/shard_map/ppermute | solution.py:24
  46.7 1.8 %collective-permute-done.6.got = f32[2,32,512]{2,1,0:T(8,128)S(1)} collective-permute-done((f32[2,32,512]{2,1,0:T(8,128)S(1)}, f32[2,32,512]{2,1,0:T(8,128)S(1)}, u32[]{:S(2)}, u32[]{:S(2)}) %collective-permute-start.6) | collective-permute-done | bytes 131104 | tf_op jit(solution)/shard_map/ppermute | solution.py:24
  48.5 2.8 %collective-permute-done.26.got = f32[2,32,512]{2,1,0:T(8,128)S(1)} collective-permute-done((f32[2,32,512]{2,1,0:T(8,128)S(1)}, f32[2,32,512]{2,1,0:T(8,128)S(1)}, u32[]{:S(2)}, u32[]{:S(2)}) %collective-permute-start.26) | collective-permute-done | bytes 131104 | tf_op jit(solution)/shard_map/ppermute | solution.py:24
  51.3 2.8 %collective-permute-done.31.got = f32[2,32,512]{2,1,0:T(8,128)S(1)} collective-permute-done((f32[2,32,512]{2,1,0:T(8,128)S(1)}, f32[2,32,512]{2,1,0:T(8,128)S(1)}, u32[]{:S(2)}, u32[]{:S(2)}) %collective-permute-start.31) | collective-permute-done | bytes 131104 | tf_op jit(solution)/shard_map/ppermute | solution.py:24
  54.1 2.3 %collective-permute-done.36.got = f32[2,32,512]{2,1,0:T(8,128)S(1)} collective-permute-done((f32[2,32,512]{2,1,0:T(8,128)S(1)}, f32[2,32,512]{2,1,0:T(8,128)S(1)}, u32[]{:S(2)}, u32[]{:S(2)}) %collective-permute-start.36) | collective-permute-done | bytes 131104 | tf_op jit(solution)/shard_map/ppermute | solution.py:24
  61.8 2.9 %collective-permute-done.22.refs_0_ = f32[2,32,512]{2,1,0:T(8,128)S(1)} collective-permute-done((f32[2,32,512]{2,1,0:T(8,128)S(1)}, f32[2,32,512]{2,1,0:T(8,128)S(1)}, u32[]{:S(2)}, u32[]{:S(2)}) %collective-permute-start.22) | collective-permute-done | bytes 131104 | tf_op jit(solution)/shard_map/ppermute | solution.py:336
  74.9 1.6 %collective-permute-start.23 = (f32[2,32,512]{2,1,0:T(8,128)S(1)}, f32[2,32,512]{2,1,0:T(8,128)S(1)}, u32[]{:S(2)}, u32[]{:S(2)}) collective-permute-start(f32[2,32,512]{2,1,0:T(8,128)S(1)} %get-tuple-element.81), channel_id=1, source_target_pairs={{0,4},{1,5},{2,6},{3,7},{4,0},{5,1},{6,2},{7,3},{8,12},{9,13},{10,... | collective-permute-start | bytes 393224 | tf_op jit(solution)/shard_map/ppermute | solution.py:34
  77.9 1.6 %collective-permute-start.35 = (f32[2,32,512]{2,1,0:T(8,128)S(1)}, f32[2,32,512]{2,1,0:T(8,128)S(1)}, u32[]{:S(2)}, u32[]{:S(2)}) collective-permute-start(f32[2,32,512]{2,1,0:T(8,128)S(1)} %get-tuple-element.108), channel_id=1, source_target_pairs={{0,4},{4,0},{8,12},{12,8},{16,20},{20,16},{24,28},{28,24},{1,5},{5... | collective-permute-start | bytes 393224 | tf_op jit(solution)/shard_map/ppermute | solution.py:24
  81.0 2.7 %collective-permute-done.30.refs_2_ = f32[2,32,512]{2,1,0:T(8,128)S(1)} collective-permute-done((f32[2,32,512]{2,1,0:T(8,128)S(1)}, f32[2,32,512]{2,1,0:T(8,128)S(1)}, u32[]{:S(2)}, u32[]{:S(2)}) %collective-permute-start.30) | collective-permute-done | bytes 131104 | tf_op jit(solution)/shard_map/ppermute | solution.py:24
  83.7 2.8 %collective-permute-done.35.refs_3_ = f32[2,32,512]{2,1,0:T(8,128)S(1)} collective-permute-done((f32[2,32,512]{2,1,0:T(8,128)S(1)}, f32[2,32,512]{2,1,0:T(8,128)S(1)}, u32[]{:S(2)}, u32[]{:S(2)}) %collective-permute-start.35) | collective-permute-done | bytes 131104 | tf_op jit(solution)/shard_map/ppermute | solution.py:24
  86.5 1.9 %collective-permute-done.40.refs_4_ = f32[2,32,512]{2,1,0:T(8,128)S(1)} collective-permute-done((f32[2,32,512]{2,1,0:T(8,128)S(1)}, f32[2,32,512]{2,1,0:T(8,128)S(1)}, u32[]{:S(2)}, u32[]{:S(2)}) %collective-permute-start.40) | collective-permute-done | bytes 131104 | tf_op jit(solution)/shard_map/ppermute | solution.py:24
  (95 shorter events, 28.1 us)
Async XLA Ops:
  1.1 9.2 %collective-permute-start.1 = (f32[2,256,128]{2,1,0:T(8,128)S(1)}, f32[2,256,128]{2,1,0:T(8,128)S(1)}, u32[]{:S(2)}, u32[]{:S(2)}) collective-permute-start(f32[2,256,128]{2,1,0:T(8,128)S(1)} %slice.8.refs_0_), channel_id=1, source_target_pairs={{0,2},{1,3},{2,0},{3,1},{4,6},{5,7},{6,4},{7,5},{8,10},{9,11},{10,... | collective-permute-start | bytes 786440 | tf_op jit(solution)/shard_map/ppermute | solution.py:24
  2.7 12.1 %collective-permute-start.4 = (f32[2,256,128]{2,1,0:T(8,128)S(1)}, f32[2,256,128]{2,1,0:T(8,128)S(1)}, u32[]{:S(2)}, u32[]{:S(2)}) collective-permute-start(f32[2,256,128]{2,1,0:T(8,128)S(1)} %slice.9.refs_4_.refs_0_), channel_id=1, source_target_pairs={{0,2},{1,3},{2,0},{3,1},{4,6},{5,7},{6,4},{7,5},{8,10},{9,11},{10,... | collective-permute-start | bytes 786440 | tf_op jit(solution)/shard_map/ppermute | solution.py:24
  3.2 12.4 %collective-permute-start = (f32[2,256,128]{2,1,0:T(8,128)S(1)}, f32[2,256,128]{2,1,0:T(8,128)S(1)}, u32[]{:S(2)}, u32[]{:S(2)}) collective-permute-start(f32[2,256,128]{2,1,0:T(8,128)S(1)} %slice.8.refs_0_), channel_id=1, source_target_pairs={{0,1},{1,0},{2,3},{3,2},{4,5},{5,4},{6,7},{7,6},{8,9},{9,8},{10,11... | collective-permute-start | bytes 786440 | tf_op jit(solution)/shard_map/ppermute | solution.py:24
  10.3 9.8 %collective-permute-start.3 = (f32[2,256,128]{2,1,0:T(8,128)S(1)}, f32[2,256,128]{2,1,0:T(8,128)S(1)}, u32[]{:S(2)}, u32[]{:S(2)}) collective-permute-start(f32[2,256,128]{2,1,0:T(8,128)S(1)} %slice.9.refs_4_.refs_0_), channel_id=1, source_target_pairs={{0,1},{1,0},{2,3},{3,2},{4,5},{5,4},{6,7},{7,6},{8,9},{9,8},{10,11... | collective-permute-start | bytes 786440 | tf_op jit(solution)/shard_map/ppermute | solution.py:24
  17.1 9.0 %collective-permute-start.8 = (f32[2,128,256]{2,1,0:T(8,128)S(1)}, f32[2,128,256]{2,1,0:T(8,128)S(1)}, u32[]{:S(2)}, u32[]{:S(2)}) collective-permute-start(f32[2,128,256]{2,1,0:T(8,128)S(1)} %shard_map.50.refs_0_), channel_id=1, source_target_pairs={{0,2},{1,3},{2,0},{3,1},{4,6},{5,7},{6,4},{7,5},{8,10},{9,11},{10,... | collective-permute-start | bytes 786440 | tf_op jit(solution)/shard_map/ppermute | solution.py:24
  18.6 9.2 %collective-permute-start.10 = (f32[2,128,256]{2,1,0:T(8,128)S(1)}, f32[2,128,256]{2,1,0:T(8,128)S(1)}, u32[]{:S(2)}, u32[]{:S(2)}) collective-permute-start(f32[2,128,256]{2,1,0:T(8,128)S(1)} %shard_map.50.refs_0_), channel_id=1, source_target_pairs={{0,4},{4,0},{8,12},{12,8},{16,20},{20,16},{24,28},{28,24},{1,5},{5... | collective-permute-start | bytes 786440 | tf_op jit(solution)/shard_map/ppermute | solution.py:24
  21.0 12.4 %collective-permute-start.17 = (f32[2,128,256]{2,1,0:T(8,128)S(1)}, f32[2,128,256]{2,1,0:T(8,128)S(1)}, u32[]{:S(2)}, u32[]{:S(2)}) collective-permute-start(f32[2,128,256]{2,1,0:T(8,128)S(1)} %shard_map.53.refs_0_), channel_id=1, source_target_pairs={{0,4},{4,0},{8,12},{12,8},{16,20},{20,16},{24,28},{28,24},{1,5},{5... | collective-permute-start | bytes 786440 | tf_op jit(solution)/shard_map/ppermute | solution.py:24
  21.6 12.4 %collective-permute-start.14 = (f32[2,128,256]{2,1,0:T(8,128)S(1)}, f32[2,128,256]{2,1,0:T(8,128)S(1)}, u32[]{:S(2)}, u32[]{:S(2)}) collective-permute-start(f32[2,128,256]{2,1,0:T(8,128)S(1)} %shard_map.53.refs_0_), channel_id=1, source_target_pairs={{0,1},{1,0},{2,3},{3,2},{4,5},{5,4},{6,7},{7,6},{8,9},{9,8},{10,11... | collective-permute-start | bytes 786440 | tf_op jit(solution)/shard_map/ppermute | solution.py:24
  21.6 12.4 %collective-permute-start.15 = (f32[2,128,256]{2,1,0:T(8,128)S(1)}, f32[2,128,256]{2,1,0:T(8,128)S(1)}, u32[]{:S(2)}, u32[]{:S(2)}) collective-permute-start(f32[2,128,256]{2,1,0:T(8,128)S(1)} %shard_map.53.refs_0_), channel_id=1, source_target_pairs={{0,2},{1,3},{2,0},{3,1},{4,6},{5,7},{6,4},{7,5},{8,10},{9,11},{10,... | collective-permute-start | bytes 786440 | tf_op jit(solution)/shard_map/ppermute | solution.py:24
  26.1 8.3 %collective-permute-start.9 = (f32[2,128,256]{2,1,0:T(8,128)S(1)}, f32[2,128,256]{2,1,0:T(8,128)S(1)}, u32[]{:S(2)}, u32[]{:S(2)}) collective-permute-start(f32[2,128,256]{2,1,0:T(8,128)S(1)} %collective-permute-done.8.refs_2_), channel_id=1, source_target_pairs={{0,1},{1,0},{2,3},{3,2},{4,5},{5,4},{6,7},{7,6},{8,9},{9,8},{10,11... | collective-permute-start | bytes 786440 | tf_op jit(solution)/shard_map/ppermute | solution.py:24
  27.8 10.1 %collective-permute-start.12 = (f32[2,128,256]{2,1,0:T(8,128)S(1)}, f32[2,128,256]{2,1,0:T(8,128)S(1)}, u32[]{:S(2)}, u32[]{:S(2)}) collective-permute-start(f32[2,128,256]{2,1,0:T(8,128)S(1)} %collective-permute-done.8.refs_2_), channel_id=1, source_target_pairs={{0,4},{4,0},{8,12},{12,8},{16,20},{20,16},{24,28},{28,24},{1,5},{5... | collective-permute-start | bytes 786440 | tf_op jit(solution)/shard_map/ppermute | solution.py:24
  34.0 8.1 %collective-permute-start.11 = (f32[2,128,256]{2,1,0:T(8,128)S(1)}, f32[2,128,256]{2,1,0:T(8,128)S(1)}, u32[]{:S(2)}, u32[]{:S(2)}) collective-permute-start(f32[2,128,256]{2,1,0:T(8,128)S(1)} %collective-permute-done.10.refs_4_), channel_id=1, source_target_pairs={{0,1},{1,0},{2,3},{3,2},{4,5},{5,4},{6,7},{7,6},{8,9},{9,8},{10,11... | collective-permute-start | bytes 786440 | tf_op jit(solution)/shard_map/ppermute | solution.py:24
  34.0 9.6 %collective-permute-start.16 = (f32[2,128,256]{2,1,0:T(8,128)S(1)}, f32[2,128,256]{2,1,0:T(8,128)S(1)}, u32[]{:S(2)}, u32[]{:S(2)}) collective-permute-start(f32[2,128,256]{2,1,0:T(8,128)S(1)} %collective-permute-done.15.refs_2_), channel_id=1, source_target_pairs={{0,1},{1,0},{2,3},{3,2},{4,5},{5,4},{6,7},{7,6},{8,9},{9,8},{10,11... | collective-permute-start | bytes 786440 | tf_op jit(solution)/shard_map/ppermute | solution.py:24
  34.5 9.6 %collective-permute-start.18 = (f32[2,128,256]{2,1,0:T(8,128)S(1)}, f32[2,128,256]{2,1,0:T(8,128)S(1)}, u32[]{:S(2)}, u32[]{:S(2)}) collective-permute-start(f32[2,128,256]{2,1,0:T(8,128)S(1)} %collective-permute-done.17.refs_4_), channel_id=1, source_target_pairs={{0,1},{1,0},{2,3},{3,2},{4,5},{5,4},{6,7},{7,6},{8,9},{9,8},{10,11... | collective-permute-start | bytes 786440 | tf_op jit(solution)/shard_map/ppermute | solution.py:24
  44.1 10.0 %collective-permute-start.31 = (f32[2,32,512]{2,1,0:T(8,128)S(1)}, f32[2,32,512]{2,1,0:T(8,128)S(1)}, u32[]{:S(2)}, u32[]{:S(2)}) collective-permute-start(f32[2,32,512]{2,1,0:T(8,128)S(1)} %get-tuple-element.98), channel_id=1, source_target_pairs={{0,4},{4,0},{8,12},{12,8},{16,20},{20,16},{24,28},{28,24},{1,5},{5... | collective-permute-start | bytes 393224 | tf_op jit(solution)/shard_map/ppermute | solution.py:24
  45.6 10.8 %collective-permute-start.36 = (f32[2,32,512]{2,1,0:T(8,128)S(1)}, f32[2,32,512]{2,1,0:T(8,128)S(1)}, u32[]{:S(2)}, u32[]{:S(2)}) collective-permute-start(f32[2,32,512]{2,1,0:T(8,128)S(1)} %get-tuple-element.110), channel_id=1, source_target_pairs={{0,4},{4,0},{8,12},{12,8},{16,20},{20,16},{24,28},{28,24},{1,5},{5... | collective-permute-start | bytes 393224 | tf_op jit(solution)/shard_map/ppermute | solution.py:24
  56.5 8.3 %collective-permute-start.22 = (f32[2,32,512]{2,1,0:T(8,128)S(1)}, f32[2,32,512]{2,1,0:T(8,128)S(1)}, u32[]{:S(2)}, u32[]{:S(2)}) collective-permute-start(f32[2,32,512]{2,1,0:T(8,128)S(1)} %get-tuple-element.78), channel_id=1, source_target_pairs={{8,16},{12,20},{9,17},{13,21},{10,18},{14,22},{11,19},{15,23}} | collective-permute-start | bytes 393224 | tf_op jit(solution)/shard_map/ppermute | solution.py:336
  57.8 9.7 %collective-permute-start.28 = (f32[2,32,512]{2,1,0:T(8,128)S(1)}, f32[2,32,512]{2,1,0:T(8,128)S(1)}, u32[]{:S(2)}, u32[]{:S(2)}) collective-permute-start(f32[2,32,512]{2,1,0:T(8,128)S(1)} %get-tuple-element.90), channel_id=1, source_target_pairs={{8,16},{12,20},{9,17},{13,21},{10,18},{14,22},{11,19},{15,23}} | collective-permute-start | bytes 393224 | tf_op jit(solution)/shard_map/ppermute | solution.py:336
  59.2 11.2 %collective-permute-start.33 = (f32[2,32,512]{2,1,0:T(8,128)S(1)}, f32[2,32,512]{2,1,0:T(8,128)S(1)}, u32[]{:S(2)}, u32[]{:S(2)}) collective-permute-start(f32[2,32,512]{2,1,0:T(8,128)S(1)} %get-tuple-element.102), channel_id=1, source_target_pairs={{8,16},{12,20},{9,17},{13,21},{10,18},{14,22},{11,19},{15,23}} | collective-permute-start | bytes 393224 | tf_op jit(solution)/shard_map/ppermute | solution.py:336
  60.5 12.1 %collective-permute-start.38 = (f32[2,32,512]{2,1,0:T(8,128)S(1)}, f32[2,32,512]{2,1,0:T(8,128)S(1)}, u32[]{:S(2)}, u32[]{:S(2)}) collective-permute-start(f32[2,32,512]{2,1,0:T(8,128)S(1)} %get-tuple-element.114), channel_id=1, source_target_pairs={{8,16},{12,20},{9,17},{13,21},{10,18},{14,22},{11,19},{15,23}} | collective-permute-start | bytes 393224 | tf_op jit(solution)/shard_map/ppermute | solution.py:336
  65.6 10.9 %collective-permute-start.24 = (f32[2,32,512]{2,1,0:T(8,128)S(1)}, f32[2,32,512]{2,1,0:T(8,128)S(1)}, u32[]{:S(2)}, u32[]{:S(2)}) collective-permute-start(f32[2,32,512]{2,1,0:T(8,128)S(1)} %get-tuple-element.82), channel_id=1, source_target_pairs={{16,24},{20,28},{17,25},{21,29},{18,26},{22,30},{19,27},{23,31}} | collective-permute-start | bytes 393224 | tf_op jit(solution)/shard_map/ppermute | solution.py:336
  68.4 8.8 %collective-permute-start.29 = (f32[2,32,512]{2,1,0:T(8,128)S(1)}, f32[2,32,512]{2,1,0:T(8,128)S(1)}, u32[]{:S(2)}, u32[]{:S(2)}) collective-permute-start(f32[2,32,512]{2,1,0:T(8,128)S(1)} %get-tuple-element.93), channel_id=1, source_target_pairs={{16,24},{20,28},{17,25},{21,29},{18,26},{22,30},{19,27},{23,31}} | collective-permute-start | bytes 393224 | tf_op jit(solution)/shard_map/ppermute | solution.py:336
  77.9 8.6 %collective-permute-start.35 = (f32[2,32,512]{2,1,0:T(8,128)S(1)}, f32[2,32,512]{2,1,0:T(8,128)S(1)}, u32[]{:S(2)}, u32[]{:S(2)}) collective-permute-start(f32[2,32,512]{2,1,0:T(8,128)S(1)} %get-tuple-element.108), channel_id=1, source_target_pairs={{0,4},{4,0},{8,12},{12,8},{16,20},{20,16},{24,28},{28,24},{1,5},{5... | collective-permute-start | bytes 393224 | tf_op jit(solution)/shard_map/ppermute | solution.py:24
  79.5 8.9 %collective-permute-start.40 = (f32[2,32,512]{2,1,0:T(8,128)S(1)}, f32[2,32,512]{2,1,0:T(8,128)S(1)}, u32[]{:S(2)}, u32[]{:S(2)}) collective-permute-start(f32[2,32,512]{2,1,0:T(8,128)S(1)} %get-tuple-element.120), channel_id=1, source_target_pairs={{0,4},{4,0},{8,12},{12,8},{16,20},{20,16},{24,28},{28,24},{1,5},{5... | collective-permute-start | bytes 393224 | tf_op jit(solution)/shard_map/ppermute | solution.py:24
  (20 other events, 141.8 us)
